TPU v7x, 128 devices: a whole 4x4x4 slice. The times are simulated.
128 devices in a mesh: cuts: 32 (over y, z, core), tile: 4 (over x).
Axes of the slice: x: 4, y: 4, z: 4, core: 2. Of those that a mesh axis runs over, the one named last changes fastest.
Arguments:
- probe_wave: float32 [2, 256, 256], replicated, may hold values from -6 to 6
- object_field: bfloat16 [2, 32, 512, 512], P(None, 'cuts', 'tile'), may hold values from -1.03 to 1.03, as said below
- pos_rows: int32 [16], P('tile'), may hold values from 0 to 256
- pos_cols: int32 [16], P('tile'), may hold values from 0 to 256
- intensity: float32 [16, 256, 256], P('tile'), may hold values from 0.05 to 2
- prop_phase: float32 [256, 256], replicated, may hold values from -3.140625 to 3.140625
Outputs:
- object_grad: float32 [2, 32, 512, 512], P(None, 'cuts', 'tile')
Inputs may be any that keep to these rules, and one draw needn't show every extreme that they name: `object_field`: each slice's transmission has magnitude between 0.95 and 1.025.
All inputs are finite; a program needn't handle non-finite values.
Results may differ from a plain program's by a relative error of at most 0.0003.
Values may be sent and summed in bfloat16 or wider, within the bound.
No kernel may reach another device: no remote copies, remote signals or barrier semaphores. Data moves between devices by JAX's collectives and lax.ppermute only.
A program may use at most 64 MiB of HBM per device.

v0:
```python
import math

import jax
import jax.numpy as jnp
from jax import lax
from jax.sharding import PartitionSpec as P


def passed_along(block, axis, distance):
    devices = range(lax.axis_size(axis))
    route = [(i - distance, i) for i in devices if i - distance in devices]
    return lax.ppermute(block, axis, route)


def dft_tables(win_size):
    indices = jnp.arange(win_size, dtype=jnp.int32)
    products = indices[:, None] * indices[None, :] % win_size
    angles = products.astype(jnp.float32) * (2.0 * math.pi / win_size)
    norm_scale = 1.0 / math.sqrt(win_size)
    return jnp.stack([jnp.cos(angles) * norm_scale, jnp.sin(angles) * norm_scale])


def transform(field, tables, sign_flip):
    left_prod = jnp.einsum("tjk,...ckl->...tcjl", tables, field, precision=lax.Precision.HIGHEST)
    half_real = left_prod[..., 0, 0, :, :] + sign_flip * left_prod[..., 1, 1, :, :]
    half_imag = left_prod[..., 0, 1, :, :] - sign_flip * left_prod[..., 1, 0, :, :]
    half = jnp.stack([half_real, half_imag], axis=-3)
    right_prod = jnp.einsum("...cjk,tkl->...ctjl", half, tables, precision=lax.Precision.HIGHEST)
    out_real = right_prod[..., 0, 0, :, :] + sign_flip * right_prod[..., 1, 1, :, :]
    out_imag = right_prod[..., 1, 0, :, :] - sign_flip * right_prod[..., 0, 1, :, :]
    return jnp.stack([out_real, out_imag], axis=-3)


def slice_step(in_wave, obj_layer, tables, prop_cos, prop_sin):
    mixed_real = (
        in_wave[..., 0, :, :] * obj_layer[..., 0, :, :]
        - in_wave[..., 1, :, :] * obj_layer[..., 1, :, :]
    )
    mixed_imag = (
        in_wave[..., 0, :, :] * obj_layer[..., 1, :, :]
        + in_wave[..., 1, :, :] * obj_layer[..., 0, :, :]
    )
    mixed_wave = jnp.stack([mixed_real, mixed_imag], axis=-3)
    spectrum = transform(mixed_wave, tables, 1.0)
    spread_real = spectrum[..., 0, :, :] * prop_cos - spectrum[..., 1, :, :] * prop_sin
    spread_imag = spectrum[..., 0, :, :] * prop_sin + spectrum[..., 1, :, :] * prop_cos
    spread = jnp.stack([spread_real, spread_imag], axis=-3)
    return transform(spread, tables, -1.0)


def farfield_loss(exit_wave, measured, tables):
    spectrum = transform(exit_wave, tables, 1.0)
    magnitude = (
        spectrum[..., 0, :, :] * spectrum[..., 0, :, :]
        + spectrum[..., 1, :, :] * spectrum[..., 1, :, :]
    )
    return 0.5 * jnp.sum((magnitude - measured) ** 2)


def cut_patches(piece, rows_sel, cols_sel, win_size):
    row_span = piece.shape[2]
    padded = jnp.pad(piece, ((0, 0), (0, 0), (win_size, win_size), (0, 0)))

    def cut_one(pos_row, pos_col):
        offset = jnp.clip(pos_row + win_size, 0, row_span + win_size)
        return lax.dynamic_slice(
            padded, (0, 0, offset, pos_col), (2, piece.shape[1], win_size, win_size)
        )

    return jax.vmap(cut_one)(rows_sel, cols_sel)


def on_device(probe_wave, object_field, pos_rows, pos_cols, intensity, prop_phase):
    win_size = probe_wave.shape[-1]
    tables = dft_tables(win_size)
    prop_cos = jnp.cos(prop_phase)
    prop_sin = jnp.sin(prop_phase)
    layers_dev = object_field.shape[1]
    strip_rows = object_field.shape[2]
    row_width = object_field.shape[3]
    tile_count = lax.axis_size("tile")
    pos_count = pos_rows.shape[0]
    patches = cut_patches(
        lax.all_gather(object_field, "tile", axis=2, tiled=True), pos_rows, pos_cols, win_size
    )

    def group_forward(in_wave, patch_block):
        out_wave = in_wave
        out_wave = slice_step(out_wave, patch_block[..., 0, :, :], tables, prop_cos, prop_sin)
        return out_wave

    cut_index = lax.axis_index("cuts")
    cut_count = lax.axis_size("cuts")
    last_cut = cut_count - 1
    batch_size = 1
    group_count = pos_count // batch_size
    turns = cut_count + group_count - 1
    probe_block = jnp.broadcast_to(probe_wave, (batch_size, 2, win_size, win_size))
    zero_wave = jnp.zeros((batch_size, 2, win_size, win_size), jnp.float32)
    wave_store = jnp.zeros((group_count, batch_size, 2, win_size, win_size), jnp.float32)

    def forward_turn(turn, loop_state):
        incoming, stored, exits = loop_state
        group = turn - cut_index
        is_valid = (group >= 0) & (group < group_count)
        group_slot = jnp.clip(group, 0, group_count - 1)
        in_wave = jnp.where(cut_index == 0, probe_block, incoming)
        patch_block = lax.dynamic_slice_in_dim(
            patches, group_slot * batch_size, batch_size, 0
        ).astype(jnp.float32)
        out_wave = lax.cond(
            is_valid, lambda: group_forward(in_wave, patch_block), lambda: zero_wave
        )
        stored = jnp.where(
            is_valid, lax.dynamic_update_index_in_dim(stored, incoming, group_slot, 0), stored
        )
        exits = jnp.where(
            is_valid, lax.dynamic_update_index_in_dim(exits, out_wave, group_slot, 0), exits
        )
        incoming = passed_along(out_wave, "cuts", 1)
        return (incoming, stored, exits)

    _, stored, exits = lax.fori_loop(0, turns, forward_turn, (zero_wave, wave_store, wave_store))

    def exit_grads():
        flat_exits = exits.reshape(pos_count, 2, win_size, win_size)
        _, pull = jax.vjp(lambda waves: farfield_loss(waves, intensity, tables), flat_exits)
        return pull(jnp.ones((), jnp.float32))[0].reshape(
            group_count, batch_size, 2, win_size, win_size
        )

    exit_cts = lax.cond(cut_index == last_cut, exit_grads, lambda: wave_store)
    grad_region = jnp.zeros((2, layers_dev, strip_rows * tile_count, row_width), jnp.float32)

    def backward_turn(turn, loop_state):
        incoming_ct, grad_region = loop_state
        group = turn - (last_cut - cut_index)
        is_valid = (group >= 0) & (group < group_count)
        group_slot = jnp.clip(group, 0, group_count - 1)
        out_ct = jnp.where(
            cut_index == last_cut,
            lax.dynamic_index_in_dim(exit_cts, group_slot, 0, keepdims=False),
            incoming_ct,
        )
        saved_wave = lax.dynamic_index_in_dim(stored, group_slot, 0, keepdims=False)
        in_wave = jnp.where(cut_index == 0, probe_block, saved_wave)
        patch_block = lax.dynamic_slice_in_dim(
            patches, group_slot * batch_size, batch_size, 0
        ).astype(jnp.float32)

        def adjoint():
            _, pull = jax.vjp(group_forward, in_wave, patch_block)
            wave_ct, patch_ct = pull(out_ct)
            return (wave_ct, patch_ct)

        wave_ct, patch_ct = lax.cond(
            is_valid, adjoint, lambda: (zero_wave, jnp.zeros_like(patch_block))
        )
        pos_index = group_slot * batch_size + 0
        start = (0, 0, pos_rows[pos_index], pos_cols[pos_index])
        current = lax.dynamic_slice(grad_region, start, (2, layers_dev, win_size, win_size))
        grad_region = lax.dynamic_update_slice(grad_region, current + patch_ct[0], start)
        incoming_ct = passed_along(wave_ct, "cuts", -1)
        return (incoming_ct, grad_region)

    _, grad_region = lax.fori_loop(0, turns, backward_turn, (zero_wave, grad_region))
    return lax.psum_scatter(grad_region, "tile", scatter_dimension=2, tiled=True)


def solution(mesh):
    return jax.shard_map(
        on_device,
        mesh=mesh,
        in_specs=(
            P(),
            P(None, "cuts", "tile", None),
            P("tile"),
            P("tile"),
            P("tile", None, None),
            P(),
        ),
        out_specs=P(None, "cuts", "tile", None),
        check_vma=False,
    )
```

profile of v0, /device:TPU:0, one launch (start us, length us, event | category | flops | bytes accessed | tf_op | source)
XLA Modules:
  0.0 1344.5 jit_solution(8560658533553695025)
XLA Ops:
  14.3 21.2 %all-gather.2.cloned.1.call-done = bf16[2,1,512,512]{3,2,1,0:T(8,128)(2,1)} async-done(((bf16[2,1,128,512]{3,2,1,0:T(8,128)(2,1)}), bf16[2,1,512,512]{3,2,1,0:T(8,128)(2,1)}) %all-gather.2.cloned.1.call-update) | async-done | bytes 1048592 | tf_op jit(solution)/shard_map/all_gather | solution.py:84
  38.2 15.8 %while.38 = (s32[]{:T(128)}, bf16[2,1,1024,512]{3,2,1,0:T(8,128)(2,1)}, s32[4,4]{1,0:T(4,128)S(1)}, bf16[4,2,1,256,256]{3,4,1,2,0:T(8,128)(2,1)}, s32[]{:T(128)}) while((s32[]{:T(128)}, bf16[2,1,1024,512]{3,2,1,0:T(8,128)(2,1)}, s32[4,4]{1,0:T(4,128)S(1)}, bf16[4,2,1,256,256]{3,4,1,2,0:T(8,128)(2,1)}, s32[]{:T(128)}) %tuple.159), condition=%wide.while_cond, body=%wide.while_body.sunk | while | flops 2 | bytes 1573497 | solution.py:66
  57.0 467.5 %while.36 = (s32[]{:T(128)}, f32[1,2,256,256]{2,3,1,0:T(8,128)S(1)}, f32[4,1,2,256,256]{3,4,2,1,0:T(8,128)}, f32[4,1,2,256,256]{3,4,2,1,0:T(8,128)}, s32[]{:T(12...) while((s32[]{:T(128)}, ...), condition=%wide.region_3.4_spmd, body=%wide.region_0.3_spmd.sunk | while | flops 3224109056 | bytes 27525444 | solution.py:123
  103.5 8.2 collective-permute-start
  115.2 14.8 %collective-permute-start = (f32[1,2,256,256]{2,3,1,0:T(8,128)S(1)}, f32[1,2,256,256]{2,3,1,0:T(8,128)S(1)}, u32[]{:S(2)}, u32[]{:S(2)}) collective-permute-start(f32[1,2,256,256]{2,3,1,0:T(8,128)S(1)} %get-tuple-element.1004), channel_id=1, source_target_pairs={{0,4},{4,8},{8,12},{12,16},{16,20},{20,24},{24,28},{28,32},{32,36}... | collective-permute-start | bytes 1572872 | tf_op jit(solution)/shard_map/while/body/eval_jaxpr/ppermute | solution.py:12
  145.1 14.8 %collective-permute-start = (f32[1,2,256,256]{2,3,1,0:T(8,128)S(1)}, f32[1,2,256,256]{2,3,1,0:T(8,128)S(1)}, u32[]{:S(2)}, u32[]{:S(2)}) collective-permute-start(f32[1,2,256,256]{2,3,1,0:T(8,128)S(1)} %get-tuple-element.1004), channel_id=1, source_target_pairs={{0,4},{4,8},{8,12},{12,16},{16,20},{20,24},{24,28},{28,32},{32,36}... | collective-permute-start | bytes 1572872 | tf_op jit(solution)/shard_map/while/body/eval_jaxpr/ppermute | solution.py:12
  163.4 8.2 collective-permute-start
  175.1 8.2 collective-permute-start
  291.8 9.9 collective-permute-start
  305.2 10.3 collective-permute-start
  319.0 10.3 collective-permute-start
  332.8 10.3 collective-permute-start
  346.6 10.3 collective-permute-start
  360.4 10.3 collective-permute-start
  374.1 10.3 collective-permute-start
  387.9 10.3 collective-permute-start
  401.7 10.3 collective-permute-start
  415.5 10.3 collective-permute-start
  429.2 10.3 collective-permute-start
  443.0 10.3 collective-permute-start
  456.8 10.3 collective-permute-start
  470.6 10.3 collective-permute-start
  484.4 10.3 collective-permute-start
  498.1 10.3 collective-permute-start
  511.9 10.3 collective-permute-start
  528.1 782.9 %while.37 = (s32[]{:T(128)}, f32[1,2,256,256]{2,3,1,0:T(8,128)S(1)}, f32[2,1,512,512]{3,2,1,0:T(8,128)}, s32[]{:T(128)}, bf16[4,2,1,256,256]{3,4,1,2,0:T(8,128)(...) while((s32[]{:T(128)}, ...), condition=%wide.region_9.10_spmd, body=%wide.region_6.9_spmd.sunk | while | flops 3227516928 | bytes 38535668 | solution.py:166
  1050.9 149.8 %collective-permute-done.1 = f32[1,2,256,256]{2,3,1,0:T(8,128)S(1)} collective-permute-done((f32[1,2,256,256]{2,3,1,0:T(8,128)}, f32[1,2,256,256]{2,3,1,0:T(8,128)S(1)}, u32[]{:S(2)}, u32[]{:S(2)}) %collective-permute-start.1) | collective-permute-done | bytes 524320 | tf_op jit(solution)/shard_map/while/body/eval_jaxpr/ppermute | solution.py:12
  1201.7 11.5 conditional.7
  1229.3 11.5 conditional.7
  1257.1 11.5 conditional.7
  1285.0 11.5 conditional.7
  1311.0 26.6 %reduce-scatter.2.cloned.1.call-done = f32[2,1,128,512]{3,2,1,0:T(8,128)} async-done(((f32[2,1,512,512]{3,2,1,0:T(8,128)}), f32[2,1,128,512]{3,2,1,0:T(8,128)}) %reduce-scatter.2.cloned.1.call-update) | async-done | bytes 524304 | tf_op jit(solution)/shard_map/reduce_scatter | solution.py:167
  (879 shorter events, 829.5 us)
Async XLA Ops:
  6.5 28.9 %all-gather.2.cloned.1.call-start = ((), (), s32[]{:S(2)}) async-start(), calls=%async_computation.1 | async-start | bytes 1310720 | tf_op jit(solution)/shard_map/all_gather | solution.py:84
  7.3 1330.4 %reduce-scatter.2.cloned.1.call-start = ((), (), s32[]{:S(2)}) async-start(), calls=%async_computation.2 | async-start | bytes 2621440 | tf_op jit(solution)/shard_map/reduce_scatter | solution.py:167
  115.2 17.1 %collective-permute-start = (f32[1,2,256,256]{2,3,1,0:T(8,128)S(1)}, f32[1,2,256,256]{2,3,1,0:T(8,128)S(1)}, u32[]{:S(2)}, u32[]{:S(2)}) collective-permute-start(f32[1,2,256,256]{2,3,1,0:T(8,128)S(1)} %get-tuple-element.1004), channel_id=1, source_target_pairs={{0,4},{4,8},{8,12},{12,16},{16,20},{20,24},{24,28},{28,32},{32,36}... | collective-permute-start | bytes 1572872 | tf_op jit(solution)/shard_map/while/body/eval_jaxpr/ppermute | solution.py:12
  145.1 17.1 %collective-permute-start = (f32[1,2,256,256]{2,3,1,0:T(8,128)S(1)}, f32[1,2,256,256]{2,3,1,0:T(8,128)S(1)}, u32[]{:S(2)}, u32[]{:S(2)}) collective-permute-start(f32[1,2,256,256]{2,3,1,0:T(8,128)S(1)} %get-tuple-element.1004), channel_id=1, source_target_pairs={{0,4},{4,8},{8,12},{12,16},{16,20},{20,24},{24,28},{28,32},{32,36}... | collective-permute-start | bytes 1572872 | tf_op jit(solution)/shard_map/while/body/eval_jaxpr/ppermute | solution.py:12
  628.6 15.1 %collective-permute-start.1 = (f32[1,2,256,256]{2,3,1,0:T(8,128)}, f32[1,2,256,256]{2,3,1,0:T(8,128)S(1)}, u32[]{:S(2)}, u32[]{:S(2)}) collective-permute-start(f32[1,2,256,256]{2,3,1,0:T(8,128)} %get-tuple-element.1023), channel_id=1, source_target_pairs={{4,0},{8,4},{12,8},{16,12},{20,16},{24,20},{28,24},{32,28},{36,32}... | collective-permute-start | bytes 1572872 | tf_op jit(solution)/shard_map/while/body/eval_jaxpr/ppermute | solution.py:12
  645.6 15.1 %collective-permute-start.1 = (f32[1,2,256,256]{2,3,1,0:T(8,128)}, f32[1,2,256,256]{2,3,1,0:T(8,128)S(1)}, u32[]{:S(2)}, u32[]{:S(2)}) collective-permute-start(f32[1,2,256,256]{2,3,1,0:T(8,128)} %get-tuple-element.1023), channel_id=1, source_target_pairs={{4,0},{8,4},{12,8},{16,12},{20,16},{24,20},{28,24},{32,28},{36,32}... | collective-permute-start | bytes 1572872 | tf_op jit(solution)/shard_map/while/body/eval_jaxpr/ppermute | solution.py:12
  662.6 15.1 %collective-permute-start.1 = (f32[1,2,256,256]{2,3,1,0:T(8,128)}, f32[1,2,256,256]{2,3,1,0:T(8,128)S(1)}, u32[]{:S(2)}, u32[]{:S(2)}) collective-permute-start(f32[1,2,256,256]{2,3,1,0:T(8,128)} %get-tuple-element.1023), channel_id=1, source_target_pairs={{4,0},{8,4},{12,8},{16,12},{20,16},{24,20},{28,24},{32,28},{36,32}... | collective-permute-start | bytes 1572872 | tf_op jit(solution)/shard_map/while/body/eval_jaxpr/ppermute | solution.py:12
  679.6 15.1 %collective-permute-start.1 = (f32[1,2,256,256]{2,3,1,0:T(8,128)}, f32[1,2,256,256]{2,3,1,0:T(8,128)S(1)}, u32[]{:S(2)}, u32[]{:S(2)}) collective-permute-start(f32[1,2,256,256]{2,3,1,0:T(8,128)} %get-tuple-element.1023), channel_id=1, source_target_pairs={{4,0},{8,4},{12,8},{16,12},{20,16},{24,20},{28,24},{32,28},{36,32}... | collective-permute-start | bytes 1572872 | tf_op jit(solution)/shard_map/while/body/eval_jaxpr/ppermute | solution.py:12
  696.6 15.1 %collective-permute-start.1 = (f32[1,2,256,256]{2,3,1,0:T(8,128)}, f32[1,2,256,256]{2,3,1,0:T(8,128)S(1)}, u32[]{:S(2)}, u32[]{:S(2)}) collective-permute-start(f32[1,2,256,256]{2,3,1,0:T(8,128)} %get-tuple-element.1023), channel_id=1, source_target_pairs={{4,0},{8,4},{12,8},{16,12},{20,16},{24,20},{28,24},{32,28},{36,32}... | collective-permute-start | bytes 1572872 | tf_op jit(solution)/shard_map/while/body/eval_jaxpr/ppermute | solution.py:12
  713.6 15.1 %collective-permute-start.1 = (f32[1,2,256,256]{2,3,1,0:T(8,128)}, f32[1,2,256,256]{2,3,1,0:T(8,128)S(1)}, u32[]{:S(2)}, u32[]{:S(2)}) collective-permute-start(f32[1,2,256,256]{2,3,1,0:T(8,128)} %get-tuple-element.1023), channel_id=1, source_target_pairs={{4,0},{8,4},{12,8},{16,12},{20,16},{24,20},{28,24},{32,28},{36,32}... | collective-permute-start | bytes 1572872 | tf_op jit(solution)/shard_map/while/body/eval_jaxpr/ppermute | solution.py:12
  730.6 15.1 %collective-permute-start.1 = (f32[1,2,256,256]{2,3,1,0:T(8,128)}, f32[1,2,256,256]{2,3,1,0:T(8,128)S(1)}, u32[]{:S(2)}, u32[]{:S(2)}) collective-permute-start(f32[1,2,256,256]{2,3,1,0:T(8,128)} %get-tuple-element.1023), channel_id=1, source_target_pairs={{4,0},{8,4},{12,8},{16,12},{20,16},{24,20},{28,24},{32,28},{36,32}... | collective-permute-start | bytes 1572872 | tf_op jit(solution)/shard_map/while/body/eval_jaxpr/ppermute | solution.py:12
  747.6 15.1 %collective-permute-start.1 = (f32[1,2,256,256]{2,3,1,0:T(8,128)}, f32[1,2,256,256]{2,3,1,0:T(8,128)S(1)}, u32[]{:S(2)}, u32[]{:S(2)}) collective-permute-start(f32[1,2,256,256]{2,3,1,0:T(8,128)} %get-tuple-element.1023), channel_id=1, source_target_pairs={{4,0},{8,4},{12,8},{16,12},{20,16},{24,20},{28,24},{32,28},{36,32}... | collective-permute-start | bytes 1572872 | tf_op jit(solution)/shard_map/while/body/eval_jaxpr/ppermute | solution.py:12
  764.6 15.1 %collective-permute-start.1 = (f32[1,2,256,256]{2,3,1,0:T(8,128)}, f32[1,2,256,256]{2,3,1,0:T(8,128)S(1)}, u32[]{:S(2)}, u32[]{:S(2)}) collective-permute-start(f32[1,2,256,256]{2,3,1,0:T(8,128)} %get-tuple-element.1023), channel_id=1, source_target_pairs={{4,0},{8,4},{12,8},{16,12},{20,16},{24,20},{28,24},{32,28},{36,32}... | collective-permute-start | bytes 1572872 | tf_op jit(solution)/shard_map/while/body/eval_jaxpr/ppermute | solution.py:12
  781.6 15.1 %collective-permute-start.1 = (f32[1,2,256,256]{2,3,1,0:T(8,128)}, f32[1,2,256,256]{2,3,1,0:T(8,128)S(1)}, u32[]{:S(2)}, u32[]{:S(2)}) collective-permute-start(f32[1,2,256,256]{2,3,1,0:T(8,128)} %get-tuple-element.1023), channel_id=1, source_target_pairs={{4,0},{8,4},{12,8},{16,12},{20,16},{24,20},{28,24},{32,28},{36,32}... | collective-permute-start | bytes 1572872 | tf_op jit(solution)/shard_map/while/body/eval_jaxpr/ppermute | solution.py:12
  798.6 15.1 %collective-permute-start.1 = (f32[1,2,256,256]{2,3,1,0:T(8,128)}, f32[1,2,256,256]{2,3,1,0:T(8,128)S(1)}, u32[]{:S(2)}, u32[]{:S(2)}) collective-permute-start(f32[1,2,256,256]{2,3,1,0:T(8,128)} %get-tuple-element.1023), channel_id=1, source_target_pairs={{4,0},{8,4},{12,8},{16,12},{20,16},{24,20},{28,24},{32,28},{36,32}... | collective-permute-start | bytes 1572872 | tf_op jit(solution)/shard_map/while/body/eval_jaxpr/ppermute | solution.py:12
  815.5 15.1 %collective-permute-start.1 = (f32[1,2,256,256]{2,3,1,0:T(8,128)}, f32[1,2,256,256]{2,3,1,0:T(8,128)S(1)}, u32[]{:S(2)}, u32[]{:S(2)}) collective-permute-start(f32[1,2,256,256]{2,3,1,0:T(8,128)} %get-tuple-element.1023), channel_id=1, source_target_pairs={{4,0},{8,4},{12,8},{16,12},{20,16},{24,20},{28,24},{32,28},{36,32}... | collective-permute-start | bytes 1572872 | tf_op jit(solution)/shard_map/while/body/eval_jaxpr/ppermute | solution.py:12
  832.5 15.1 %collective-permute-start.1 = (f32[1,2,256,256]{2,3,1,0:T(8,128)}, f32[1,2,256,256]{2,3,1,0:T(8,128)S(1)}, u32[]{:S(2)}, u32[]{:S(2)}) collective-permute-start(f32[1,2,256,256]{2,3,1,0:T(8,128)} %get-tuple-element.1023), channel_id=1, source_target_pairs={{4,0},{8,4},{12,8},{16,12},{20,16},{24,20},{28,24},{32,28},{36,32}... | collective-permute-start | bytes 1572872 | tf_op jit(solution)/shard_map/while/body/eval_jaxpr/ppermute | solution.py:12
  849.5 15.1 %collective-permute-start.1 = (f32[1,2,256,256]{2,3,1,0:T(8,128)}, f32[1,2,256,256]{2,3,1,0:T(8,128)S(1)}, u32[]{:S(2)}, u32[]{:S(2)}) collective-permute-start(f32[1,2,256,256]{2,3,1,0:T(8,128)} %get-tuple-element.1023), channel_id=1, source_target_pairs={{4,0},{8,4},{12,8},{16,12},{20,16},{24,20},{28,24},{32,28},{36,32}... | collective-permute-start | bytes 1572872 | tf_op jit(solution)/shard_map/while/body/eval_jaxpr/ppermute | solution.py:12
  866.5 15.1 %collective-permute-start.1 = (f32[1,2,256,256]{2,3,1,0:T(8,128)}, f32[1,2,256,256]{2,3,1,0:T(8,128)S(1)}, u32[]{:S(2)}, u32[]{:S(2)}) collective-permute-start(f32[1,2,256,256]{2,3,1,0:T(8,128)} %get-tuple-element.1023), channel_id=1, source_target_pairs={{4,0},{8,4},{12,8},{16,12},{20,16},{24,20},{28,24},{32,28},{36,32}... | collective-permute-start | bytes 1572872 | tf_op jit(solution)/shard_map/while/body/eval_jaxpr/ppermute | solution.py:12
  883.5 15.1 %collective-permute-start.1 = (f32[1,2,256,256]{2,3,1,0:T(8,128)}, f32[1,2,256,256]{2,3,1,0:T(8,128)S(1)}, u32[]{:S(2)}, u32[]{:S(2)}) collective-permute-start(f32[1,2,256,256]{2,3,1,0:T(8,128)} %get-tuple-element.1023), channel_id=1, source_target_pairs={{4,0},{8,4},{12,8},{16,12},{20,16},{24,20},{28,24},{32,28},{36,32}... | collective-permute-start | bytes 1572872 | tf_op jit(solution)/shard_map/while/body/eval_jaxpr/ppermute | solution.py:12
  900.5 15.1 %collective-permute-start.1 = (f32[1,2,256,256]{2,3,1,0:T(8,128)}, f32[1,2,256,256]{2,3,1,0:T(8,128)S(1)}, u32[]{:S(2)}, u32[]{:S(2)}) collective-permute-start(f32[1,2,256,256]{2,3,1,0:T(8,128)} %get-tuple-element.1023), channel_id=1, source_target_pairs={{4,0},{8,4},{12,8},{16,12},{20,16},{24,20},{28,24},{32,28},{36,32}... | collective-permute-start | bytes 1572872 | tf_op jit(solution)/shard_map/while/body/eval_jaxpr/ppermute | solution.py:12
  917.5 15.1 %collective-permute-start.1 = (f32[1,2,256,256]{2,3,1,0:T(8,128)}, f32[1,2,256,256]{2,3,1,0:T(8,128)S(1)}, u32[]{:S(2)}, u32[]{:S(2)}) collective-permute-start(f32[1,2,256,256]{2,3,1,0:T(8,128)} %get-tuple-element.1023), channel_id=1, source_target_pairs={{4,0},{8,4},{12,8},{16,12},{20,16},{24,20},{28,24},{32,28},{36,32}... | collective-permute-start | bytes 1572872 | tf_op jit(solution)/shard_map/while/body/eval_jaxpr/ppermute | solution.py:12
  934.5 15.1 %collective-permute-start.1 = (f32[1,2,256,256]{2,3,1,0:T(8,128)}, f32[1,2,256,256]{2,3,1,0:T(8,128)S(1)}, u32[]{:S(2)}, u32[]{:S(2)}) collective-permute-start(f32[1,2,256,256]{2,3,1,0:T(8,128)} %get-tuple-element.1023), channel_id=1, source_target_pairs={{4,0},{8,4},{12,8},{16,12},{20,16},{24,20},{28,24},{32,28},{36,32}... | collective-permute-start | bytes 1572872 | tf_op jit(solution)/shard_map/while/body/eval_jaxpr/ppermute | solution.py:12
  951.5 15.1 %collective-permute-start.1 = (f32[1,2,256,256]{2,3,1,0:T(8,128)}, f32[1,2,256,256]{2,3,1,0:T(8,128)S(1)}, u32[]{:S(2)}, u32[]{:S(2)}) collective-permute-start(f32[1,2,256,256]{2,3,1,0:T(8,128)} %get-tuple-element.1023), channel_id=1, source_target_pairs={{4,0},{8,4},{12,8},{16,12},{20,16},{24,20},{28,24},{32,28},{36,32}... | collective-permute-start | bytes 1572872 | tf_op jit(solution)/shard_map/while/body/eval_jaxpr/ppermute | solution.py:12
  968.5 15.1 %collective-permute-start.1 = (f32[1,2,256,256]{2,3,1,0:T(8,128)}, f32[1,2,256,256]{2,3,1,0:T(8,128)S(1)}, u32[]{:S(2)}, u32[]{:S(2)}) collective-permute-start(f32[1,2,256,256]{2,3,1,0:T(8,128)} %get-tuple-element.1023), channel_id=1, source_target_pairs={{4,0},{8,4},{12,8},{16,12},{20,16},{24,20},{28,24},{32,28},{36,32}... | collective-permute-start | bytes 1572872 | tf_op jit(solution)/shard_map/while/body/eval_jaxpr/ppermute | solution.py:12
  985.5 15.1 %collective-permute-start.1 = (f32[1,2,256,256]{2,3,1,0:T(8,128)}, f32[1,2,256,256]{2,3,1,0:T(8,128)S(1)}, u32[]{:S(2)}, u32[]{:S(2)}) collective-permute-start(f32[1,2,256,256]{2,3,1,0:T(8,128)} %get-tuple-element.1023), channel_id=1, source_target_pairs={{4,0},{8,4},{12,8},{16,12},{20,16},{24,20},{28,24},{32,28},{36,32}... | collective-permute-start | bytes 1572872 | tf_op jit(solution)/shard_map/while/body/eval_jaxpr/ppermute | solution.py:12
  1002.4 15.1 %collective-permute-start.1 = (f32[1,2,256,256]{2,3,1,0:T(8,128)}, f32[1,2,256,256]{2,3,1,0:T(8,128)S(1)}, u32[]{:S(2)}, u32[]{:S(2)}) collective-permute-start(f32[1,2,256,256]{2,3,1,0:T(8,128)} %get-tuple-element.1023), channel_id=1, source_target_pairs={{4,0},{8,4},{12,8},{16,12},{20,16},{24,20},{28,24},{32,28},{36,32}... | collective-permute-start | bytes 1572872 | tf_op jit(solution)/shard_map/while/body/eval_jaxpr/ppermute | solution.py:12
  1019.4 15.1 %collective-permute-start.1 = (f32[1,2,256,256]{2,3,1,0:T(8,128)}, f32[1,2,256,256]{2,3,1,0:T(8,128)S(1)}, u32[]{:S(2)}, u32[]{:S(2)}) collective-permute-start(f32[1,2,256,256]{2,3,1,0:T(8,128)} %get-tuple-element.1023), channel_id=1, source_target_pairs={{4,0},{8,4},{12,8},{16,12},{20,16},{24,20},{28,24},{32,28},{36,32}... | collective-permute-start | bytes 1572872 | tf_op jit(solution)/shard_map/while/body/eval_jaxpr/ppermute | solution.py:12
  1036.4 164.3 %collective-permute-start.1 = (f32[1,2,256,256]{2,3,1,0:T(8,128)}, f32[1,2,256,256]{2,3,1,0:T(8,128)S(1)}, u32[]{:S(2)}, u32[]{:S(2)}) collective-permute-start(f32[1,2,256,256]{2,3,1,0:T(8,128)} %get-tuple-element.1023), channel_id=1, source_target_pairs={{4,0},{8,4},{12,8},{16,12},{20,16},{24,20},{28,24},{32,28},{36,32}... | collective-permute-start | bytes 1572872 | tf_op jit(solution)/shard_map/while/body/eval_jaxpr/ppermute | solution.py:12
  1213.2 15.1 %collective-permute-start.1 = (f32[1,2,256,256]{2,3,1,0:T(8,128)}, f32[1,2,256,256]{2,3,1,0:T(8,128)S(1)}, u32[]{:S(2)}, u32[]{:S(2)}) collective-permute-start(f32[1,2,256,256]{2,3,1,0:T(8,128)} %get-tuple-element.1023), channel_id=1, source_target_pairs={{4,0},{8,4},{12,8},{16,12},{20,16},{24,20},{28,24},{32,28},{36,32}... | collective-permute-start | bytes 1572872 | tf_op jit(solution)/shard_map/while/body/eval_jaxpr/ppermute | solution.py:12
  1240.8 15.3 %collective-permute-start.1 = (f32[1,2,256,256]{2,3,1,0:T(8,128)}, f32[1,2,256,256]{2,3,1,0:T(8,128)S(1)}, u32[]{:S(2)}, u32[]{:S(2)}) collective-permute-start(f32[1,2,256,256]{2,3,1,0:T(8,128)} %get-tuple-element.1023), channel_id=1, source_target_pairs={{4,0},{8,4},{12,8},{16,12},{20,16},{24,20},{28,24},{32,28},{36,32}... | collective-permute-start | bytes 1572872 | tf_op jit(solution)/shard_map/while/body/eval_jaxpr/ppermute | solution.py:12
  1268.7 15.4 %collective-permute-start.1 = (f32[1,2,256,256]{2,3,1,0:T(8,128)}, f32[1,2,256,256]{2,3,1,0:T(8,128)S(1)}, u32[]{:S(2)}, u32[]{:S(2)}) collective-permute-start(f32[1,2,256,256]{2,3,1,0:T(8,128)} %get-tuple-element.1023), channel_id=1, source_target_pairs={{4,0},{8,4},{12,8},{16,12},{20,16},{24,20},{28,24},{32,28},{36,32}... | collective-permute-start | bytes 1572872 | tf_op jit(solution)/shard_map/while/body/eval_jaxpr/ppermute | solution.py:12
  (44 other events, 488.0 us)
Sparse Core Ops, SparseCore 0:
  9.0 26.3 all-gather.1
  1311.1 26.4 reduce-scatter.1
where the time goes:
time: 1370 us; the launch traced here: 1340 us
  local copies, waits for them, and re-layouts  394 us (29%)
  starting transfers between devices  364 us (27%)
  waiting for transfers between devices  216 us (16%)
  other arithmetic  179 us (13%)
  loops' own time  133 us (10%)
  matrix products  45.9 us (3%)
    ppermute x70, starting transfers between devices, passed_along(): return lax.ppermute(block, axis, route)  364 us
    dynamic_update_slice x70, local copies, waits for them, and re-layouts, backward_turn(): lax.dynamic_update_slice(grad_region, current + patch_ct[0], start)  235 us
    ppermute x70, waiting for transfers between devices, passed_along(): return lax.ppermute(block, axis, route)  167 us
    another operation x1, loops' own time, on_device(): lax.fori_loop(0, turns, backward_turn, (zero_wave, grad_region))  129 us
    select_n x35, other arithmetic, forward_turn(): jnp.where(is_valid, lax.dynamic_update_index_in_dim(stored, incoming, gro...  81.5 us
    dynamic_slice x70, local copies, waits for them, and re-layouts, backward_turn(): lax.dynamic_slice(grad_region, start, (2, layers_dev, win_size, win_size))  54.8 us
    dynamic_slice x70, local copies, waits for them, and re-layouts, backward_turn(): start = (0, 0, pos_rows[pos_index], pos_cols[pos_index])  42.2 us
    convert_element_type x35, other arithmetic, forward_turn(): patch_block = lax.dynamic_slice_in_dim(patches, group_slot * batch_size,...  34.6 us
  transfers between devices with their start and end apart: 72, of which 31 were waited for; matrix products, arithmetic and copies ran while one was open for 31% of the time, Pallas kernels for 0%

commit v1 on v0

v1 whole, which is shorter than its diff:
```python
import math

import jax
import jax.numpy as jnp
import ml_dtypes
import numpy as np
from jax import lax
from jax.experimental import pallas as pl
from jax.experimental.pallas import tpu as pltpu
from jax.sharding import Mesh, PartitionSpec as P

N = 256
M = N // 2
F32 = jnp.float32
BF16 = jnp.bfloat16


def tables():
    half = np.arange(M) + 0.5
    angles = 2.0 * math.pi / N * half[:, None] * half[None, :]
    packed, gain = [], []
    for values in (np.cos(angles) / 16.0, np.sin(angles) / 16.0):
        high = values.astype(ml_dtypes.bfloat16)
        low = (values - high.astype(np.float64)).astype(ml_dtypes.bfloat16)
        packed.append(np.block([[high, low], [high, low]]))
        both = high.astype(np.float64) + low.astype(np.float64)
        gain.append(4.0 * np.trace(both @ both) / M)
    return packed[0], packed[1], np.ascontiguousarray(packed[0].T), np.ascontiguousarray(packed[1].T), float(np.mean(gain)) ** 2


def split(x):
    high = x.astype(BF16)
    return high, (x - high.astype(F32)).astype(BF16)


def dot(a, b):
    return jnp.dot(a, b, preferred_element_type=F32)


def right(blocks, table):
    high, low = split(jnp.concatenate(blocks, axis=0))
    out = dot(jnp.concatenate([high, low], axis=1), table)
    out = out[:, :M] + out[:, M:]
    return [out[i * M : (i + 1) * M] for i in range(4)]


def left(blocks, table):
    high, low = split(jnp.concatenate(blocks, axis=1))
    out = dot(table, jnp.concatenate([high, low], axis=0))
    out = out[:M] + out[M:]
    return [out[:, i * M : (i + 1) * M] for i in range(4)]


def spectrum(quads, tabs):
    folded = []
    for x11, x12, x21, x22 in quads:
        d1, d2, s1, s2 = x11 - x21, x12 - x22, x11 + x21, x12 + x22
        folded.append((d1 - d2, d1 + d2, s1 - s2, s1 + s2))
    (ddr, dsr, sdr, ssr), (ddi, dsi, sdi, ssi) = folded
    cos_r, sin_r, cos_l, sin_l = tabs
    ddr, sdr, ddi, sdi = right([ddr, sdr, ddi, sdi], cos_r)
    dsr, ssr, dsi, ssi = right([dsr, ssr, dsi, ssi], sin_r)
    ppr, pqr, ppi, pqi = left([ddr, dsr, ddi, dsi], cos_l)
    qpr, qqr, qpi, qqi = left([sdr, ssr, sdi, ssi], sin_l)
    ar, ai, br, bi = ppr - qqr, ppi - qqi, ppr + qqr, ppi + qqi
    er, ei, gr, gi = pqr + qpr, pqi + qpi, pqr - qpr, pqi - qpi
    real = (ar + ei, br - gi, br + gi, ar - ei)
    imag = (ai - er, bi + gr, bi - gr, ai + er)
    return real, imag


def wave_of(spec, tabs):
    cos_r, sin_r, cos_l, sin_l = tabs
    (yr11, yr12, yr21, yr22), (yi11, yi12, yi21, yi22) = spec
    apr, api, amr, ami = yr11 + yr22, yi11 + yi22, yr11 - yr22, yi11 - yi22
    bpr, bpi, bmr, bmi = yr12 + yr21, yi12 + yi21, yr12 - yr21, yi12 - yi21
    ppr, ppi, qqr, qqi = apr + bpr, api + bpi, bpr - apr, bpi - api
    pqr, pqi = bmi - ami, amr - bmr
    qpr, qpi = -(ami + bmi), amr + bmr
    ppr, pqr, ppi, pqi = left([ppr, pqr, ppi, pqi], cos_l)
    qpr, qqr, qpi, qqi = left([qpr, qqr, qpi, qqi], sin_l)
    uur, vur, uui, vui = right([ppr, qpr, ppi, qpi], cos_r)
    uvr, vvr, uvi, vvi = right([pqr, qqr, pqi, qqi], sin_r)
    quads = []
    for uu, uv, vu, vv in ((uur, uvr, vur, vvr), (uui, uvi, vui, vvi)):
        p1, m1, p2, m2 = vv + uu, vv - uu, vu + uv, vu - uv
        quads.append((p1 + p2, m1 - m2, m1 + m2, p1 - p2))
    return quads


def quarters(ref, *lead):
    return tuple(ref[(*lead, slice(i * M, i * M + M), slice(j * M, j * M + M))] for i in (0, 1) for j in (0, 1))


def put(ref, quads, *lead):
    for part in (0, 1):
        for at, value in enumerate(quads[part]):
            i, j = divmod(at, 2)
            ref[(*lead, part, slice(i * M, i * M + M), slice(j * M, j * M + M))] = value


def times(ar, ai, br, bi):
    real = tuple(w * x - y * z for w, x, y, z in zip(ar, br, ai, bi))
    imag = tuple(w * z + y * x for w, x, y, z in zip(ar, br, ai, bi))
    return real, imag


def conj_times(ar, ai, br, bi):
    real = tuple(w * x + y * z for w, x, y, z in zip(ar, br, ai, bi))
    imag = tuple(w * z - y * x for w, x, y, z in zip(ar, br, ai, bi))
    return real, imag


def as_f32(values):
    return tuple(v.astype(F32) for v in values)


def forward_kernel(gain, is_last, steps, mine_ref, obj_ref, wave_ref, prop_ref, cr, sr, cl, sl, *rest):
    if is_last:
        inten_ref, out_ref, kept_ref = rest
    else:
        out_ref, kept_ref = rest
    step = pl.program_id(0)
    tabs = (cr[...], sr[...], cl[...], sl[...])

    @pl.when(step == 0)
    def _():
        out_ref[...] = wave_ref[...]

    @pl.when(step == mine_ref[0])
    def _():
        kept_ref[...] = out_ref[...]

    objr, obji = as_f32(quarters(obj_ref, 0, 0)), as_f32(quarters(obj_ref, 0, 1))
    mixed = times(quarters(out_ref, 0), quarters(out_ref, 1), objr, obji)
    spec = spectrum(mixed, tabs)
    spread = times(spec[0], spec[1], quarters(prop_ref, 0), quarters(prop_ref, 1))
    put(out_ref, wave_of(spread, tabs))

    if is_last:

        @pl.when(step == steps - 1)
        def _():
            real, imag = spectrum((quarters(out_ref, 0), quarters(out_ref, 1)), tabs)
            scale = [(2.0 / gain) * (x * x + y * y - z) for x, y, z in zip(real, imag, quarters(inten_ref))]
            slope = tuple(s * x for s, x in zip(scale, real)), tuple(s * x for s, x in zip(scale, imag))
            put(out_ref, wave_of(slope, tabs))


def paired_index(shape, axis):
    at = lax.broadcasted_iota(jnp.int32, shape, axis)
    return jnp.where(at < M, at, N + M - 1 - at)


def chosen(start, shape, window_axis):
    window = paired_index(shape, window_axis) + start
    return jnp.where(window == lax.broadcasted_iota(jnp.int32, shape, 1 - window_axis), 1.0, 0.0).astype(BF16)


def backward_kernel(steps, width, height, scalars, obj_ref, ct_ref, prop_ref, cr, sr, cl, sl, kept_ref, out_ref, region_ref, grad_ref):
    step = pl.program_id(0)
    tabs = (cr[...], sr[...], cl[...], sl[...])

    @pl.when(step == 0)
    def _():
        out_ref[...] = ct_ref[...]

    spec = spectrum((quarters(out_ref, 0), quarters(out_ref, 1)), tabs)
    back = conj_times(quarters(prop_ref, 0), quarters(prop_ref, 1), spec[0], spec[1])
    put(out_ref, wave_of(back, tabs))

    @pl.when(steps - 1 - step == scalars[0])
    def _():
        ct = quarters(out_ref, 0), quarters(out_ref, 1)
        put(grad_ref, conj_times(quarters(kept_ref, 0), quarters(kept_ref, 1), ct[0], ct[1]))

    objr, obji = as_f32(quarters(obj_ref, 0, 0)), as_f32(quarters(obj_ref, 0, 1))
    put(out_ref, conj_times(objr, obji, quarters(out_ref, 0), quarters(out_ref, 1)))

    @pl.when(step == steps - 1)
    def _():
        rows = chosen(scalars[1], (height, N), 1)
        cols = chosen(scalars[2], (N, width), 0)
        for part in (0, 1):
            high, low = split(grad_ref[part])
            spread = [dot(rows, dot(x, cols).astype(BF16)) for x in (high, low)]
            region_ref[part] = spread[0] + spread[1]


def cut_kernel(rows_ref, cols_ref, obj_ref, out_ref):
    height, width = obj_ref.shape[-2:]
    at = pl.program_id(0)
    rows = chosen(rows_ref[at], (N, height), 0)
    cols = chosen(cols_ref[at], (width, N), 1)
    for part in (0, 1):
        out_ref[0, part] = dot(dot(rows, obj_ref[part, 0]).astype(BF16), cols).astype(BF16)


def whole(shape):
    return pl.BlockSpec(shape, lambda *_: (0,) * len(shape))


SMEM = pl.BlockSpec(memory_space=pltpu.SMEM)
PARAMS = pltpu.CompilerParams(dimension_semantics=("arbitrary",), vmem_limit_bytes=48 << 20)
WAVE = (2, N, N)


def cut(full, pos_rows, pos_cols):
    count = pos_rows.shape[0]
    return pl.pallas_call(
        cut_kernel,
        grid=(count,),
        in_specs=[SMEM, SMEM, whole(full.shape)],
        out_specs=pl.BlockSpec((1, 2, N, N), lambda i: (i, 0, 0, 0)),
        out_shape=jax.ShapeDtypeStruct((count, 2, N, N), BF16),
        compiler_params=PARAMS,
        name="cut",
    )(pos_rows, pos_cols, full)


def run_forward(mine, chunk, wave, prop, tabs, gain, inten=None):
    steps = chunk.shape[0]
    last = inten is not None
    extra = (inten,) if last else ()

    def body(*refs):
        forward_kernel(gain, last, steps, *refs)

    return pl.pallas_call(
        body,
        grid=(steps,),
        in_specs=[SMEM, pl.BlockSpec((1, 2, N, N), lambda i: (i, 0, 0, 0)), whole(WAVE), whole(WAVE)]
        + [whole((N, N))] * (4 + len(extra)),
        out_specs=[whole(WAVE), whole(WAVE)],
        out_shape=[jax.ShapeDtypeStruct(WAVE, F32)] * 2,
        compiler_params=PARAMS,
        name="forward",
    )(mine, chunk, wave, prop, *tabs, *extra)


def run_backward(scalars, chunk, ct, prop, tabs, kept, height, width):
    steps = chunk.shape[0]

    def body(*refs):
        backward_kernel(steps, width, height, *refs)

    return pl.pallas_call(
        body,
        grid=(steps,),
        in_specs=[SMEM, pl.BlockSpec((1, 2, N, N), lambda i: (steps - 1 - i, 0, 0, 0)), whole(WAVE), whole(WAVE)]
        + [whole((N, N))] * 4
        + [whole(WAVE)],
        out_specs=[whole(WAVE), whole((2, height, width))],
        out_shape=[jax.ShapeDtypeStruct(WAVE, F32), jax.ShapeDtypeStruct((2, height, width), F32)],
        scratch_shapes=[pltpu.VMEM(WAVE, F32)],
        compiler_params=PARAMS,
        name="backward",
    )(scalars, chunk, ct, prop, *tabs, kept)


def paired(x):
    for axis in (-2, -1):
        first, second = jnp.split(x, 2, axis=axis)
        x = jnp.concatenate([first, jnp.flip(second, axis=axis)], axis=axis)
    return x


def start_wave(probe_wave):
    at = np.arange(N)
    angle = math.pi / N * (at[:, None] + at[None, :])
    cos, sin = np.cos(angle).astype(np.float32), np.sin(angle).astype(np.float32)
    real, imag = probe_wave[0], probe_wave[1]
    return paired(jnp.stack([real * cos - imag * sin, real * sin + imag * cos]))


def on_device(probe_wave, object_field, pos_rows, pos_cols, intensity, prop_phase):
    row = lax.axis_index("y")
    mine = lax.axis_index("zc").astype(jnp.int32)
    chunks_count = lax.axis_size("y")
    height = object_field.shape[2] * lax.axis_size("x")
    width = object_field.shape[3]
    full = lax.all_gather(object_field, "x", axis=2, tiled=True)
    patches = cut(full, pos_rows, pos_cols)
    patches = lax.all_to_all(patches, "y", 0, 0, tiled=True)
    chunks = [lax.all_gather(patches[i], "zc", axis=0) for i in range(chunks_count)]

    *tabs, gain = tables()
    tabs = [jnp.asarray(t) for t in tabs]
    prop = paired(jnp.stack([jnp.cos(prop_phase), jnp.sin(prop_phase)]) * (1.0 / gain))
    inten = paired(lax.dynamic_index_in_dim(intensity, row, 0, keepdims=False))
    wave = start_wave(probe_wave)
    mine_at = mine[None]
    scalars = jnp.stack([mine, pos_rows[row], pos_cols[row]])

    kept = []
    for i in range(chunks_count):
        last = i == chunks_count - 1
        wave, saved = run_forward(mine_at, chunks[i], wave, prop, tabs, gain, inten if last else None)
        kept.append(saved)
    pieces = [None] * chunks_count
    for i in reversed(range(chunks_count)):
        wave, region = run_backward(scalars, chunks[i], wave, prop, tabs, kept[i], height, width)
        pieces[i] = lax.psum_scatter(region, ("x", "y"), scatter_dimension=1, tiled=True)
    out = lax.all_to_all(jnp.stack(pieces), "y", 0, 0, tiled=True)
    out = jnp.transpose(out, (1, 0, 2, 3)).reshape(2, 1, object_field.shape[2], width)
    return out


def solution(mesh):
    devices = mesh.devices
    fine = Mesh(devices.reshape(4, devices.shape[0] // 4, devices.shape[1]), ("y", "zc", "x"))
    return jax.shard_map(
        on_device,
        mesh=fine,
        in_specs=(
            P(),
            P(None, ("y", "zc"), "x", None),
            P("x"),
            P("x"),
            P("x", None, None),
            P(),
        ),
        out_specs=P(None, ("y", "zc"), "x", None),
        check_vma=False,
    )
```

time: 1370 us -> 564 us (0.41); the launches traced: 1340 us -> 563 us
  local copies, waits for them, and re-layouts: 394 us -> 17.4 us
  starting transfers between devices: 364 us -> 0.31 us
  waiting for transfers between devices: 216 us -> 397 us
  other arithmetic: 179 us -> 2.89 us
  loops' own time: 133 us -> 0 us
  Pallas kernels: 0 us -> 102 us
  matrix products: 45.9 us -> 0 us
  blocking collectives: 0 us -> 30 us
    ppermute x70 -> x0, starting transfers between devices: 364 us -> none  [passed_along(): return lax.ppermute(block, axis, route)]
    reduce_scatter x1 -> x4, waiting for transfers between devices: 26.6 us -> 304 us  [on_device(): lax.psum_scatter(region, ('x', 'y'), scatter_dimension=1, tiled=True)]
    dynamic_update_slice x70 -> x0, local copies, waits for them, and re-layouts: 235 us -> none  [backward_turn(): lax.dynamic_update_slice(grad_region, current + patch_ct[0], start)]
    ppermute x70 -> x0, waiting for transfers between devices: 167 us -> none  [passed_along(): return lax.ppermute(block, axis, route)]
    another operation x74 -> x0, loops' own time: 133 us -> none  [the longest x1 129 us: on_device(): lax.fori_loop(0, turns, backward_turn, (zero_wave, grad_region))]
    pallas_call x0 -> x9, Pallas kernels: none -> 102 us  [the longest x4 57.1 us: run_backward(): pl.pallas_call(body, grid=(steps,), in_specs=[SMEM, pl.BlockSpec((1, 2, N...]
    dynamic_slice x140 -> x2, local copies, waits for them, and re-layouts: 97.1 us -> 1.27 us  [on_device(): scalars = jnp.stack([mine, pos_rows[row], pos_cols[row]])]
    select_n x47 -> x0, other arithmetic: 90.7 us -> none  [the longest x35 81.5 us: forward_turn(): jnp.where(is_valid, lax.dynamic_update_index_in_dim(stored, incoming, gro...]
  transfers between devices with their start and end apart: 72 -> 9, of which waited for: 31 -> 9; matrix products, arithmetic and copies ran while one was open for 31% -> 1% of each run, Pallas kernels for 0% -> 5%
where the time goes in v1:
time: 564 us; the launch traced here: 563 us
  waiting for transfers between devices  397 us (70%)
  Pallas kernels  102 us (18%)
  blocking collectives  30 us (5%)
  local copies, waits for them, and re-layouts  17.4 us (3%)
  between operations  13.5 us (2%)
    reduce_scatter x4, waiting for transfers between devices, on_device(): lax.psum_scatter(region, ('x', 'y'), scatter_dimension=1, tiled=True)  304 us
    all_gather x4, waiting for transfers between devices, on_device(): lax.all_gather(patches[i], 'zc', axis=0)  60.8 us
    pallas_call x4, Pallas kernels, run_backward(): pl.pallas_call(body, grid=(steps,), in_specs=[SMEM, pl.BlockSpec((1, 2, N...  57.1 us
    pallas_call x4, Pallas kernels, run_forward(): pl.pallas_call(body, grid=(steps,), in_specs=[SMEM, pl.BlockSpec((1, 2, N...  41.2 us
    all_gather x1, waiting for transfers between devices, on_device(): full = lax.all_gather(object_field, 'x', axis=2, tiled=True)  28.1 us
    all_to_all x1, blocking collectives, on_device(): patches = lax.all_to_all(patches, 'y', 0, 0, tiled=True)  18.3 us
    all_to_all x1, blocking collectives, on_device(): out = lax.all_to_all(jnp.stack(pieces), 'y', 0, 0, tiled=True)  11.7 us
  transfers between devices with their start and end apart: 9, of which 9 were waited for; matrix products, arithmetic and copies ran while one was open for 1% of the time, Pallas kernels for 5%

profile of v1, /device:TPU:0, one launch (start us, length us, event | category | flops | bytes accessed | tf_op | source)
XLA Modules:
  0.0 563.4 jit_solution(8287354042155985473)
XLA Ops:
  7.3 28.1 %all-gather.6.cloned.1.call-done.obj_ref = bf16[2,1,512,512]{3,2,1,0:T(8,128)(2,1)} async-done(((bf16[2,1,128,512]{3,2,1,0:T(8,128)(2,1)}), bf16[2,1,512,512]{3,2,1,0:T(8,128)(2,1)}) %all-gather.6.cloned.1.call-update) | async-done | bytes 1048592 | tf_op jit(solution)/shard_map/all_gather | solution.py:282
  35.5 1.2 copy-done.8
  38.0 3.6 cut.1
  41.6 18.3 %all_to_all.10 = bf16[4,2,256,256]{3,2,1,0:T(8,128)(2,1)S(1)} all-to-all(bf16[4,2,256,256]{3,2,1,0:T(8,128)(2,1)S(1)} %cut.1), channel_id=1, replica_groups=mesh['y'=4,'zc'=8,'x'=4] {'y'}, dimensions={0} | all-to-all | bytes 2097152 | tf_op jit(solution)/shard_map/all_to_all | solution.py:284
  59.9 1.0 fusion.4
  64.2 1.0 dynamic-slice_bitcast_fusion.1
  66.5 0.9 cosine_bitcast_fusion
  68.1 1.4 pad_add_fusion.refs_0_
  69.7 15.4 %all-gather.8.cloned.1.call-done.refs_1_ = bf16[8,2,256,256]{3,2,1,0:T(8,128)(2,1)} async-done(((bf16[1,2,256,256]{3,2,1,0:T(8,128)(2,1)}), bf16[8,2,256,256]{3,2,1,0:T(8,128)(2,1)}) %all-gather.8.cloned.1.call-update) | async-done | bytes 2097168 | tf_op jit(solution)/shard_map/all_gather | solution.py:285
  85.1 1.6 copy-done.4
  86.7 10.0 %forward.4 = (f32[2,256,256]{2,1,0:T(8,128)S(1)}, f32[2,256,256]{2,1,0:T(8,128)S(1)}) custom-call(s32[1]{0:T(128)} %bitcast.refs_0_, bf16[8,2,256,256]{3,2,1,0:T(8,128)(2,1)S(1)} %copy-done.4, f32[2,256,256]{2,1,0:T(8,128)S(1)} %pad_maximum_fusion.refs_2_, f32[2,256,256]{2,1,0:T(8,128)S(1)} %pad_maximum_fusion.1.refs_3_, bf16[256,256]{1,0:T(8,128)(2,1)S(1)} %copy-done.3, ...), custom_call_target="tpu_custom_call" | custom-call | tf_op jit(solution)/shard_map/forward/pallas_call | solution.py:229
  96.7 15.9 %all-gather.10.cloned.1.call-done.refs_1_ = bf16[8,2,256,256]{3,2,1,0:T(8,128)(2,1)} async-done(((bf16[1,2,256,256]{3,2,1,0:T(8,128)(2,1)}), bf16[8,2,256,256]{3,2,1,0:T(8,128)(2,1)}) %all-gather.10.cloned.1.call-update) | async-done | bytes 2097168 | tf_op jit(solution)/shard_map/all_gather | solution.py:285
  112.6 1.6 copy-done.5
  114.2 10.0 %forward.5 = (f32[2,256,256]{2,1,0:T(8,128)S(1)}, f32[2,256,256]{2,1,0:T(8,128)S(1)}) custom-call(s32[1]{0:T(128)} %bitcast.refs_0_, bf16[8,2,256,256]{3,2,1,0:T(8,128)(2,1)S(1)} %copy-done.5, f32[2,256,256]{2,1,0:T(8,128)S(1)} %get-tuple-element.20.refs_2_, f32[2,256,256]{2,1,0:T(8,128)S(1)} %pad_maximum_fusion.1.refs_3_, bf16[256,256]{1,0:T(8,128)(2,1)S(1)} %copy-done.3, ...), custom_call_target="tpu_custom_call" | custom-call | tf_op jit(solution)/shard_map/forward/pallas_call | solution.py:229
  125.0 14.9 %all-gather.12.cloned.1.call-done.refs_1_ = bf16[8,2,256,256]{3,2,1,0:T(8,128)(2,1)} async-done(((bf16[1,2,256,256]{3,2,1,0:T(8,128)(2,1)}), bf16[8,2,256,256]{3,2,1,0:T(8,128)(2,1)}) %all-gather.12.cloned.1.call-update) | async-done | bytes 2097168 | tf_op jit(solution)/shard_map/all_gather | solution.py:285
  139.9 1.6 copy-done.6
  141.5 1.0 copy-done.10
  142.6 10.0 %forward.6 = (f32[2,256,256]{2,1,0:T(8,128)S(1)}, f32[2,256,256]{2,1,0:T(8,128)S(1)}) custom-call(s32[1]{0:T(128)} %bitcast.refs_0_, bf16[8,2,256,256]{3,2,1,0:T(8,128)(2,1)S(1)} %copy-done.6, f32[2,256,256]{2,1,0:T(8,128)S(1)} %copy-done.10, f32[2,256,256]{2,1,0:T(8,128)S(1)} %pad_maximum_fusion.1.refs_3_, bf16[256,256]{1,0:T(8,128)(2,1)S(1)} %copy-done.3, ...), custom_call_target="tpu_custom_call" | custom-call | tf_op jit(solution)/shard_map/forward/pallas_call | solution.py:229
  152.6 14.6 %all-gather.14.cloned.1.call-done.refs_1_ = bf16[8,2,256,256]{3,2,1,0:T(8,128)(2,1)} async-done(((bf16[1,2,256,256]{3,2,1,0:T(8,128)(2,1)}), bf16[8,2,256,256]{3,2,1,0:T(8,128)(2,1)}) %all-gather.14.cloned.1.call-update) | async-done | bytes 2097168 | tf_op jit(solution)/shard_map/all_gather | solution.py:285
  167.2 1.6 copy-done.7
  168.8 11.2 %forward.7 = (f32[2,256,256]{2,1,0:T(8,128)S(1)}, f32[2,256,256]{2,1,0:T(8,128)S(1)}) custom-call(s32[1]{0:T(128)} %bitcast.refs_0_, bf16[8,2,256,256]{3,2,1,0:T(8,128)(2,1)S(1)} %copy-done.7, f32[2,256,256]{2,1,0:T(8,128)S(1)} %get-tuple-element.22.refs_2_, f32[2,256,256]{2,1,0:T(8,128)S(1)} %pad_maximum_fusion.1.refs_3_, bf16[256,256]{1,0:T(8,128)(2,1)S(1)} %copy-done.3, ...), custom_call_target="tpu_custom_call" | custom-call | tf_op jit(solution)/shard_map/forward/pallas_call | solution.py:229
  180.0 14.3 %backward.4 = (f32[2,256,256]{2,1,0:T(8,128)S(1)}, f32[2,512,512]{2,1,0:T(8,128)}) custom-call(s32[3]{0:T(128)S(1)} %pad_add_fusion.refs_0_, bf16[8,2,256,256]{3,2,1,0:T(8,128)(2,1)} %all-gather.14.cloned.1.call-done.refs_1_, f32[2,256,256]{2,1,0:T(8,128)S(1)} %get-tuple-element.23.refs_2_, f32[2,256,256]{2,1,0:T(8,128)S(1)} %pad_maximum_fusion.1.refs_3_, ...), custom_call_target="tpu_custom_call" | custom-call | tf_op jit(solution)/shard_map/backward/pallas_call | solution.py:247
  194.2 14.2 %backward.5 = (f32[2,256,256]{2,1,0:T(8,128)S(1)}, f32[2,512,512]{2,1,0:T(8,128)}) custom-call(s32[3]{0:T(128)S(1)} %pad_add_fusion.refs_0_, bf16[8,2,256,256]{3,2,1,0:T(8,128)(2,1)} %all-gather.12.cloned.1.call-done.refs_1_, f32[2,256,256]{2,1,0:T(8,128)S(1)} %get-tuple-element.25.refs_2_, f32[2,256,256]{2,1,0:T(8,128)S(1)} %pad_maximum_fusion.1.refs_3_, ...), custom_call_target="tpu_custom_call" | custom-call | tf_op jit(solution)/shard_map/backward/pallas_call | solution.py:247
  208.4 14.3 %backward.6 = (f32[2,256,256]{2,1,0:T(8,128)S(1)}, f32[2,512,512]{2,1,0:T(8,128)}) custom-call(s32[3]{0:T(128)S(1)} %pad_add_fusion.refs_0_, bf16[8,2,256,256]{3,2,1,0:T(8,128)(2,1)} %all-gather.10.cloned.1.call-done.refs_1_, f32[2,256,256]{2,1,0:T(8,128)S(1)} %get-tuple-element.27.refs_2_, f32[2,256,256]{2,1,0:T(8,128)S(1)} %pad_maximum_fusion.1.refs_3_, ...), custom_call_target="tpu_custom_call" | custom-call | tf_op jit(solution)/shard_map/backward/pallas_call | solution.py:247
  222.7 14.4 %backward.7 = (f32[2,256,256]{2,1,0:T(8,128)}, f32[2,512,512]{2,1,0:T(8,128)}) custom-call(s32[3]{0:T(128)S(1)} %pad_add_fusion.refs_0_, bf16[8,2,256,256]{3,2,1,0:T(8,128)(2,1)} %all-gather.8.cloned.1.call-done.refs_1_, f32[2,256,256]{2,1,0:T(8,128)S(1)} %get-tuple-element.29.refs_2_, f32[2,256,256]{2,1,0:T(8,128)S(1)} %pad_maximum_fusion.1.refs_3_, ...), custom_call_target="tpu_custom_call" | custom-call | tf_op jit(solution)/shard_map/backward/pallas_call | solution.py:247
  239.4 72.5 %reduce-scatter.5.cloned.1.call-done = f32[2,32,512]{2,1,0:T(8,128)} async-done(((f32[2,512,512]{2,1,0:T(8,128)}), f32[2,32,512]{2,1,0:T(8,128)}) %reduce-scatter.5.cloned.1.call-update) | async-done | bytes 131088 | tf_op jit(solution)/shard_map/reduce_scatter | solution.py:303
  311.9 77.2 %reduce-scatter.7.cloned.1.call-done = f32[2,32,512]{2,1,0:T(8,128)} async-done(((f32[2,512,512]{2,1,0:T(8,128)}), f32[2,32,512]{2,1,0:T(8,128)}) %reduce-scatter.7.cloned.1.call-update) | async-done | bytes 131088 | tf_op jit(solution)/shard_map/reduce_scatter | solution.py:303
  389.1 76.9 %reduce-scatter.9.cloned.1.call-done = f32[2,32,512]{2,1,0:T(8,128)} async-done(((f32[2,512,512]{2,1,0:T(8,128)}), f32[2,32,512]{2,1,0:T(8,128)}) %reduce-scatter.9.cloned.1.call-update) | async-done | bytes 131088 | tf_op jit(solution)/shard_map/reduce_scatter | solution.py:303
  465.9 77.2 %reduce-scatter.11.cloned.1.call-done = f32[2,32,512]{2,1,0:T(8,128)} async-done(((f32[2,512,512]{2,1,0:T(8,128)}), f32[2,32,512]{2,1,0:T(8,128)}) %reduce-scatter.11.cloned.1.call-update) | async-done | bytes 131088 | tf_op jit(solution)/shard_map/reduce_scatter | solution.py:303
  543.2 1.1 pad_maximum_fusion.2
  544.3 11.7 %all_to_all.11 = f32[4,2,32,512]{3,2,1,0:T(8,128)S(1)} all-to-all(f32[4,2,32,512]{3,2,1,0:T(8,128)S(1)} %pad_maximum_fusion.2), channel_id=1, replica_groups=mesh['y'=4,'zc'=8,'x'=4] {'y'}, dimensions={0} | all-to-all | bytes 1048576 | tf_op jit(solution)/shard_map/all_to_all | solution.py:304
  556.1 0.8 copy.15
  (68 shorter events, 10.2 us)
Async XLA Ops:
  6.5 28.9 %all-gather.6.cloned.1.call-start = ((), (), s32[]{:S(2)}) async-start(), calls=%async_computation.6 | async-start | bytes 1310720 | tf_op jit(solution)/shard_map/all_gather | solution.py:282
  7.3 77.8 %all-gather.8.cloned.1.call-start = ((), (), s32[]{:S(2)}) async-start(), calls=%async_computation.7 | async-start | bytes 2359296 | tf_op jit(solution)/shard_map/all_gather | solution.py:285
  35.4 1.2 copy-start.8
  36.7 0.7 copy-start.11
  37.3 0.7 copy-start.13
  59.9 3.0 copy-start.12
  59.9 3.6 copy-start.14
  59.9 5.6 copy-start.15
  59.9 5.6 copy-start.17
  59.9 5.6 copy-start.18
  61.0 51.6 %all-gather.10.cloned.1.call-start = ((), (), s32[]{:S(2)}) async-start(), calls=%async_computation.8 | async-start | bytes 2359296 | tf_op jit(solution)/shard_map/all_gather | solution.py:285
  61.7 78.2 %all-gather.12.cloned.1.call-start = ((), (), s32[]{:S(2)}) async-start(), calls=%async_computation.9 | async-start | bytes 2359296 | tf_op jit(solution)/shard_map/all_gather | solution.py:285
  62.3 104.9 %all-gather.14.cloned.1.call-start = ((), (), s32[]{:S(2)}) async-start(), calls=%async_computation.10 | async-start | bytes 2359296 | tf_op jit(solution)/shard_map/all_gather | solution.py:285
  62.9 249.0 %reduce-scatter.5.cloned.1.call-start = ((), (), s32[]{:S(2)}) async-start(), calls=%async_computation.11 | async-start | bytes 2228224 | tf_op jit(solution)/shard_map/reduce_scatter | solution.py:303
  65.5 1.0 copy-start.16
  67.7 17.4 %copy-start = (bf16[256,256]{1,0:T(8,128)(2,1)S(1)}, bf16[256,256]{1,0:T(8,128)(2,1)}, u32[]{:S(2)}) copy-start(bf16[256,256]{1,0:T(8,128)(2,1)} %constant.36.clone.refs_7_) | copy-start | bytes 393220
  67.7 17.4 %copy-start.1 = (bf16[256,256]{1,0:T(8,128)(2,1)S(1)}, bf16[256,256]{1,0:T(8,128)(2,1)}, u32[]{:S(2)}) copy-start(bf16[256,256]{1,0:T(8,128)(2,1)} %constant.35.clone.refs_6_) | copy-start | bytes 393220
  67.7 17.4 %copy-start.2 = (bf16[256,256]{1,0:T(8,128)(2,1)S(1)}, bf16[256,256]{1,0:T(8,128)(2,1)}, u32[]{:S(2)}) copy-start(bf16[256,256]{1,0:T(8,128)(2,1)} %constant.34.clone.refs_5_) | copy-start | bytes 393220
  67.7 17.4 %copy-start.3 = (bf16[256,256]{1,0:T(8,128)(2,1)S(1)}, bf16[256,256]{1,0:T(8,128)(2,1)}, u32[]{:S(2)}) copy-start(bf16[256,256]{1,0:T(8,128)(2,1)} %constant.33.clone.refs_4_) | copy-start | bytes 393220
  85.1 1.6 copy-start.4
  112.6 1.6 copy-start.5
  124.2 0.8 copy-start.9
  139.9 1.6 copy-start.6
  141.5 1.0 copy-start.10
  167.2 1.6 copy-start.7
  237.1 152.0 %reduce-scatter.7.cloned.1.call-start = ((), (), s32[]{:S(2)}) async-start(), calls=%async_computation.12 | async-start | bytes 2228224 | tf_op jit(solution)/shard_map/reduce_scatter | solution.py:303
  237.9 228.1 %reduce-scatter.9.cloned.1.call-start = ((), (), s32[]{:S(2)}) async-start(), calls=%async_computation.13 | async-start | bytes 2228224 | tf_op jit(solution)/shard_map/reduce_scatter | solution.py:303
  238.6 304.6 %reduce-scatter.11.cloned.1.call-start = ((), (), s32[]{:S(2)}) async-start(), calls=%async_computation.14 | async-start | bytes 2228224 | tf_op jit(solution)/shard_map/reduce_scatter | solution.py:303
Sparse Core Ops, SparseCore 0:
  9.0 26.3 all-gather.5
  61.1 23.9 all-gather.7
  86.8 25.7 all-gather.9
  114.2 25.7 all-gather.11
  141.5 25.6 all-gather.13
  237.2 74.6 reduce-scatter.4
  315.5 73.5 reduce-scatter.6
  392.3 73.5 reduce-scatter.8
  469.6 73.5 reduce-scatter.10

commit v2 on v1

--- a/solution.py
+++ b/solution.py
@@ -152,12 +152,16 @@
     return jnp.where(at < M, at, N + M - 1 - at)
 
 
-def chosen(start, shape, window_axis):
-    window = paired_index(shape, window_axis) + start
-    return jnp.where(window == lax.broadcasted_iota(jnp.int32, shape, 1 - window_axis), 1.0, 0.0).astype(BF16)
-
-
-def backward_kernel(steps, width, height, scalars, obj_ref, ct_ref, prop_ref, cr, sr, cl, sl, kept_ref, out_ref, region_ref, grad_ref):
+def one_hot(a, b):
+    return jnp.where(a == b, 1.0, 0.0).astype(BF16)
+
+
+def iota(shape, axis):
+    return lax.broadcasted_iota(jnp.int32, shape, axis)
+
+
+def backward_kernel(steps, scalars, obj_ref, ct_ref, prop_ref, cr, sr, cl, sl, kept_ref, *rest):
+    out_ref, sent_ref, grad_ref = rest[-3:]
     step = pl.program_id(0)
     tabs = (cr[...], sr[...], cl[...], sl[...])
 
@@ -179,21 +183,49 @@
 
     @pl.when(step == steps - 1)
     def _():
-        rows = chosen(scalars[1], (height, N), 1)
-        cols = chosen(scalars[2], (N, width), 0)
+        at = iota((N, N), 0)
+        slot = M * (at // 8 % 2) + 8 * (at // 16) + at % 8
+        rows = one_hot((paired_index((N, N), 1) + scalars[1]) % N, slot)
+        cols = one_hot((paired_index((N, N), 0) + scalars[2]) % N, iota((N, N), 1))
         for part in (0, 1):
             high, low = split(grad_ref[part])
-            spread = [dot(rows, dot(x, cols).astype(BF16)) for x in (high, low)]
-            region_ref[part] = spread[0] + spread[1]
-
-
-def cut_kernel(rows_ref, cols_ref, obj_ref, out_ref):
-    height, width = obj_ref.shape[-2:]
+            rolled = [dot(rows, dot(x, cols).astype(BF16)) for x in (high, low)]
+            sent_ref[:, 0, part] = (rolled[0] + rolled[1]).reshape(16, 16, N)
+
+
+def reduce_kernel(count, scalars, rows_ref, cols_ref, got_ref, out_ref):
+    at = iota((16, N), 0)
+    slot = M * (at // 8) + 8 * scalars[0] + at % 8
+    lane = iota((16, N), 1)
+    for part in (0, 1):
+        sums = [jnp.zeros((16, N), F32)] * 4
+        for p in range(count):
+            value = got_ref[p, 0, part]
+            low, wide = slot < rows_ref[p], lane < cols_ref[p]
+            zero = jnp.zeros_like(value)
+            below, above = jnp.where(low, value, zero), jnp.where(low, zero, value)
+            for i, rows in enumerate((above, below)):
+                sums[2 * i] += jnp.where(wide, zero, rows)
+                sums[2 * i + 1] += jnp.where(wide, rows, zero)
+        for strip in range(4):
+            half, fold = strip % 2, strip // 2
+            for side in (0, 1):
+                out_ref[strip, 0, part, :, side * N : side * N + N] = sums[2 * fold + side][8 * half : 8 * half + 8]
+
+
+def cut_kernel(rows_ref, cols_ref, starts_ref, *refs):
+    blocks, out_ref = refs[:-1], refs[-1]
+    strip, width = blocks[0].shape[-2:]
+    height = strip * len(blocks)
     at = pl.program_id(0)
-    rows = chosen(rows_ref[at], (N, height), 0)
-    cols = chosen(cols_ref[at], (width, N), 1)
+    held = iota((N, height), 1) % strip
+    for i in range(len(blocks)):
+        held += jnp.where(iota((N, height), 1) // strip == i, starts_ref[i], 0)
+    rows = one_hot(paired_index((N, height), 0) + rows_ref[at], held)
+    cols = one_hot(paired_index((width, N), 1) + cols_ref[at], iota((width, N), 0))
     for part in (0, 1):
-        out_ref[0, part] = dot(dot(rows, obj_ref[part, 0]).astype(BF16), cols).astype(BF16)
+        whole_part = jnp.concatenate([block[part, 0] for block in blocks], axis=0)
+        out_ref[0, part] = dot(dot(rows, whole_part).astype(BF16), cols).astype(BF16)
 
 
 def whole(shape):
@@ -205,17 +237,17 @@
 WAVE = (2, N, N)
 
 
-def cut(full, pos_rows, pos_cols):
+def cut(blocks, starts, pos_rows, pos_cols):
     count = pos_rows.shape[0]
     return pl.pallas_call(
         cut_kernel,
         grid=(count,),
-        in_specs=[SMEM, SMEM, whole(full.shape)],
+        in_specs=[SMEM] * 3 + [whole(blocks[0].shape)] * len(blocks),
         out_specs=pl.BlockSpec((1, 2, N, N), lambda i: (i, 0, 0, 0)),
         out_shape=jax.ShapeDtypeStruct((count, 2, N, N), BF16),
         compiler_params=PARAMS,
         name="cut",
-    )(pos_rows, pos_cols, full)
+    )(pos_rows, pos_cols, starts, *blocks)
 
 
 def run_forward(mine, chunk, wave, prop, tabs, gain, inten=None):
@@ -238,24 +270,49 @@
     )(mine, chunk, wave, prop, *tabs, *extra)
 
 
-def run_backward(scalars, chunk, ct, prop, tabs, kept, height, width):
+def run_backward(scalars, chunk, ct, prop, tabs, kept, index, count, sent=None):
     steps = chunk.shape[0]
 
     def body(*refs):
-        backward_kernel(steps, width, height, *refs)
-
+        backward_kernel(steps, *refs)
+
+    more = () if sent is None else (sent,)
     return pl.pallas_call(
         body,
         grid=(steps,),
         in_specs=[SMEM, pl.BlockSpec((1, 2, N, N), lambda i: (steps - 1 - i, 0, 0, 0)), whole(WAVE), whole(WAVE)]
         + [whole((N, N))] * 4
-        + [whole(WAVE)],
-        out_specs=[whole(WAVE), whole((2, height, width))],
-        out_shape=[jax.ShapeDtypeStruct(WAVE, F32), jax.ShapeDtypeStruct((2, height, width), F32)],
+        + [whole(WAVE)]
+        + [pl.BlockSpec(memory_space=pl.ANY)] * len(more),
+        out_specs=[whole(WAVE), pl.BlockSpec((16, 1, 2, 16, N), lambda i: (0, index, 0, 0, 0))],
+        out_shape=[jax.ShapeDtypeStruct(WAVE, F32), jax.ShapeDtypeStruct((16, count, 2, 16, N), F32)],
         scratch_shapes=[pltpu.VMEM(WAVE, F32)],
+        input_output_aliases={9: 1} if more else {},
         compiler_params=PARAMS,
         name="backward",
-    )(scalars, chunk, ct, prop, *tabs, kept)
+    )(scalars, chunk, ct, prop, *tabs, kept, *more)
+
+
+def run_reduce(piece, all_rows, all_cols, got):
+    sources, count = got.shape[:2]
+
+    def body(*refs):
+        reduce_kernel(sources, *refs)
+
+    return pl.pallas_call(
+        body,
+        grid=(count,),
+        in_specs=[SMEM] * 3 + [pl.BlockSpec((sources, 1, 2, 16, N), lambda i: (0, i, 0, 0, 0))],
+        out_specs=pl.BlockSpec((4, 1, 2, 8, 2 * N), lambda i: (0, i, 0, 0, 0)),
+        out_shape=jax.ShapeDtypeStruct((4, count, 2, 8, 2 * N), F32),
+        compiler_params=PARAMS,
+        name="reduce",
+    )(piece, all_rows, all_cols, got)
+
+
+def from_neighbour(block, axis, distance):
+    size = lax.axis_size(axis)
+    return lax.ppermute(block, axis, [(i, (i + distance) % size) for i in range(size)])
 
 
 def paired(x):
@@ -274,15 +331,17 @@
 
 
 def on_device(probe_wave, object_field, pos_rows, pos_cols, intensity, prop_phase):
-    row = lax.axis_index("y")
+    row, tile = lax.axis_index("y"), lax.axis_index("x")
     mine = lax.axis_index("zc").astype(jnp.int32)
     chunks_count = lax.axis_size("y")
-    height = object_field.shape[2] * lax.axis_size("x")
-    width = object_field.shape[3]
-    full = lax.all_gather(object_field, "x", axis=2, tiled=True)
-    patches = cut(full, pos_rows, pos_cols)
+    strip, width = object_field.shape[2:]
+    moves = (0, 1, 3, 2)
+    blocks = [object_field] + [from_neighbour(object_field, "x", d) for d in moves[1:]]
+    starts = jnp.stack([(tile - d) % 4 for d in moves]).astype(jnp.int32) * strip
+    patches = cut(blocks, starts, pos_rows, pos_cols)
     patches = lax.all_to_all(patches, "y", 0, 0, tiled=True)
     chunks = [lax.all_gather(patches[i], "zc", axis=0) for i in range(chunks_count)]
+    all_rows, all_cols = lax.all_gather(jnp.stack([pos_rows, pos_cols]), "x", axis=1, tiled=True)
 
     *tabs, gain = tables()
     tabs = [jnp.asarray(t) for t in tabs]
@@ -297,13 +356,14 @@
         last = i == chunks_count - 1
         wave, saved = run_forward(mine_at, chunks[i], wave, prop, tabs, gain, inten if last else None)
         kept.append(saved)
-    pieces = [None] * chunks_count
+    sent = None
     for i in reversed(range(chunks_count)):
-        wave, region = run_backward(scalars, chunks[i], wave, prop, tabs, kept[i], height, width)
-        pieces[i] = lax.psum_scatter(region, ("x", "y"), scatter_dimension=1, tiled=True)
-    out = lax.all_to_all(jnp.stack(pieces), "y", 0, 0, tiled=True)
-    out = jnp.transpose(out, (1, 0, 2, 3)).reshape(2, 1, object_field.shape[2], width)
-    return out
+        wave, sent = run_backward(scalars, chunks[i], wave, prop, tabs, kept[i], i, chunks_count, sent)
+    got = lax.all_to_all(sent, ("x", "y"), 0, 0, tiled=True)
+    piece = (tile * 4 + row).astype(jnp.int32)[None]
+    sums = run_reduce(piece, all_rows, all_cols, got).reshape(16, 2, 8, width)
+    out = lax.all_to_all(sums, ("x", "y"), 0, 0, tiled=True)
+    return jnp.transpose(out, (1, 0, 2, 3)).reshape(2, 1, strip, width)
 
 
 def solution(mesh):

time: 564 us -> 283 us (0.50)
  waiting for transfers between devices: 397 us -> 74.6 us
  blocking collectives: 30 us -> 63.6 us
  starting transfers between devices: 0.31 us -> 12.1 us
    reduce_scatter x4 -> x0, waiting for transfers between devices: 304 us -> none  [on_device(): lax.psum_scatter(region, ('x', 'y'), scatter_dimension=1, tiled=True)]
    all_gather x0 -> x1, blocking collectives: none -> 30.1 us  [on_device(): lax.all_gather(jnp.stack([pos_rows, pos_cols]), 'x', axis=1, tiled=True)]
    all_gather x1 -> x0, waiting for transfers between devices: 28.1 us -> none  [on_device(): full = lax.all_gather(object_field, 'x', axis=2, tiled=True)]
    ppermute x0 -> x3, waiting for transfers between devices: none -> 10.9 us  [from_neighbour(): lax.ppermute(block, axis, [(i, (i + distance) % size) for i in range(size)])]
    all_to_all x0 -> x1, starting transfers between devices: none -> 6.81 us  [on_device(): got = lax.all_to_all(sent, ('x', 'y'), 0, 0, tiled=True)]
  transfers between devices with their start and end apart: 9 -> 8, of which waited for: 9 -> 8; matrix products, arithmetic and copies ran while one was open for 1% -> 2% of each run, Pallas kernels for 5% -> 11%
where the time goes in v2:
time: 283 us; the launch traced here: 282 us
  Pallas kernels  99.5 us (35%)
  waiting for transfers between devices  74.6 us (26%)
  blocking collectives  63.6 us (22%)
  local copies, waits for them, and re-layouts  17.4 us (6%)
  between operations  13.4 us (5%)
  starting transfers between devices  12.1 us (4%)
    all_gather x4, waiting for transfers between devices, on_device(): lax.all_gather(patches[i], 'zc', axis=0)  61.1 us
    pallas_call x4, Pallas kernels, run_backward(): pl.pallas_call(body, grid=(steps,), in_specs=[SMEM, pl.BlockSpec((1, 2, N...  52.7 us
    pallas_call x4, Pallas kernels, run_forward(): pl.pallas_call(body, grid=(steps,), in_specs=[SMEM, pl.BlockSpec((1, 2, N...  41.2 us
    all_gather x1, blocking collectives, on_device(): lax.all_gather(jnp.stack([pos_rows, pos_cols]), 'x', axis=1, tiled=True)  30.1 us
    all_to_all x1, blocking collectives, on_device(): patches = lax.all_to_all(patches, 'y', 0, 0, tiled=True)  18.5 us
    all_to_all x1, blocking collectives, on_device(): out = lax.all_to_all(sums, ('x', 'y'), 0, 0, tiled=True)  15.1 us
    unnamed x39, local copies, waits for them, and re-layouts  11.1 us
    ppermute x3, waiting for transfers between devices, from_neighbour(): lax.ppermute(block, axis, [(i, (i + distance) % size) for i in range(size)])  10.9 us
  transfers between devices with their start and end apart: 8, of which 8 were waited for; matrix products, arithmetic and copies ran while one was open for 2% of the time, Pallas kernels for 11%

profile of v2, /device:TPU:0, one launch (start us, length us, event | category | flops | bytes accessed | tf_op | source)
XLA Modules:
  0.0 282.3 jit_solution(16340163909013210629)
XLA Ops:
  6.5 1.6 collective-permute-start
  8.1 1.7 collective-permute-start.1
  9.8 1.9 collective-permute-start.2
  11.7 4.1 %collective-permute-done.refs_1_ = bf16[2,1,128,512]{3,2,1,0:T(8,128)(2,1)S(1)} collective-permute-done((bf16[2,1,128,512]{3,2,1,0:T(8,128)(2,1)}, bf16[2,1,128,512]{3,2,1,0:T(8,128)(2,1)S(1)}, u32[]{:S(2)}, u32[]{:S(2)}) %collective-permute-start) | collective-permute-done | bytes 262176 | tf_op jit(solution)/shard_map/ppermute | solution.py:315
  15.9 1.7 collective-permute-done.1.refs_2_
  17.6 5.1 %collective-permute-done.2.refs_3_ = bf16[2,1,128,512]{3,2,1,0:T(8,128)(2,1)S(1)} collective-permute-done((bf16[2,1,128,512]{3,2,1,0:T(8,128)(2,1)}, bf16[2,1,128,512]{3,2,1,0:T(8,128)(2,1)S(1)}, u32[]{:S(2)}, u32[]{:S(2)}) %collective-permute-start.2) | collective-permute-done | bytes 262176 | tf_op jit(solution)/shard_map/ppermute | solution.py:315
  25.0 3.6 %cut.1 = bf16[4,2,256,256]{3,2,1,0:T(8,128)(2,1)S(1)} custom-call(s32[4]{0:T(128)S(1)} %copy-done.13, s32[4]{0:T(128)S(1)} %copy-done.11, s32[4]{0:T(128)S(1)} %add_multiply_fusion.starts_ref, bf16[2,1,128,512]{3,2,1,0:T(8,128)(2,1)S(1)} %copy-done.10, bf16[2,1,128,512]{3,2,1,0:T(8,128)(2,1)S(1)} %collective-permute-done.refs_1_, ...), custom_call_target="tpu_custom_call" | custom-call | tf_op jit(solution)/shard_map/cut/pallas_call | solution.py:242
  28.6 18.5 %all_to_all.15 = bf16[4,2,256,256]{3,2,1,0:T(8,128)(2,1)S(1)} all-to-all(bf16[4,2,256,256]{3,2,1,0:T(8,128)(2,1)S(1)} %cut.1), channel_id=1, replica_groups=mesh['y'=4,'zc'=8,'x'=4] {'y'}, dimensions={0} | all-to-all | bytes 2097152 | tf_op jit(solution)/shard_map/all_to_all | solution.py:342
  47.1 1.0 fusion.4
  54.2 1.1 dynamic-slice_bitcast_fusion.1
  55.5 1.3 pad_add_fusion.refs_0_
  56.9 15.7 %all-gather.6.cloned.1.call-done.refs_1_ = bf16[8,2,256,256]{3,2,1,0:T(8,128)(2,1)} async-done(((bf16[1,2,256,256]{3,2,1,0:T(8,128)(2,1)}), bf16[8,2,256,256]{3,2,1,0:T(8,128)(2,1)}) %all-gather.6.cloned.1.call-update) | async-done | bytes 2097168 | tf_op jit(solution)/shard_map/all_gather | solution.py:343
  72.6 1.6 copy-done.4
  74.2 10.0 %forward.4 = (f32[2,256,256]{2,1,0:T(8,128)S(1)}, f32[2,256,256]{2,1,0:T(8,128)S(1)}) custom-call(s32[1]{0:T(128)} %bitcast.8.refs_0_, bf16[8,2,256,256]{3,2,1,0:T(8,128)(2,1)S(1)} %copy-done.4, f32[2,256,256]{2,1,0:T(8,128)S(1)} %pad_maximum_fusion.refs_2_, f32[2,256,256]{2,1,0:T(8,128)S(1)} %pad_maximum_fusion.1.refs_3_, bf16[256,256]{1,0:T(8,128)(2,1)S(1)} %copy-done, ...), custom_call_target="tpu_custom_call" | custom-call | tf_op jit(solution)/shard_map/forward/pallas_call | solution.py:261
  84.2 15.6 %all-gather.8.cloned.1.call-done.refs_1_ = bf16[8,2,256,256]{3,2,1,0:T(8,128)(2,1)} async-done(((bf16[1,2,256,256]{3,2,1,0:T(8,128)(2,1)}), bf16[8,2,256,256]{3,2,1,0:T(8,128)(2,1)}) %all-gather.8.cloned.1.call-update) | async-done | bytes 2097168 | tf_op jit(solution)/shard_map/all_gather | solution.py:343
  99.9 1.6 copy-done.5
  101.5 10.0 %forward.5 = (f32[2,256,256]{2,1,0:T(8,128)S(1)}, f32[2,256,256]{2,1,0:T(8,128)S(1)}) custom-call(s32[1]{0:T(128)} %bitcast.8.refs_0_, bf16[8,2,256,256]{3,2,1,0:T(8,128)(2,1)S(1)} %copy-done.5, f32[2,256,256]{2,1,0:T(8,128)S(1)} %get-tuple-element.20.refs_2_, f32[2,256,256]{2,1,0:T(8,128)S(1)} %pad_maximum_fusion.1.refs_3_, bf16[256,256]{1,0:T(8,128)(2,1)S(1)} %copy-done, ...), custom_call_target="tpu_custom_call" | custom-call | tf_op jit(solution)/shard_map/forward/pallas_call | solution.py:261
  112.3 15.1 %all-gather.10.cloned.1.call-done.refs_1_ = bf16[8,2,256,256]{3,2,1,0:T(8,128)(2,1)} async-done(((bf16[1,2,256,256]{3,2,1,0:T(8,128)(2,1)}), bf16[8,2,256,256]{3,2,1,0:T(8,128)(2,1)}) %all-gather.10.cloned.1.call-update) | async-done | bytes 2097168 | tf_op jit(solution)/shard_map/all_gather | solution.py:343
  127.4 1.6 copy-done.6
  129.0 1.0 copy-done.9
  130.0 10.0 %forward.6 = (f32[2,256,256]{2,1,0:T(8,128)S(1)}, f32[2,256,256]{2,1,0:T(8,128)S(1)}) custom-call(s32[1]{0:T(128)} %bitcast.8.refs_0_, bf16[8,2,256,256]{3,2,1,0:T(8,128)(2,1)S(1)} %copy-done.6, f32[2,256,256]{2,1,0:T(8,128)S(1)} %copy-done.9, f32[2,256,256]{2,1,0:T(8,128)S(1)} %pad_maximum_fusion.1.refs_3_, bf16[256,256]{1,0:T(8,128)(2,1)S(1)} %copy-done, ...), custom_call_target="tpu_custom_call" | custom-call | tf_op jit(solution)/shard_map/forward/pallas_call | solution.py:261
  140.0 14.7 %all-gather.12.cloned.1.call-done.refs_1_ = bf16[8,2,256,256]{3,2,1,0:T(8,128)(2,1)} async-done(((bf16[1,2,256,256]{3,2,1,0:T(8,128)(2,1)}), bf16[8,2,256,256]{3,2,1,0:T(8,128)(2,1)}) %all-gather.12.cloned.1.call-update) | async-done | bytes 2097168 | tf_op jit(solution)/shard_map/all_gather | solution.py:343
  154.7 1.6 copy-done.7
  156.3 11.2 %forward.7 = (f32[2,256,256]{2,1,0:T(8,128)S(1)}, f32[2,256,256]{2,1,0:T(8,128)S(1)}) custom-call(s32[1]{0:T(128)} %bitcast.8.refs_0_, bf16[8,2,256,256]{3,2,1,0:T(8,128)(2,1)S(1)} %copy-done.7, f32[2,256,256]{2,1,0:T(8,128)S(1)} %get-tuple-element.22.refs_2_, f32[2,256,256]{2,1,0:T(8,128)S(1)} %pad_maximum_fusion.1.refs_3_, bf16[256,256]{1,0:T(8,128)(2,1)S(1)} %copy-done, ...), custom_call_target="tpu_custom_call" | custom-call | tf_op jit(solution)/shard_map/forward/pallas_call | solution.py:261
  167.5 13.1 %backward.4 = (f32[2,256,256]{2,1,0:T(8,128)S(1)}, f32[16,4,2,16,256]{4,3,2,1,0:T(8,128)}) custom-call(s32[3]{0:T(128)S(1)} %pad_add_fusion.refs_0_, bf16[8,2,256,256]{3,2,1,0:T(8,128)(2,1)} %all-gather.12.cloned.1.call-done.refs_1_, f32[2,256,256]{2,1,0:T(8,128)S(1)} %get-tuple-element.23.refs_2_, f32[2,256,256]{2,1,0:T(8,128)S(1)} %pad_maximum_fusion.1.refs_3_, ...), custom_call_target="tpu_custom_call" | custom-call | tf_op jit(solution)/shard_map/backward/pallas_call | solution.py:280
  180.6 13.1 %backward.5 = (f32[2,256,256]{2,1,0:T(8,128)S(1)}, f32[16,4,2,16,256]{4,3,2,1,0:T(8,128)}) custom-call(s32[3]{0:T(128)S(1)} %pad_add_fusion.refs_0_, bf16[8,2,256,256]{3,2,1,0:T(8,128)(2,1)} %all-gather.10.cloned.1.call-done.refs_1_, f32[2,256,256]{2,1,0:T(8,128)S(1)} %get-tuple-element.25.refs_2_, ...), custom_call_target="tpu_custom_call", output_to_operand_aliasing={{1}: (9, {})} | custom-call | tf_op jit(solution)/shard_map/backward/pallas_call | solution.py:280
  193.7 13.1 %backward.6 = (f32[2,256,256]{2,1,0:T(8,128)S(1)}, f32[16,4,2,16,256]{4,3,2,1,0:T(8,128)}) custom-call(s32[3]{0:T(128)S(1)} %pad_add_fusion.refs_0_, bf16[8,2,256,256]{3,2,1,0:T(8,128)(2,1)} %all-gather.8.cloned.1.call-done.refs_1_, f32[2,256,256]{2,1,0:T(8,128)S(1)} %get-tuple-element.28.refs_2_, ...), custom_call_target="tpu_custom_call", output_to_operand_aliasing={{1}: (9, {})} | custom-call | tf_op jit(solution)/shard_map/backward/pallas_call | solution.py:280
  206.8 13.3 %backward.7 = (f32[2,256,256]{2,1,0:T(8,128)}, f32[16,4,2,16,256]{4,3,2,1,0:T(8,128)}) custom-call(s32[3]{0:T(128)S(1)} %pad_add_fusion.refs_0_, bf16[8,2,256,256]{3,2,1,0:T(8,128)(2,1)} %all-gather.6.cloned.1.call-done.refs_1_, f32[2,256,256]{2,1,0:T(8,128)S(1)} %get-tuple-element.31.refs_2_, ...), custom_call_target="tpu_custom_call", output_to_operand_aliasing={{1}: (9, {})} | custom-call | tf_op jit(solution)/shard_map/backward/pallas_call | solution.py:280
  220.1 6.8 %all-to-all-start.1 = ((f32[16,4,2,16,256]{4,3,2,1,0:T(8,128)}), f32[16,4,2,16,256]{4,3,2,1,0:T(8,128)S(1)}, u32[]{:S(2)}, u32[]{:S(2)}) async-start(f32[16,4,2,16,256]{4,3,2,1,0:T(8,128)} %get-tuple-element.34), calls=%async_computation.1 | async-start | bytes 4194304 | tf_op jit(solution)/shard_map/all_to_all | solution.py:362
  227.0 30.1 %all-gather = s32[4,4,2]{1,2,0:T(2,128)S(1)} all-gather(s32[1,4,2]{1,2,0:T(2,128)S(1)} %add_bitcast_fusion), channel_id=1, replica_groups=mesh['y'=4,'zc'=8,'x'=4] {'x'}, dimensions={0}, use_global_device_ids=true | all-gather | bytes 160 | tf_op jit(solution)/shard_map/all_gather | solution.py:344
  257.9 2.0 reduce.1
  259.9 15.1 %all_to_all.16 = f32[16,2,8,512]{3,2,1,0:T(8,128)S(1)} all-to-all(f32[16,2,8,512]{3,2,1,0:T(8,128)S(1)} %bitcast.33), channel_id=1, replica_groups=mesh['y'=4,'zc'=8,'x'=4] {'x','y'}, dimensions={0} | all-to-all | bytes 1048576 | tf_op jit(solution)/shard_map/all_to_all | solution.py:365
  (67 shorter events, 11.1 us)
Async XLA Ops:
  6.5 66.1 %all-gather.6.cloned.1.call-start = ((), (), s32[]{:S(2)}) async-start(), calls=%async_computation.3 | async-start | bytes 2359296 | tf_op jit(solution)/shard_map/all_gather | solution.py:343
  6.5 9.4 %collective-permute-start = (bf16[2,1,128,512]{3,2,1,0:T(8,128)(2,1)}, bf16[2,1,128,512]{3,2,1,0:T(8,128)(2,1)S(1)}, u32[]{:S(2)}, u32[]{:S(2)}) collective-permute-start(bf16[2,1,128,512]{3,2,1,0:T(8,128)(2,1)} %refs_0_.1), channel_id=1, source_target_pairs={{0,1},{1,2},{2,3},{3,0},{4,5},{5,6},{6,7},{7,4},{8,9},{9,10},{10,1... | collective-permute-start | bytes 786440 | tf_op jit(solution)/shard_map/ppermute | solution.py:315
  8.1 9.4 %collective-permute-start.1 = (bf16[2,1,128,512]{3,2,1,0:T(8,128)(2,1)}, bf16[2,1,128,512]{3,2,1,0:T(8,128)(2,1)S(1)}, u32[]{:S(2)}, u32[]{:S(2)}) collective-permute-start(bf16[2,1,128,512]{3,2,1,0:T(8,128)(2,1)} %refs_0_.1), channel_id=1, source_target_pairs={{0,3},{1,0},{2,1},{3,2},{4,7},{5,4},{6,5},{7,6},{8,11},{9,8},{10,9... | collective-permute-start | bytes 786440 | tf_op jit(solution)/shard_map/ppermute | solution.py:315
  9.8 12.9 %collective-permute-start.2 = (bf16[2,1,128,512]{3,2,1,0:T(8,128)(2,1)}, bf16[2,1,128,512]{3,2,1,0:T(8,128)(2,1)S(1)}, u32[]{:S(2)}, u32[]{:S(2)}) collective-permute-start(bf16[2,1,128,512]{3,2,1,0:T(8,128)(2,1)} %refs_0_.1), channel_id=1, source_target_pairs={{0,2},{1,3},{2,0},{3,1},{4,6},{5,7},{6,4},{7,5},{8,10},{9,11},{10,... | collective-permute-start | bytes 786440 | tf_op jit(solution)/shard_map/ppermute | solution.py:315
  22.7 1.0 copy-start.10
  23.6 0.7 copy-start.11
  24.3 0.7 copy-start.13
  47.1 3.1 %copy-start.14 = (s32[4]{0:T(128)S(1)}, s32[4]{0:T(128)}, u32[]{:S(2)}) copy-start(s32[4]{0:T(128)} %rows_ref.1) | copy-start | bytes 52
  47.1 3.6 %copy-start.12 = (s32[4]{0:T(128)S(1)}, s32[4]{0:T(128)}, u32[]{:S(2)}) copy-start(s32[4]{0:T(128)} %cols_ref.1) | copy-start | bytes 52
  47.1 4.2 %copy-start.16 = (f32[256,256]{1,0:T(8,128)S(1)}, f32[256,256]{1,0:T(8,128)}, u32[]{:S(2)}) copy-start(f32[256,256]{1,0:T(8,128)} %param.17) | copy-start | bytes 786436
  48.1 51.8 %all-gather.8.cloned.1.call-start = ((), (), s32[]{:S(2)}) async-start(), calls=%async_computation.4 | async-start | bytes 2359296 | tf_op jit(solution)/shard_map/all_gather | solution.py:343
  48.8 78.5 %all-gather.10.cloned.1.call-start = ((), (), s32[]{:S(2)}) async-start(), calls=%async_computation.5 | async-start | bytes 2359296 | tf_op jit(solution)/shard_map/all_gather | solution.py:343
  49.6 105.1 %all-gather.12.cloned.1.call-start = ((), (), s32[]{:S(2)}) async-start(), calls=%async_computation.6 | async-start | bytes 2359296 | tf_op jit(solution)/shard_map/all_gather | solution.py:343
  52.3 1.0 copy-start.15
  52.3 1.1 copy-start.17
  52.3 1.2 copy-start.18
  54.1 18.5 %copy-start = (bf16[256,256]{1,0:T(8,128)(2,1)S(1)}, bf16[256,256]{1,0:T(8,128)(2,1)}, u32[]{:S(2)}) copy-start(bf16[256,256]{1,0:T(8,128)(2,1)} %constant.68.clone.refs_4_) | copy-start | bytes 393220
  54.2 18.4 %copy-start.1 = (bf16[256,256]{1,0:T(8,128)(2,1)S(1)}, bf16[256,256]{1,0:T(8,128)(2,1)}, u32[]{:S(2)}) copy-start(bf16[256,256]{1,0:T(8,128)(2,1)} %constant.69.clone.refs_5_) | copy-start | bytes 393220
  54.2 18.4 %copy-start.2 = (bf16[256,256]{1,0:T(8,128)(2,1)S(1)}, bf16[256,256]{1,0:T(8,128)(2,1)}, u32[]{:S(2)}) copy-start(bf16[256,256]{1,0:T(8,128)(2,1)} %constant.70.clone.refs_6_) | copy-start | bytes 393220
  54.2 18.4 %copy-start.3 = (bf16[256,256]{1,0:T(8,128)(2,1)S(1)}, bf16[256,256]{1,0:T(8,128)(2,1)}, u32[]{:S(2)}) copy-start(bf16[256,256]{1,0:T(8,128)(2,1)} %constant.71.clone.refs_7_) | copy-start | bytes 393220
  72.6 1.6 copy-start.4
  99.9 1.6 copy-start.5
  111.5 0.8 copy-start.8
  127.4 1.6 copy-start.6
  129.0 1.0 copy-start.9
  154.7 1.6 copy-start.7
  220.1 37.7 %all-to-all-start.1 = ((f32[16,4,2,16,256]{4,3,2,1,0:T(8,128)}), f32[16,4,2,16,256]{4,3,2,1,0:T(8,128)S(1)}, u32[]{:S(2)}, u32[]{:S(2)}) async-start(f32[16,4,2,16,256]{4,3,2,1,0:T(8,128)} %get-tuple-element.34), calls=%async_computation.1 | async-start | bytes 4194304 | tf_op jit(solution)/shard_map/all_to_all | solution.py:362
Sparse Core Ops, SparseCore 0:
  48.2 24.3 all-gather.5
  74.3 25.5 all-gather.7
  101.6 25.7 all-gather.9
  128.9 25.7 all-gather.11

commit v3 on v2

v3 whole, which is shorter than its diff:
```python
import math

import jax
import jax.numpy as jnp
import ml_dtypes
import numpy as np
from jax import lax
from jax.experimental import pallas as pl
from jax.experimental.pallas import tpu as pltpu
from jax.sharding import Mesh, PartitionSpec as P

N = 256
M = N // 2
ROWS = 16
F32 = jnp.float32
BF16 = jnp.bfloat16


def tables():
    half = np.arange(M) + 0.5
    angles = 2.0 * math.pi / N * half[:, None] * half[None, :]
    packed, gain = [], []
    for values in (np.cos(angles) / 16.0, np.sin(angles) / 16.0):
        high = values.astype(ml_dtypes.bfloat16)
        low = (values - high.astype(np.float64)).astype(ml_dtypes.bfloat16)
        packed.append(np.block([[high, low], [high, low]]))
        both = high.astype(np.float64) + low.astype(np.float64)
        gain.append(4.0 * np.trace(both @ both) / M)
    at = np.arange(N)
    order = M * (at // ROWS % 2) + ROWS * (at // (2 * ROWS)) + at % ROWS
    lefts = [np.ascontiguousarray(table.T[order]) for table in packed]
    return *packed, *lefts, float(np.mean(gain)) ** 2


def split(x):
    high = x.astype(BF16)
    return high, (x - high.astype(F32)).astype(BF16)


def dot(a, b):
    return jnp.dot(a, b, preferred_element_type=F32)


def put_parts(ref, lead, at, value):
    high, low = split(value)
    ref[(*lead, pl.ds(at, ROWS), slice(0, M))] = high
    ref[(*lead, pl.ds(at, ROWS), slice(M, N))] = low


def put_folded(lhs_ref, part, at, values):
    for i, value in enumerate(values):
        put_parts(lhs_ref, (part, i % 2), M * (i // 2) + at, value)


def two_sided(lhs_ref, rhs_ref, tabs):
    cos_r, sin_r, cos_l, sin_l = tabs
    half = [[dot(lhs_ref[part, 0], cos_r), dot(lhs_ref[part, 1], sin_r)] for part in (0, 1)]
    out = []
    for part in (0, 1):
        for parity in (0, 1):
            for side in (0, 1):
                for at in range(0, M, ROWS):
                    rows = half[part][side][parity * M + at : parity * M + at + ROWS]
                    high, low = split(rows[:, :M] + rows[:, M:])
                    cols = slice(side * M, side * M + M)
                    rhs_ref[part, parity, at : at + ROWS, cols] = high
                    rhs_ref[part, parity, M + at : M + at + ROWS, cols] = low
        out.append([dot(cos_l, rhs_ref[part, 0]), dot(sin_l, rhs_ref[part, 1])])
    return out


def rows_of(out, part, at):
    got = []
    for parity in (0, 1):
        block = out[part][parity]
        rows = block[2 * at : 2 * at + ROWS] + block[2 * at + ROWS : 2 * at + 2 * ROWS]
        got += [rows[:, :M], rows[:, M:]]
    return got


def fold(x11, x12, x21, x22):
    d1, d2, s1, s2 = x11 - x21, x12 - x22, x11 + x21, x12 + x22
    return d1 - d2, d1 + d2, s1 - s2, s1 + s2


def unfold(uu, uv, vu, vv):
    p1, m1, p2, m2 = vv + uu, vv - uu, vu + uv, vu - uv
    return p1 + p2, m1 - m2, m1 + m2, p1 - p2


def spectrum_rows(out, at):
    ppr, pqr, qpr, qqr = rows_of(out, 0, at)
    ppi, pqi, qpi, qqi = rows_of(out, 1, at)
    ar, ai, br, bi = ppr - qqr, ppi - qqi, ppr + qqr, ppi + qqi
    er, ei, gr, gi = pqr + qpr, pqi + qpi, pqr - qpr, pqi - qpi
    return (ar + ei, br - gi, br + gi, ar - ei), (ai - er, bi + gr, bi - gr, ai + er)


def put_spectrum(lhs_ref, at, real, imag):
    yr11, yr12, yr21, yr22 = real
    yi11, yi12, yi21, yi22 = imag
    apr, api, amr, ami = yr11 + yr22, yi11 + yi22, yr11 - yr22, yi11 - yi22
    bpr, bpi, bmr, bmi = yr12 + yr21, yi12 + yi21, yr12 - yr21, yi12 - yi21
    put_folded(lhs_ref, 0, at, (apr + bpr, bmi - ami, -(ami + bmi), bpr - apr))
    put_folded(lhs_ref, 1, at, (api + bpi, amr - bmr, amr + bmr, bpi - api))


BLOCKS = range(0, M, ROWS)


def quads_at(ref, lead, at):
    return tuple(ref[(*lead, pl.ds(i * M + at, ROWS), slice(j * M, j * M + M))] for i in (0, 1) for j in (0, 1))


def put_quads(ref, part, at, values):
    for k, value in enumerate(values):
        ref[part, pl.ds(k // 2 * M + at, ROWS), slice(k % 2 * M, k % 2 * M + M)] = value


def times(ar, ai, br, bi):
    real = tuple(w * x - y * z for w, x, y, z in zip(ar, br, ai, bi))
    imag = tuple(w * z + y * x for w, x, y, z in zip(ar, br, ai, bi))
    return real, imag


def conj_times(ar, ai, br, bi):
    real = tuple(w * x + y * z for w, x, y, z in zip(ar, br, ai, bi))
    imag = tuple(w * z - y * x for w, x, y, z in zip(ar, br, ai, bi))
    return real, imag


def as_f32(values):
    return tuple(v.astype(F32) for v in values)


def load_pair(order, core, at, held, pair_ref):
    if len(held) == 2:
        pair_ref[core] = held[0][0, 0]
        pair_ref[1 - core] = held[1][0, 0]
        return
    for i in range(4):

        @pl.when(order[at] == i)
        def _():
            pair_ref[core] = held[i][...]
            pair_ref[1 - core] = held[4 + i][...]


def load_chunk(counts, refs, order, core, turn, at, pair_ref):
    first = 0
    for k, count in enumerate(counts):

        @pl.when(turn == k)
        def _(held=refs[first : first + count]):
            load_pair(order, core, at, held, pair_ref)

        first += count


def forward_kernel(gain, is_last, counts, stacks, order, scalars, *rest):
    held, (wave_ref, prop_ref, tabs_ref, *rest) = rest[: sum(counts)], rest[sum(counts) :]
    inten_ref, rest = (rest[0], rest[1:]) if is_last else (None, rest)
    out_ref, kept_ref, *stack_refs, pair_ref, lhs_ref, rhs_ref = rest
    step = pl.program_id(0)
    turn, at_z = step // 4, step % 4
    core = scalars[1]
    tabs = [tabs_ref[i] for i in range(4)]

    @pl.when(step == 0)
    def _():
        out_ref[...] = wave_ref[...]

    load_chunk(counts, held, order, core, turn, at_z, pair_ref)
    if stacks:
        stack_refs[0][0, 0] = pair_ref[core]
        stack_refs[1][0, 0] = pair_ref[1 - core]

    def one_slice(j, carry):
        @pl.when((at_z == scalars[0]) & (j == core))
        def _():
            kept_ref[turn] = out_ref[...]

        for at in BLOCKS:
            objr, obji = as_f32(quads_at(pair_ref, (j, 0), at)), as_f32(quads_at(pair_ref, (j, 1), at))
            mixed = times(quads_at(out_ref, (0,), at), quads_at(out_ref, (1,), at), objr, obji)
            for part in (0, 1):
                put_folded(lhs_ref, part, at, fold(*mixed[part]))
        spec = two_sided(lhs_ref, rhs_ref, tabs)
        for at in BLOCKS:
            real, imag = spectrum_rows(spec, at)
            put_spectrum(lhs_ref, at, *times(real, imag, quads_at(prop_ref, (0,), at), quads_at(prop_ref, (1,), at)))
        wave = two_sided(lhs_ref, rhs_ref, tabs)
        for at in BLOCKS:
            for part in (0, 1):
                put_quads(out_ref, part, at, unfold(*rows_of(wave, part, at)))
        return carry

    lax.fori_loop(0, 2, one_slice, 0)

    if is_last:

        @pl.when(step == pl.num_programs(0) - 1)
        def _():
            for at in BLOCKS:
                for part in (0, 1):
                    put_folded(lhs_ref, part, at, fold(*quads_at(out_ref, (part,), at)))
            spec = two_sided(lhs_ref, rhs_ref, tabs)
            for at in BLOCKS:
                real, imag = spectrum_rows(spec, at)
                measured = quads_at(inten_ref, (), at)
                scale = [(2.0 / gain) * (x * x + y * y - z) for x, y, z in zip(real, imag, measured)]
                put_spectrum(lhs_ref, at, [s * x for s, x in zip(scale, real)], [s * x for s, x in zip(scale, imag)])
            wave = two_sided(lhs_ref, rhs_ref, tabs)
            for at in BLOCKS:
                for part in (0, 1):
                    put_quads(out_ref, part, at, unfold(*rows_of(wave, part, at)))


def paired_index(shape, axis):
    at = lax.broadcasted_iota(jnp.int32, shape, axis)
    return jnp.where(at < M, at, N + M - 1 - at)


def one_hot(a, b):
    return jnp.where(a == b, 1.0, 0.0).astype(BF16)


def iota(shape, axis):
    return lax.broadcasted_iota(jnp.int32, shape, axis)


def backward_kernel(counts, order, scalars, *rest):
    chunks = len(counts)
    held, (ct_ref, prop_ref, tabs_ref, *rest) = rest[: sum(counts)], rest[sum(counts) :]
    kept_refs, rest = rest[:chunks], rest[chunks:]
    out_ref, sent_ref, grad_ref, mixed_ref, pair_ref, lhs_ref, rhs_ref = rest
    step = pl.program_id(0)
    chunk, at_z = chunks - 1 - step // 4, 3 - step % 4
    core = scalars[1]
    tabs = [tabs_ref[i] for i in range(4)]

    @pl.when(step == 0)
    def _():
        out_ref[...] = ct_ref[...]

    load_chunk(counts, held, order, core, chunk, at_z, pair_ref)

    def one_slice(turn, carry):
        j = 1 - turn
        for at in BLOCKS:
            for part in (0, 1):
                put_folded(lhs_ref, part, at, fold(*quads_at(out_ref, (part,), at)))
        spec = two_sided(lhs_ref, rhs_ref, tabs)
        for at in BLOCKS:
            prop = quads_at(prop_ref, (0,), at), quads_at(prop_ref, (1,), at)
            put_spectrum(lhs_ref, at, *conj_times(*prop, *spectrum_rows(spec, at)))
        wave = two_sided(lhs_ref, rhs_ref, tabs)
        for at in BLOCKS:
            mixed = [unfold(*rows_of(wave, part, at)) for part in (0, 1)]
            objr, obji = as_f32(quads_at(pair_ref, (j, 0), at)), as_f32(quads_at(pair_ref, (j, 1), at))
            back = conj_times(objr, obji, *mixed)
            for part in (0, 1):
                put_quads(mixed_ref, part, at, mixed[part])
                put_quads(out_ref, part, at, back[part])

        for k in range(chunks):

            @pl.when((chunk == k) & (at_z == scalars[0]) & (j == core))
            def _(kept_ref=kept_refs[k]):
                kr, ki, cr, ci = kept_ref[0, 0], kept_ref[0, 1], mixed_ref[0], mixed_ref[1]
                grad_ref[0] = kr * cr + ki * ci
                grad_ref[1] = kr * ci - ki * cr

        return carry

    lax.fori_loop(0, 2, one_slice, 0)

    @pl.when(at_z == 0)
    def _():
        at = iota((N, N), 0)
        slot = M * (at // 8 % 2) + 8 * (at // 16) + at % 8
        rows = one_hot((paired_index((N, N), 1) + scalars[2]) % N, slot)
        cols = one_hot((paired_index((N, N), 0) + scalars[3]) % N, iota((N, N), 1))
        for part in (0, 1):
            high, low = split(grad_ref[part])
            rolled = [dot(rows, dot(x, cols).astype(BF16)) for x in (high, low)]
            sent_ref[:, chunk, part] = (rolled[0] + rolled[1]).reshape(16, 16, N)


def reduce_kernel(count, scalars, tiles_ref, pos_ref, got_ref, out_ref):
    at = iota((16, N), 0)
    slot = M * (at // 8) + 8 * scalars[0] + at % 8
    lane = iota((16, N), 1)
    for part in (0, 1):
        sums = [jnp.zeros((16, N), F32)] * 4
        for p in range(count):
            value = got_ref[p, 0, part]
            held = tiles_ref[p // 4]
            low, wide = slot < pos_ref[held, 0, p % 4], lane < pos_ref[held, 1, p % 4]
            zero = jnp.zeros_like(value)
            below, above = jnp.where(low, value, zero), jnp.where(low, zero, value)
            for i, rows in enumerate((above, below)):
                sums[2 * i] += jnp.where(wide, zero, rows)
                sums[2 * i + 1] += jnp.where(wide, rows, zero)
        for strip in range(4):
            half, fold = strip % 2, strip // 2
            for side in (0, 1):
                out_ref[strip, 0, part, :, side * N : side * N + N] = sums[2 * fold + side][8 * half : 8 * half + 8]


def cut_kernel(rows_ref, cols_ref, starts_ref, *refs):
    blocks, out_ref = refs[:-1], refs[-1]
    strip, width = blocks[0].shape[-2:]
    height = strip * len(blocks)
    at = pl.program_id(0)
    held = iota((N, height), 1) % strip
    for i in range(len(blocks)):
        held += jnp.where(iota((N, height), 1) // strip == i, starts_ref[i], 0)
    rows = one_hot(paired_index((N, height), 0) + rows_ref[at], held)
    cols = one_hot(paired_index((width, N), 1) + cols_ref[at], iota((width, N), 0))
    for part in (0, 1):
        whole_part = jnp.concatenate([block[part, 0] for block in blocks], axis=0)
        out_ref[0, part] = dot(dot(rows, whole_part).astype(BF16), cols).astype(BF16)


def whole(shape):
    return pl.BlockSpec(shape, lambda *_: (0,) * len(shape))


SMEM = pl.BlockSpec(memory_space=pltpu.SMEM)
PARAMS = pltpu.CompilerParams(dimension_semantics=("arbitrary",), vmem_limit_bytes=24 << 20)
WAVE = (2, N, N)


def cost(chunks):
    return pl.CostEstimate(flops=chunks * 8 * 32 * N**3, bytes_accessed=chunks << 22, transcendentals=0)


def cut(blocks, starts, pos_rows, pos_cols):
    count = pos_rows.shape[0]
    return pl.pallas_call(
        cut_kernel,
        grid=(count,),
        in_specs=[SMEM] * 3 + [whole(blocks[0].shape)] * len(blocks),
        out_specs=pl.BlockSpec((1, 2, N, N), lambda i: (i, 0, 0, 0)),
        out_shape=jax.ShapeDtypeStruct((count, 2, N, N), BF16),
        compiler_params=PARAMS,
        name="cut",
    )(pos_rows, pos_cols, starts, *blocks)


def chunk_specs(chunks, reverse):
    specs, last = [], len(chunks) - 1
    for k, (blocks, at) in enumerate(chunks):
        if len(blocks) == 8:
            specs += [whole(WAVE)] * 8
            continue

        def block(i, *_, k=k, at=at):
            first = 4 * (last - k if reverse else k)
            inside = jnp.clip(i - first, 0, 3)
            return (3 - inside if reverse else inside, at, 0, 0, 0)

        specs += [pl.BlockSpec((1, 1, 2, N, N), block)] * 2
    return specs


def run_forward(order, scalars, chunks, wave, prop, tabs, gain, inten=None, stacks=False):
    counts = [len(blocks) for blocks, _ in chunks]
    last = inten is not None
    extra = (inten,) if last else ()

    def body(*refs):
        forward_kernel(gain, last, counts, stacks, *refs)

    kept = (len(chunks), *WAVE)
    stack = pl.BlockSpec((1, 1, 2, N, N), lambda i, *_: (i, 0, 0, 0, 0))
    return pl.pallas_call(
        body,
        grid_spec=pltpu.PrefetchScalarGridSpec(
            num_scalar_prefetch=2,
            grid=(4 * len(chunks),),
            in_specs=chunk_specs(chunks, False)
            + [whole(WAVE), whole(WAVE), whole((4, N, N))]
            + [whole((N, N))] * len(extra),
            out_specs=[whole(WAVE), whole(kept)] + [stack] * (2 * stacks),
            scratch_shapes=[pltpu.VMEM((2, 2, N, N), BF16)] * 3,
        ),
        out_shape=[jax.ShapeDtypeStruct(WAVE, F32), jax.ShapeDtypeStruct(kept, F32)]
        + [jax.ShapeDtypeStruct((4, 1, 2, N, N), BF16)] * (2 * stacks),
        compiler_params=PARAMS,
        cost_estimate=cost(len(chunks)),
        name="forward",
    )(order, scalars, *[x for blocks, _ in chunks for x in blocks], wave, prop, tabs, *extra)


def run_backward(order, scalars, chunks, ct, prop, tabs, kept):
    counts = [len(blocks) for blocks, _ in chunks]

    def body(*refs):
        backward_kernel(counts, *refs)

    sent = (16, len(chunks), 2, 16, N)
    return pl.pallas_call(
        body,
        grid_spec=pltpu.PrefetchScalarGridSpec(
            num_scalar_prefetch=2,
            grid=(4 * len(chunks),),
            in_specs=chunk_specs(chunks, True)
            + [whole(WAVE), whole(WAVE), whole((4, N, N))]
            + [pl.BlockSpec((1, *WAVE), lambda *_, at=at: (at, 0, 0, 0)) for _, at in kept],
            out_specs=[whole(WAVE), whole(sent)],
            scratch_shapes=[pltpu.VMEM(WAVE, F32)] * 2 + [pltpu.VMEM((2, 2, N, N), BF16)] * 3,
        ),
        out_shape=[jax.ShapeDtypeStruct(WAVE, F32), jax.ShapeDtypeStruct(sent, F32)],
        compiler_params=PARAMS,
        cost_estimate=cost(len(chunks)),
        name="backward",
    )(order, scalars, *[x for blocks, _ in chunks for x in blocks], ct, prop, tabs, *[x for x, _ in kept])


def run_reduce(piece, tiles, positions, got):
    sources, count = got.shape[:2]

    def body(*refs):
        reduce_kernel(sources, *refs)

    return pl.pallas_call(
        body,
        grid=(count,),
        in_specs=[SMEM] * 3 + [pl.BlockSpec((sources, 1, 2, 16, N), lambda i: (0, i, 0, 0, 0))],
        out_specs=pl.BlockSpec((4, 1, 2, 8, 2 * N), lambda i: (0, i, 0, 0, 0)),
        out_shape=jax.ShapeDtypeStruct((4, count, 2, 8, 2 * N), F32),
        compiler_params=PARAMS,
        name="reduce",
    )(piece, tiles, positions, got)


def from_neighbour(block, axis, distance):
    size = lax.axis_size(axis)
    return lax.ppermute(block, axis, [(i, (i + distance) % size) for i in range(size)])


def paired(x):
    for axis in (-2, -1):
        first, second = jnp.split(x, 2, axis=axis)
        x = jnp.concatenate([first, jnp.flip(second, axis=axis)], axis=axis)
    return x


def start_wave(probe_wave):
    at = np.arange(N)
    angle = math.pi / N * (at[:, None] + at[None, :])
    cos, sin = np.cos(angle).astype(np.float32), np.sin(angle).astype(np.float32)
    real, imag = probe_wave[0], probe_wave[1]
    return paired(jnp.stack([real * cos - imag * sin, real * sin + imag * cos]))


def around_of(at):
    return (at - jnp.arange(4, dtype=jnp.int32)) % 4


def ring_gather(block, z, core):
    size = lax.axis_size("z")
    below, above = from_neighbour(block, "z", 1), from_neighbour(block, "z", -1)
    route = [(2 * i + c, 2 * ((i + 1 - 2 * c) % size) + c) for i in range(size) for c in (0, 1)]
    far = lax.ppermute(jnp.where(core == 0, below, above), ("z", "core"), route)
    own = [block, below, far, above]
    return own + [from_neighbour(x, "core", 1) for x in own]


def on_device(probe_wave, object_field, pos_rows, pos_cols, intensity, prop_phase):
    row, tile, z, core = (lax.axis_index(name).astype(jnp.int32) for name in ("y", "x", "z", "core"))
    chunks_count = lax.axis_size("y")
    strip, width = object_field.shape[2:]
    moves = (0, 1, 3, 2)
    positions = jnp.stack([pos_rows, pos_cols])
    blocks = [object_field] + [from_neighbour(object_field, "x", d) for d in moves[1:]]
    positions = jnp.stack([positions] + [from_neighbour(positions, "x", d) for d in (1, 2, 3)])
    starts = jnp.stack([(tile - d) % 4 for d in moves]) * strip

    *tabs, gain = tables()
    tabs = jnp.asarray(np.stack(tabs))
    prop = paired(jnp.stack([jnp.cos(prop_phase), jnp.sin(prop_phase)]) * (1.0 / gain))
    inten = paired(lax.dynamic_index_in_dim(intensity, row, 0, keepdims=False))
    wave = start_wave(probe_wave)
    scalars = jnp.stack([z, core, pos_rows[row], pos_cols[row]])
    blocks, positions, prop, inten, wave, scalars = lax.optimization_barrier(
        (blocks, positions, prop, inten, wave, scalars)
    )

    patches = cut(blocks, starts, pos_rows, pos_cols)
    patches = lax.all_to_all(patches, "y", 0, 0, tiled=True)
    middle = lax.all_gather(patches[1:3], "z", axis=0)
    final = lax.all_gather(patches[3:], "z", axis=0)
    order = around_of(z)

    def forward(chunks, wave, **more):
        return run_forward(order, scalars, chunks, wave, prop, tabs, gain, **more)

    wave, kept0, *stacked = forward([(ring_gather(patches[0], z, core), 0)], wave, stacks=True)
    middle, wave = lax.optimization_barrier((middle, wave))
    middle = [middle, from_neighbour(middle, "core", 1)]
    wave, kept12 = forward([(middle, 0), (middle, 1)], wave)
    final, wave = lax.optimization_barrier((final, wave))
    final = [final, from_neighbour(final, "core", 1)]
    wave, kept3 = forward([(final, 0)], wave, inten=inten)

    def backward(chunks, wave, kept):
        return run_backward(order, scalars, chunks, wave, prop, tabs, kept)

    wave, sent23 = backward([(middle, 1), (final, 0)], wave, [(kept12, 1), (kept3, 0)])
    got23 = lax.all_to_all(sent23, ("x", "y"), 0, 0, tiled=True)
    wave, sent01 = backward([(stacked, 0), (middle, 0)], wave, [(kept0, 0), (kept12, 0)])
    got23, sent01 = lax.optimization_barrier((got23, sent01))
    got01 = lax.all_to_all(sent01, ("x", "y"), 0, 0, tiled=True)
    got = [got01, got23]
    piece = (tile * 4 + row)[None]
    sums = [run_reduce(piece, around_of(tile), positions, x) for x in got]
    sums = jnp.concatenate(sums, axis=1).reshape(16, 2, 8, width)
    out = lax.all_to_all(sums, ("x", "y"), 0, 0, tiled=True)
    return jnp.transpose(out, (1, 0, 2, 3)).reshape(2, 1, strip, width)


def solution(mesh):
    devices = mesh.devices
    fine = Mesh(devices.reshape(4, 4, 2, devices.shape[1]), ("y", "z", "core", "x"))
    cuts = ("y", "z", "core")
    return jax.shard_map(
        on_device,
        mesh=fine,
        in_specs=(
            P(),
            P(None, cuts, "x", None),
            P("x"),
            P("x"),
            P("x", None, None),
            P(),
        ),
        out_specs=P(None, cuts, "x", None),
        check_vma=False,
    )
```

time: 283 us -> 244 us (0.86)
  blocking collectives: 63.6 us -> 30.5 us
  waiting for transfers between devices: 74.6 us -> 47 us
  starting transfers between devices: 12.1 us -> 26.1 us
  local copies, waits for them, and re-layouts: 17.4 us -> 21.9 us
    all_gather x4 -> x2, waiting for transfers between devices: 61.1 us -> 0.01 us  [the longest x1 0.01 us: on_device(): middle = lax.all_gather(patches[1:3], 'z', axis=0)]
    all_gather x1 -> x0, blocking collectives: 30.1 us -> none  [on_device(): lax.all_gather(jnp.stack([pos_rows, pos_cols]), 'x', axis=1, tiled=True)]
    all_to_all x1 -> x2, waiting for transfers between devices: 0.73 us -> 15.9 us  [the longest x1 15.9 us: on_device(): got01 = lax.all_to_all(sent01, ('x', 'y'), 0, 0, tiled=True)]
    ppermute x0 -> x1, waiting for transfers between devices: none -> 12.5 us  [ring_gather(): far = lax.ppermute(jnp.where(core == 0, below, above), ('z', 'core'), route)]
    ppermute x3 -> x14, starting transfers between devices: 5.13 us -> 14.7 us  [from_neighbour(): lax.ppermute(block, axis, [(i, (i + distance) % size) for i in range(size)])]
    ppermute x3 -> x14, waiting for transfers between devices: 10.9 us -> 18.6 us  [from_neighbour(): lax.ppermute(block, axis, [(i, (i + distance) % size) for i in range(size)])]
    all_to_all x1 -> x2, starting transfers between devices: 6.81 us -> 11.4 us  [the longest x1 7.22 us: on_device(): got01 = lax.all_to_all(sent01, ('x', 'y'), 0, 0, tiled=True)]
    unnamed x39 -> x42, local copies, waits for them, and re-layouts: 11.1 us -> 13.8 us
  transfers between devices with their start and end apart: 8 -> 19, of which waited for: 8 -> 8; matrix products, arithmetic and copies ran while one was open for 2% -> 4% of each run, Pallas kernels for 11% -> 24%
where the time goes in v3:
time: 244 us; the launch traced here: 243 us
  Pallas kernels  100 us (41%)
  waiting for transfers between devices  47 us (19%)
  blocking collectives  30.5 us (12%)
  starting transfers between devices  26.1 us (11%)
  local copies, waits for them, and re-layouts  21.9 us (9%)
  between operations  13.8 us (6%)
  other arithmetic  3.68 us (2%)
    pallas_call x2, Pallas kernels, run_backward(): pl.pallas_call(body, grid_spec=pltpu.PrefetchScalarGridSpec(num_scalar_pr...  48.6 us
    pallas_call x3, Pallas kernels, run_forward(): pl.pallas_call(body, grid_spec=pltpu.PrefetchScalarGridSpec(num_scalar_pr...  45.5 us
    ppermute x14, waiting for transfers between devices, from_neighbour(): lax.ppermute(block, axis, [(i, (i + distance) % size) for i in range(size)])  18.6 us
    all_to_all x1, blocking collectives, on_device(): patches = lax.all_to_all(patches, 'y', 0, 0, tiled=True)  17.4 us
    all_to_all x1, waiting for transfers between devices, on_device(): got01 = lax.all_to_all(sent01, ('x', 'y'), 0, 0, tiled=True)  15.9 us
    ppermute x14, starting transfers between devices, from_neighbour(): lax.ppermute(block, axis, [(i, (i + distance) % size) for i in range(size)])  14.7 us
    unnamed x42, local copies, waits for them, and re-layouts  13.8 us
    all_to_all x1, blocking collectives, on_device(): out = lax.all_to_all(sums, ('x', 'y'), 0, 0, tiled=True)  13.1 us
  transfers between devices with their start and end apart: 19, of which 8 were waited for; matrix products, arithmetic and copies ran while one was open for 4% of the time, Pallas kernels for 24%

profile of v3, /device:TPU:0, one launch (start us, length us, event | category | flops | bytes accessed | tf_op | source)
XLA Modules:
  0.0 243.5 jit_solution(7141909579627290632)
XLA Ops:
  7.2 3.1 %collective-permute-start.4 = (s32[2,4]{1,0:T(2,128)S(1)}, s32[2,4]{1,0:T(2,128)S(1)}, u32[]{:S(2)}, u32[]{:S(2)}) collective-permute-start(s32[2,4]{1,0:T(2,128)S(1)} %get-tuple-element.76), channel_id=1, source_target_pairs={{0,2},{1,3},{2,0},{3,1},{4,6},{5,7},{6,4},{7,5},{8,10},{9,11},{10,... | collective-permute-start | bytes 104 | tf_op jit(solution)/shard_map/ppermute | solution.py:441
  10.9 2.6 %collective-permute-start.1 = (bf16[2,1,128,512]{3,2,1,0:T(8,128)(2,1)}, bf16[2,1,128,512]{3,2,1,0:T(8,128)(2,1)S(1)}, u32[]{:S(2)}, u32[]{:S(2)}) collective-permute-start(bf16[2,1,128,512]{3,2,1,0:T(8,128)(2,1)} %refs_0_), channel_id=1, source_target_pairs={{0,3},{1,0},{2,1},{3,2},{4,7},{5,4},{6,5},{7,6},{8,11},{9,8},{10,9... | collective-permute-start | bytes 786440 | tf_op jit(solution)/shard_map/ppermute | solution.py:441
  13.6 1.5 collective-permute-start.2
  15.0 1.2 dynamic_slice.12
  16.3 1.2 dynamic_slice.11
  18.8 1.3 multiply_subtract_fusion
  21.8 1.3 pad_add_fusion.2.refs_1_
  23.9 1.8 collective-permute-start.5
  25.7 2.4 collective-permute-done.5
  28.2 3.6 %cut.1 = bf16[4,2,256,256]{3,2,1,0:T(8,128)(2,1)S(1)} custom-call(s32[4]{0:T(128)S(1)} %copy-done.2, s32[4]{0:T(128)S(1)} %copy-done.1, s32[4]{0:T(128)S(1)} %add_multiply_fusion.starts_ref, bf16[2,1,128,512]{3,2,1,0:T(8,128)(2,1)S(1)} %copy-done, bf16[2,1,128,512]{3,2,1,0:T(8,128)(2,1)S(1)} %collective-permute-done.refs_1_, ...), custom_call_target="tpu_custom_call" | custom-call | tf_op jit(solution)/shard_map/cut/pallas_call | solution.py:341
  31.8 17.4 %all_to_all.20 = bf16[4,2,256,256]{3,2,1,0:T(8,128)(2,1)S(1)} all-to-all(bf16[4,2,256,256]{3,2,1,0:T(8,128)(2,1)S(1)} %cut.1), channel_id=1, replica_groups=mesh['y'=4,'z'=4,'core'=2,'x'=4] {'y'}, dimensions={0} | all-to-all | bytes 2097152 | tf_op jit(solution)/shard_map/all_to_all | solution.py:493
  50.9 4.0 %collective-permute-start.7 = (bf16[2,256,256]{2,1,0:T(8,128)(2,1)S(1)}, bf16[2,256,256]{2,1,0:T(8,128)(2,1)S(1)}, u32[]{:S(2)}, u32[]{:S(2)}) collective-permute-start(bf16[2,256,256]{2,1,0:T(8,128)(2,1)S(1)} %get-tuple-element.58.refs_2_), channel_id=1, source_target_pairs={{0,24},{8,0},{16,8},{24,16},{1,25},{9,1},{17,9},{25,17},{2,26},{10... | collective-permute-start | bytes 786440 | tf_op jit(solution)/shard_map/ppermute | solution.py:441
  54.9 4.5 %collective-permute-done.7.refs_5_ = bf16[2,256,256]{2,1,0:T(8,128)(2,1)S(1)} collective-permute-done((bf16[2,256,256]{2,1,0:T(8,128)(2,1)S(1)}, bf16[2,256,256]{2,1,0:T(8,128)(2,1)S(1)}, u32[]{:S(2)}, u32[]{:S(2)}) %collective-permute-start.7) | collective-permute-done | bytes 262176 | tf_op jit(solution)/shard_map/ppermute | solution.py:441
  59.4 3.1 %collective-permute-done.6.refs_3_ = bf16[2,256,256]{2,1,0:T(8,128)(2,1)S(1)} collective-permute-done((bf16[2,256,256]{2,1,0:T(8,128)(2,1)S(1)}, bf16[2,256,256]{2,1,0:T(8,128)(2,1)S(1)}, u32[]{:S(2)}, u32[]{:S(2)}) %collective-permute-start.6) | collective-permute-done | bytes 262176 | tf_op jit(solution)/shard_map/ppermute | solution.py:441
  63.3 12.5 %collective-permute-done.8.refs_4_ = bf16[2,256,256]{2,1,0:T(8,128)(2,1)S(1)} collective-permute-done((bf16[2,256,256]{2,1,0:T(8,128)(2,1)S(1)}, bf16[2,256,256]{2,1,0:T(8,128)(2,1)S(1)}, u32[]{:S(2)}, u32[]{:S(2)}) %collective-permute-start.8) | collective-permute-done | bytes 262176 | tf_op jit(solution)/shard_map/ppermute | solution.py:467
  75.8 1.5 collective-permute-done.11.refs_8_
  77.3 11.0 %forward.3 = (f32[2,256,256]{2,1,0:T(8,128)S(1)}, f32[1,2,256,256]{3,2,1,0:T(8,128)S(1)}, bf16[4,1,2,256,256]{4,3,2,1,0:T(8,128)(2,1)S(1)}, bf16[4,1,2,256,256]{4,3,2,1,0:T(8,128)(2,1)S(1)}) custom-call(s32[4]{0:T(128)S(1)} %and_select_fusion.refs_0_, s32[4]{0:T(128)S(1)} %pad_add_fusion.2.refs_1_, bf16[2,256,256]{2,1,0:T(8,128)(2,1)S(1)} %get-tuple-element.58.refs_2_, ...), custom_call_target="tpu_custom_call" | custom-call | flops 4294967296 | bytes 4194304 | tf_op jit(solution)/shard_map/forward/pallas_call | solution.py:378
  91.3 4.3 %collective-permute-done.13.refs_3_.refs_5_ = bf16[4,2,2,256,256]{4,3,2,1,0:T(8,128)(2,1)} collective-permute-done((bf16[4,2,2,256,256]{4,3,2,1,0:T(8,128)(2,1)}, bf16[4,2,2,256,256]{4,3,2,1,0:T(8,128)(2,1)}, u32[]{:S(2)}, u32[]{:S(2)}) %collective-permute-start.13) | collective-permute-done | bytes 2097184 | tf_op jit(solution)/shard_map/ppermute | solution.py:441
  95.6 1.7 copy-done.3
  97.3 22.2 %forward.4 = (f32[2,256,256]{2,1,0:T(8,128)S(1)}, f32[2,2,256,256]{3,2,1,0:T(8,128)S(1)}) custom-call(s32[4]{0:T(128)S(1)} %and_select_fusion.refs_0_, s32[4]{0:T(128)S(1)} %pad_add_fusion.2.refs_1_, bf16[4,2,2,256,256]{4,3,2,1,0:T(8,128)(2,1)S(1)} %bitcast.35, bf16[4,2,2,256,256]{4,3,2,1,0:T(8,128)(2,1)} %collective-permute-done.13.refs_3_.refs_5_, ...), custom_call_target="tpu_custom_call" | custom-call | flops 8589934592 | bytes 8388608 | tf_op jit(solution)/shard_map/forward/pallas_call | solution.py:378
  120.6 2.7 %collective-permute-done.14.refs_3_.refs_5_ = bf16[4,1,2,256,256]{4,3,2,1,0:T(8,128)(2,1)S(1)} collective-permute-done((bf16[4,1,2,256,256]{4,3,2,1,0:T(8,128)(2,1)}, bf16[4,1,2,256,256]{4,3,2,1,0:T(8,128)(2,1)S(1)}, u32[]{:S(2)}, u32[]{:S(2)}) %collective-permute-start.14) | collective-permute-done | bytes 1048608 | tf_op jit(solution)/shard_map/ppermute | solution.py:441
  123.3 1.2 copy-done.6
  124.6 12.4 %forward.5 = (f32[2,256,256]{2,1,0:T(8,128)S(1)}, f32[1,2,256,256]{3,2,1,0:T(8,128)S(1)}) custom-call(s32[4]{0:T(128)S(1)} %and_select_fusion.refs_0_, s32[4]{0:T(128)S(1)} %pad_add_fusion.2.refs_1_, bf16[4,1,2,256,256]{4,3,2,1,0:T(8,128)(2,1)S(1)} %bitcast.40, bf16[4,1,2,256,256]{4,3,2,1,0:T(8,128)(2,1)S(1)} %collective-permute-done.14.refs_3_.refs_5_, ...), custom_call_target="tpu_custom_call" | custom-call | flops 4294967296 | bytes 4194304 | tf_op jit(solution)/shard_map/forward/pallas_call | solution.py:378
  137.0 24.2 %backward.2 = (f32[2,256,256]{2,1,0:T(8,128)S(1)}, f32[16,2,2,16,256]{4,3,2,1,0:T(8,128)}) custom-call(s32[4]{0:T(128)S(1)} %and_select_fusion.refs_0_, s32[4]{0:T(128)S(1)} %pad_add_fusion.2.refs_1_, bf16[4,2,2,256,256]{4,3,2,1,0:T(8,128)(2,1)S(1)} %bitcast.37, bf16[4,2,2,256,256]{4,3,2,1,0:T(8,128)(2,1)} %collective-permute-done.13.refs_3_.refs_5_, ...), custom_call_target="tpu_custom_call" | custom-call | flops 8589934592 | bytes 8388608 | tf_op jit(solution)/shard_map/backward/pallas_call | solution.py:404
  161.9 4.2 %all-to-all-start.1 = ((f32[16,2,2,16,256]{4,3,2,1,0:T(8,128)}), f32[16,2,2,16,256]{4,3,2,1,0:T(8,128)S(1)}, u32[]{:S(2)}, u32[]{:S(2)}) async-start(f32[16,2,2,16,256]{4,3,2,1,0:T(8,128)} %get-tuple-element.49), calls=%async_computation.1 | async-start | bytes 2097152 | tf_op jit(solution)/shard_map/all_to_all | solution.py:513
  166.1 1.6 copy-done.5
  172.4 24.4 %backward.3 = (f32[2,256,256]{2,1,0:T(8,128)}, f32[16,2,2,16,256]{4,3,2,1,0:T(8,128)}) custom-call(s32[4]{0:T(128)S(1)} %and_select_fusion.refs_0_, s32[4]{0:T(128)S(1)} %pad_add_fusion.2.refs_1_, bf16[4,1,2,256,256]{4,3,2,1,0:T(8,128)(2,1)S(1)} %copy-done.10, bf16[4,1,2,256,256]{4,3,2,1,0:T(8,128)(2,1)S(1)} %copy-done.12, ...), custom_call_target="tpu_custom_call" | custom-call | flops 8589934592 | bytes 8388608 | tf_op jit(solution)/shard_map/backward/pallas_call | solution.py:404
  196.8 7.2 %all-to-all-start.2 = ((f32[16,2,2,16,256]{4,3,2,1,0:T(8,128)}), f32[16,2,2,16,256]{4,3,2,1,0:T(8,128)S(1)}, u32[]{:S(2)}, u32[]{:S(2)}) async-start(f32[16,2,2,16,256]{4,3,2,1,0:T(8,128)} %get-tuple-element.55), calls=%async_computation.2 | async-start | bytes 2097152 | tf_op jit(solution)/shard_map/all_to_all | solution.py:516
  204.1 1.3 reduce.3
  205.4 15.9 %all-to-all-done.2.refs_3_ = f32[16,2,2,16,256]{4,3,2,1,0:T(8,128)S(1)} async-done(((f32[16,2,2,16,256]{4,3,2,1,0:T(8,128)}), f32[16,2,2,16,256]{4,3,2,1,0:T(8,128)S(1)}, u32[]{:S(2)}, u32[]{:S(2)}) %all-to-all-start.2) | async-done | bytes 1048608 | tf_op jit(solution)/shard_map/all_to_all | solution.py:516
  221.3 1.3 reduce.2
  222.7 13.1 %all_to_all.21 = f32[16,2,8,512]{3,2,1,0:T(8,128)S(1)} all-to-all(f32[16,2,8,512]{3,2,1,0:T(8,128)S(1)} %bitcast.42), channel_id=1, replica_groups=mesh['y'=4,'z'=4,'core'=2,'x'=4] {'x','y'}, dimensions={0} | all-to-all | bytes 1048576 | tf_op jit(solution)/shard_map/all_to_all | solution.py:521
  (90 shorter events, 17.8 us)
Async XLA Ops:
  6.5 84.6 %all-gather.5.cloned.1.call-start = ((), (), s32[]{:S(2)}) async-start(), calls=%async_computation.4 | async-start | bytes 2621440 | tf_op jit(solution)/shard_map/all_gather | solution.py:494
  7.2 16.7 %collective-permute-start.4 = (s32[2,4]{1,0:T(2,128)S(1)}, s32[2,4]{1,0:T(2,128)S(1)}, u32[]{:S(2)}, u32[]{:S(2)}) collective-permute-start(s32[2,4]{1,0:T(2,128)S(1)} %get-tuple-element.76), channel_id=1, source_target_pairs={{0,2},{1,3},{2,0},{3,1},{4,6},{5,7},{6,4},{7,5},{8,10},{9,11},{10,... | collective-permute-start | bytes 104 | tf_op jit(solution)/shard_map/ppermute | solution.py:441
  10.3 15.4 %collective-permute-start.3 = (s32[2,4]{1,0:T(2,128)S(1)}, s32[2,4]{1,0:T(2,128)S(1)}, u32[]{:S(2)}, u32[]{:S(2)}) collective-permute-start(s32[2,4]{1,0:T(2,128)S(1)} %get-tuple-element.76), channel_id=1, source_target_pairs={{0,1},{1,2},{2,3},{3,0},{4,5},{5,6},{6,7},{7,4},{8,9},{9,10},{10,1... | collective-permute-start | bytes 104 | tf_op jit(solution)/shard_map/ppermute | solution.py:441
  10.9 17.2 %collective-permute-start.1 = (bf16[2,1,128,512]{3,2,1,0:T(8,128)(2,1)}, bf16[2,1,128,512]{3,2,1,0:T(8,128)(2,1)S(1)}, u32[]{:S(2)}, u32[]{:S(2)}) collective-permute-start(bf16[2,1,128,512]{3,2,1,0:T(8,128)(2,1)} %refs_0_), channel_id=1, source_target_pairs={{0,3},{1,0},{2,1},{3,2},{4,7},{5,4},{6,5},{7,6},{8,11},{9,8},{10,9... | collective-permute-start | bytes 786440 | tf_op jit(solution)/shard_map/ppermute | solution.py:441
  13.6 14.6 %collective-permute-start = (bf16[2,1,128,512]{3,2,1,0:T(8,128)(2,1)}, bf16[2,1,128,512]{3,2,1,0:T(8,128)(2,1)S(1)}, u32[]{:S(2)}, u32[]{:S(2)}) collective-permute-start(bf16[2,1,128,512]{3,2,1,0:T(8,128)(2,1)} %refs_0_), channel_id=1, source_target_pairs={{0,1},{1,2},{2,3},{3,0},{4,5},{5,6},{6,7},{7,4},{8,9},{9,10},{10,1... | collective-permute-start | bytes 786440 | tf_op jit(solution)/shard_map/ppermute | solution.py:441
  13.6 14.6 %collective-permute-start.2 = (bf16[2,1,128,512]{3,2,1,0:T(8,128)(2,1)}, bf16[2,1,128,512]{3,2,1,0:T(8,128)(2,1)S(1)}, u32[]{:S(2)}, u32[]{:S(2)}) collective-permute-start(bf16[2,1,128,512]{3,2,1,0:T(8,128)(2,1)} %refs_0_), channel_id=1, source_target_pairs={{0,2},{1,3},{2,0},{3,1},{4,6},{5,7},{6,4},{7,5},{8,10},{9,11},{10,... | collective-permute-start | bytes 786440 | tf_op jit(solution)/shard_map/ppermute | solution.py:441
  18.5 1.8 copy-start.20
  21.6 6.5 %copy-start = (bf16[2,1,128,512]{3,2,1,0:T(8,128)(2,1)S(1)}, bf16[2,1,128,512]{3,2,1,0:T(8,128)(2,1)}, u32[]{:S(2)}) copy-start(bf16[2,1,128,512]{3,2,1,0:T(8,128)(2,1)} %refs_0_) | copy-start | bytes 786436
  21.6 6.5 %copy-start.1 = (s32[4]{0:T(128)S(1)}, s32[4]{0:T(128)}, u32[]{:S(2)}) copy-start(s32[4]{0:T(128)} %cols_ref.1) | copy-start | bytes 52
  21.6 6.5 %copy-start.2 = (s32[4]{0:T(128)S(1)}, s32[4]{0:T(128)}, u32[]{:S(2)}) copy-start(s32[4]{0:T(128)} %rows_ref.1) | copy-start | bytes 52
  23.9 4.2 %collective-permute-start.5 = (s32[2,4]{1,0:T(2,128)S(1)}, s32[2,4]{1,0:T(2,128)S(1)}, u32[]{:S(2)}, u32[]{:S(2)}) collective-permute-start(s32[2,4]{1,0:T(2,128)S(1)} %get-tuple-element.76), channel_id=1, source_target_pairs={{0,3},{1,0},{2,1},{3,2},{4,7},{5,4},{6,5},{7,6},{8,11},{9,8},{10,9... | collective-permute-start | bytes 104 | tf_op jit(solution)/shard_map/ppermute | solution.py:441
  49.2 28.1 %copy-start.8 = (bf16[4,256,256]{2,1,0:T(8,128)(2,1)S(1)}, bf16[4,256,256]{2,1,0:T(8,128)(2,1)}, u32[]{:S(2)}) copy-start(bf16[4,256,256]{2,1,0:T(8,128)(2,1)} %constant.81.clone.refs_12_.refs_8_.refs_6_) | copy-start | bytes 1572868
  50.1 70.4 %all-gather.7.cloned.1.call-start = ((), (), s32[]{:S(2)}) async-start(), calls=%async_computation.5 | async-start | bytes 1310720 | tf_op jit(solution)/shard_map/all_gather | solution.py:495
  50.9 8.6 %collective-permute-start.7 = (bf16[2,256,256]{2,1,0:T(8,128)(2,1)S(1)}, bf16[2,256,256]{2,1,0:T(8,128)(2,1)S(1)}, u32[]{:S(2)}, u32[]{:S(2)}) collective-permute-start(bf16[2,256,256]{2,1,0:T(8,128)(2,1)S(1)} %get-tuple-element.58.refs_2_), channel_id=1, source_target_pairs={{0,24},{8,0},{16,8},{24,16},{1,25},{9,1},{17,9},{25,17},{2,26},{10... | collective-permute-start | bytes 786440 | tf_op jit(solution)/shard_map/ppermute | solution.py:441
  54.9 7.6 %collective-permute-start.6 = (bf16[2,256,256]{2,1,0:T(8,128)(2,1)S(1)}, bf16[2,256,256]{2,1,0:T(8,128)(2,1)S(1)}, u32[]{:S(2)}, u32[]{:S(2)}) collective-permute-start(bf16[2,256,256]{2,1,0:T(8,128)(2,1)S(1)} %get-tuple-element.58.refs_2_), channel_id=1, source_target_pairs={{0,8},{8,16},{16,24},{24,0},{1,9},{9,17},{17,25},{25,1},{2,10},{10... | collective-permute-start | bytes 786440 | tf_op jit(solution)/shard_map/ppermute | solution.py:441
  62.5 13.2 %collective-permute-start.8 = (bf16[2,256,256]{2,1,0:T(8,128)(2,1)S(1)}, bf16[2,256,256]{2,1,0:T(8,128)(2,1)S(1)}, u32[]{:S(2)}, u32[]{:S(2)}) collective-permute-start(bf16[2,256,256]{2,1,0:T(8,128)(2,1)S(1)} %broadcast_select_fusion), channel_id=1, source_target_pairs={{0,8},{4,28},{8,16},{12,4},{16,24},{20,12},{24,0},{28,20},{1,9},{5... | collective-permute-start | bytes 786440 | tf_op jit(solution)/shard_map/ppermute | solution.py:467
  62.6 13.2 %collective-permute-start.9 = (bf16[2,256,256]{2,1,0:T(8,128)(2,1)S(1)}, bf16[2,256,256]{2,1,0:T(8,128)(2,1)S(1)}, u32[]{:S(2)}, u32[]{:S(2)}) collective-permute-start(bf16[2,256,256]{2,1,0:T(8,128)(2,1)S(1)} %get-tuple-element.58.refs_2_), channel_id=1, source_target_pairs={{0,4},{4,0},{1,5},{5,1},{2,6},{6,2},{3,7},{7,3},{8,12},{12,8},{9,1... | collective-permute-start | bytes 786440 | tf_op jit(solution)/shard_map/ppermute | solution.py:441
  62.7 13.1 %collective-permute-start.12 = (bf16[2,256,256]{2,1,0:T(8,128)(2,1)S(1)}, bf16[2,256,256]{2,1,0:T(8,128)(2,1)S(1)}, u32[]{:S(2)}, u32[]{:S(2)}) collective-permute-start(bf16[2,256,256]{2,1,0:T(8,128)(2,1)S(1)} %collective-permute-done.7.refs_5_), channel_id=1, source_target_pairs={{0,4},{4,0},{1,5},{5,1},{2,6},{6,2},{3,7},{7,3},{8,12},{12,8},{9,1... | collective-permute-start | bytes 786440 | tf_op jit(solution)/shard_map/ppermute | solution.py:441
  63.2 12.6 %collective-permute-start.10 = (bf16[2,256,256]{2,1,0:T(8,128)(2,1)S(1)}, bf16[2,256,256]{2,1,0:T(8,128)(2,1)S(1)}, u32[]{:S(2)}, u32[]{:S(2)}) collective-permute-start(bf16[2,256,256]{2,1,0:T(8,128)(2,1)S(1)} %collective-permute-done.6.refs_3_), channel_id=1, source_target_pairs={{0,4},{4,0},{1,5},{5,1},{2,6},{6,2},{3,7},{7,3},{8,12},{12,8},{9,1... | collective-permute-start | bytes 786440 | tf_op jit(solution)/shard_map/ppermute | solution.py:441
  75.8 1.5 collective-permute-start.11
  91.1 4.5 %collective-permute-start.13 = (bf16[4,2,2,256,256]{4,3,2,1,0:T(8,128)(2,1)}, bf16[4,2,2,256,256]{4,3,2,1,0:T(8,128)(2,1)}, u32[]{:S(2)}, u32[]{:S(2)}) collective-permute-start(bf16[4,2,2,256,256]{4,3,2,1,0:T(8,128)(2,1)} %bitcast.34), channel_id=1, source_target_pairs={{0,4},{4,0},{1,5},{5,1},{2,6},{6,2},{3,7},{7,3},{8,12},{12,8},{9,1... | collective-permute-start | bytes 6291464 | tf_op jit(solution)/shard_map/ppermute | solution.py:441
  95.6 1.7 copy-start.3
  120.5 16.5 %copy-start.4 = (bf16[8,2,256,256]{3,2,1,0:T(8,128)(2,1)S(1)}, bf16[8,2,256,256]{3,2,1,0:T(8,128)(2,1)}, u32[]{:S(2)}) copy-start(bf16[8,2,256,256]{3,2,1,0:T(8,128)(2,1)} %all-gather.5.cloned.1.call-done) | copy-start | bytes 6291460
  120.5 2.9 %collective-permute-start.14 = (bf16[4,1,2,256,256]{4,3,2,1,0:T(8,128)(2,1)}, bf16[4,1,2,256,256]{4,3,2,1,0:T(8,128)(2,1)S(1)}, u32[]{:S(2)}, u32[]{:S(2)}) collective-permute-start(bf16[4,1,2,256,256]{4,3,2,1,0:T(8,128)(2,1)} %bitcast.39), channel_id=1, source_target_pairs={{0,4},{4,0},{1,5},{5,1},{2,6},{6,2},{3,7},{7,3},{8,12},{12,8},{9,1... | collective-permute-start | bytes 3145736 | tf_op jit(solution)/shard_map/ppermute | solution.py:441
  123.3 1.2 copy-start.6
  124.6 12.4 %copy-start.7 = (bf16[4,2,256,256]{3,2,1,0:T(8,128)(2,1)S(1)}, bf16[4,2,256,256]{3,2,1,0:T(8,128)(2,1)}, u32[]{:S(2)}) copy-start(bf16[4,2,256,256]{3,2,1,0:T(8,128)(2,1)} %all-gather.7.cloned.1.call-done) | copy-start | bytes 3145732
  124.6 12.4 %copy-start.16 = (f32[2,2,256,256]{3,2,1,0:T(8,128)S(1)}, f32[2,2,256,256]{3,2,1,0:T(8,128)}, u32[]{:S(2)}) copy-start(f32[2,2,256,256]{3,2,1,0:T(8,128)} %copy-done.15) | copy-start | bytes 3145732
  161.9 4.2 %copy-start.14 = (f32[1,2,256,256]{3,2,1,0:T(8,128)S(1)}, f32[1,2,256,256]{3,2,1,0:T(8,128)}, u32[]{:S(2)}) copy-start(f32[1,2,256,256]{3,2,1,0:T(8,128)} %copy-done.13) | copy-start | bytes 1572868
  161.9 34.9 %all-to-all-start.1 = ((f32[16,2,2,16,256]{4,3,2,1,0:T(8,128)}), f32[16,2,2,16,256]{4,3,2,1,0:T(8,128)S(1)}, u32[]{:S(2)}, u32[]{:S(2)}) async-start(f32[16,2,2,16,256]{4,3,2,1,0:T(8,128)} %get-tuple-element.49), calls=%async_computation.1 | async-start | bytes 2097152 | tf_op jit(solution)/shard_map/all_to_all | solution.py:513
  166.1 1.6 copy-start.5
  168.9 1.2 copy-start.12
  196.8 24.5 %all-to-all-start.2 = ((f32[16,2,2,16,256]{4,3,2,1,0:T(8,128)}), f32[16,2,2,16,256]{4,3,2,1,0:T(8,128)S(1)}, u32[]{:S(2)}, u32[]{:S(2)}) async-start(f32[16,2,2,16,256]{4,3,2,1,0:T(8,128)} %get-tuple-element.55), calls=%async_computation.2 | async-start | bytes 2097152 | tf_op jit(solution)/shard_map/all_to_all | solution.py:516
  (8 other events, 8.1 us)
Sparse Core Ops, SparseCore 0:
  50.2 33.3 all-gather.4
  91.4 20.1 all-gather.6

commit v4 on v3

--- a/solution.py
+++ b/solution.py
@@ -391,7 +391,7 @@
         compiler_params=PARAMS,
         cost_estimate=cost(len(chunks)),
         name="forward",
-    )(order, scalars, *[x for blocks, _ in chunks for x in blocks], wave, prop, tabs, *extra)
+    )(order, scalars, *in_hbm([x for blocks, _ in chunks for x in blocks]), wave, prop, tabs, *extra)
 
 
 def run_backward(order, scalars, chunks, ct, prop, tabs, kept):
@@ -416,7 +416,7 @@
         compiler_params=PARAMS,
         cost_estimate=cost(len(chunks)),
         name="backward",
-    )(order, scalars, *[x for blocks, _ in chunks for x in blocks], ct, prop, tabs, *[x for x, _ in kept])
+    )(order, scalars, *in_hbm([x for blocks, _ in chunks for x in blocks]), ct, prop, tabs, *[x for x, _ in kept])
 
 
 def run_reduce(piece, tiles, positions, got):
@@ -460,12 +460,12 @@
     return (at - jnp.arange(4, dtype=jnp.int32)) % 4
 
 
-def ring_gather(block, z, core):
-    size = lax.axis_size("z")
-    below, above = from_neighbour(block, "z", 1), from_neighbour(block, "z", -1)
-    route = [(2 * i + c, 2 * ((i + 1 - 2 * c) % size) + c) for i in range(size) for c in (0, 1)]
-    far = lax.ppermute(jnp.where(core == 0, below, above), ("z", "core"), route)
-    own = [block, below, far, above]
+def in_hbm(blocks):
+    return [pltpu.with_memory_space_constraint(x, pltpu.HBM) for x in blocks]
+
+
+def ring_gather(block):
+    own = [block] + [from_neighbour(block, "z", d) for d in (1, 2, 3)]
     return own + [from_neighbour(x, "core", 1) for x in own]
 
 
@@ -485,12 +485,10 @@
     inten = paired(lax.dynamic_index_in_dim(intensity, row, 0, keepdims=False))
     wave = start_wave(probe_wave)
     scalars = jnp.stack([z, core, pos_rows[row], pos_cols[row]])
-    blocks, positions, prop, inten, wave, scalars = lax.optimization_barrier(
-        (blocks, positions, prop, inten, wave, scalars)
-    )
-
     patches = cut(blocks, starts, pos_rows, pos_cols)
     patches = lax.all_to_all(patches, "y", 0, 0, tiled=True)
+    small = (positions, prop, inten, wave, scalars)
+    patches, (positions, prop, inten, wave, scalars) = lax.optimization_barrier((patches, small))
     middle = lax.all_gather(patches[1:3], "z", axis=0)
     final = lax.all_gather(patches[3:], "z", axis=0)
     order = around_of(z)
@@ -498,7 +496,7 @@
     def forward(chunks, wave, **more):
         return run_forward(order, scalars, chunks, wave, prop, tabs, gain, **more)
 
-    wave, kept0, *stacked = forward([(ring_gather(patches[0], z, core), 0)], wave, stacks=True)
+    wave, kept0, *stacked = forward([(ring_gather(patches[0]), 0)], wave, stacks=True)
     middle, wave = lax.optimization_barrier((middle, wave))
     middle = [middle, from_neighbour(middle, "core", 1)]
     wave, kept12 = forward([(middle, 0), (middle, 1)], wave)

time: 244 us -> 233 us (0.955)
  blocking collectives: 30.5 us -> 13.1 us
  local copies, waits for them, and re-layouts: 21.9 us -> 14.1 us
  starting transfers between devices: 26.1 us -> 33.8 us
  other arithmetic: 3.68 us -> 8.51 us
  Pallas kernels: 100 us -> 104 us
    all_to_all x1 -> x0, blocking collectives: 17.4 us -> none  [on_device(): patches = lax.all_to_all(patches, 'y', 0, 0, tiled=True)]
    ppermute x1 -> x0, waiting for transfers between devices: 12.5 us -> none  [ring_gather(): far = lax.ppermute(jnp.where(core == 0, below, above), ('z', 'core'), route)]
    unnamed x42 -> x40, local copies, waits for them, and re-layouts: 13.8 us -> 6.02 us
    all_to_all x0 -> x1, waiting for transfers between devices: none -> 6.37 us  [on_device(): patches = lax.all_to_all(patches, 'y', 0, 0, tiled=True)]
    all_to_all x0 -> x1, starting transfers between devices: none -> 4.46 us  [on_device(): patches = lax.all_to_all(patches, 'y', 0, 0, tiled=True)]
    concatenate x5, other arithmetic: 0.19 us -> 4.27 us  [paired(): x = jnp.concatenate([first, jnp.flip(second, axis=axis)], axis=axis)]
    ppermute x14 -> x15, waiting for transfers between devices: 18.6 us -> 22.3 us  [from_neighbour(): lax.ppermute(block, axis, [(i, (i + distance) % size) for i in range(size)])]
    ppermute x14 -> x15, starting transfers between devices: 14.7 us -> 17.4 us  [from_neighbour(): lax.ppermute(block, axis, [(i, (i + distance) % size) for i in range(size)])]
  transfers between devices with their start and end apart: 19 -> 20, of which waited for: 8 -> 8; matrix products, arithmetic and copies ran while one was open for 4% -> 6% of each run, Pallas kernels for 24% -> 28%
where the time goes in v4:
time: 233 us; the launch traced here: 232 us
  Pallas kernels  104 us (45%)
  waiting for transfers between devices  44.6 us (19%)
  starting transfers between devices  33.8 us (15%)
  local copies, waits for them, and re-layouts  14.1 us (6%)
  between operations  13.8 us (6%)
  blocking collectives  13.1 us (6%)
  other arithmetic  8.51 us (4%)
    pallas_call x2, Pallas kernels, run_backward(): pl.pallas_call(body, grid_spec=pltpu.PrefetchScalarGridSpec(num_scalar_pr...  49 us
    pallas_call x3, Pallas kernels, run_forward(): pl.pallas_call(body, grid_spec=pltpu.PrefetchScalarGridSpec(num_scalar_pr...  48.3 us
    ppermute x15, waiting for transfers between devices, from_neighbour(): lax.ppermute(block, axis, [(i, (i + distance) % size) for i in range(size)])  22.3 us
    ppermute x15, starting transfers between devices, from_neighbour(): lax.ppermute(block, axis, [(i, (i + distance) % size) for i in range(size)])  17.4 us
    all_to_all x1, waiting for transfers between devices, on_device(): got01 = lax.all_to_all(sent01, ('x', 'y'), 0, 0, tiled=True)  15.9 us
    all_to_all x1, blocking collectives, on_device(): out = lax.all_to_all(sums, ('x', 'y'), 0, 0, tiled=True)  13.1 us
    all_to_all x1, starting transfers between devices, on_device(): got01 = lax.all_to_all(sent01, ('x', 'y'), 0, 0, tiled=True)  7.22 us
    all_to_all x1, waiting for transfers between devices, on_device(): patches = lax.all_to_all(patches, 'y', 0, 0, tiled=True)  6.37 us
  transfers between devices with their start and end apart: 20, of which 8 were waited for; matrix products, arithmetic and copies ran while one was open for 6% of the time, Pallas kernels for 28%

profile of v4, /device:TPU:0, one launch (start us, length us, event | category | flops | bytes accessed | tf_op | source)
XLA Modules:
  0.0 232.2 jit_solution(7497106702398542016)
XLA Ops:
  7.3 3.1 %collective-permute-start.4 = (s32[2,4]{1,0:T(2,128)S(1)}, s32[2,4]{1,0:T(2,128)S(1)}, u32[]{:S(2)}, u32[]{:S(2)}) collective-permute-start(s32[2,4]{1,0:T(2,128)S(1)} %get-tuple-element.70), channel_id=1, source_target_pairs={{0,2},{1,3},{2,0},{3,1},{4,6},{5,7},{6,4},{7,5},{8,10},{9,11},{10,... | collective-permute-start | bytes 104 | tf_op jit(solution)/shard_map/ppermute | solution.py:441
  11.0 2.6 %collective-permute-start.1 = (bf16[2,1,128,512]{3,2,1,0:T(8,128)(2,1)}, bf16[2,1,128,512]{3,2,1,0:T(8,128)(2,1)S(1)}, u32[]{:S(2)}, u32[]{:S(2)}) collective-permute-start(bf16[2,1,128,512]{3,2,1,0:T(8,128)(2,1)} %refs_0_.1), channel_id=1, source_target_pairs={{0,3},{1,0},{2,1},{3,2},{4,7},{5,4},{6,5},{7,6},{8,11},{9,8},{10,9... | collective-permute-start | bytes 786440 | tf_op jit(solution)/shard_map/ppermute | solution.py:441
  13.6 1.5 collective-permute-start.2
  16.1 1.3 multiply_subtract_fusion
  21.5 1.6 rev.27
  23.2 1.4 collective-permute-done.1.refs_2_
  24.6 3.6 %collective-permute-start.5 = (s32[2,4]{1,0:T(2,128)S(1)}, s32[2,4]{1,0:T(2,128)}, u32[]{:S(2)}, u32[]{:S(2)}) collective-permute-start(s32[2,4]{1,0:T(2,128)S(1)} %get-tuple-element.70), channel_id=1, source_target_pairs={{0,3},{1,0},{2,1},{3,2},{4,7},{5,4},{6,5},{7,6},{8,11},{9,8},{10,9... | collective-permute-start | bytes 104 | tf_op jit(solution)/shard_map/ppermute | solution.py:441
  28.2 4.4 %cut.1 = bf16[4,2,256,256]{3,2,1,0:T(8,128)(2,1)} custom-call(s32[4]{0:T(128)S(1)} %copy-done.2, s32[4]{0:T(128)S(1)} %copy-done.1, s32[4]{0:T(128)S(1)} %add_multiply_fusion.starts_ref, bf16[2,1,128,512]{3,2,1,0:T(8,128)(2,1)S(1)} %copy-done, bf16[2,1,128,512]{3,2,1,0:T(8,128)(2,1)S(1)} %collective-permute-done.refs_1_, ...), custom_call_target="tpu_custom_call" | custom-call | tf_op jit(solution)/shard_map/cut/pallas_call | solution.py:341
  32.5 4.5 %all-to-all-start = ((bf16[4,2,256,256]{3,2,1,0:T(8,128)(2,1)}), bf16[4,2,256,256]{3,2,1,0:T(8,128)(2,1)S(1)}, u32[]{:S(2)}, u32[]{:S(2)}) async-start(bf16[4,2,256,256]{3,2,1,0:T(8,128)(2,1)} %cut.1), calls=%async_computation | async-start | bytes 2097152 | tf_op jit(solution)/shard_map/all_to_all | solution.py:489
  38.3 1.4 pad_add_fusion.2.refs_1_
  40.6 1.2 pad_maximum_fusion
  42.5 6.4 %all-to-all-done = bf16[4,2,256,256]{3,2,1,0:T(8,128)(2,1)S(1)} async-done(((bf16[4,2,256,256]{3,2,1,0:T(8,128)(2,1)}), bf16[4,2,256,256]{3,2,1,0:T(8,128)(2,1)S(1)}, u32[]{:S(2)}, u32[]{:S(2)}) %all-to-all-start) | async-done | bytes 1048608 | tf_op jit(solution)/shard_map/all_to_all | solution.py:489
  50.5 4.0 %collective-permute-start.8 = (bf16[2,256,256]{2,1,0:T(8,128)(2,1)S(1)}, bf16[2,256,256]{2,1,0:T(8,128)(2,1)S(1)}, u32[]{:S(2)}, u32[]{:S(2)}) collective-permute-start(bf16[2,256,256]{2,1,0:T(8,128)(2,1)S(1)} %get-tuple-element.52.refs_2_), channel_id=1, source_target_pairs={{0,24},{8,0},{16,8},{24,16},{1,25},{9,1},{17,9},{25,17},{2,26},{10... | collective-permute-start | bytes 786440 | tf_op jit(solution)/shard_map/ppermute | solution.py:441
  54.5 1.3 collective-permute-start.6
  55.8 8.3 %collective-permute-done.8.refs_5_ = bf16[2,256,256]{2,1,0:T(8,128)(2,1)S(1)} collective-permute-done((bf16[2,256,256]{2,1,0:T(8,128)(2,1)S(1)}, bf16[2,256,256]{2,1,0:T(8,128)(2,1)S(1)}, u32[]{:S(2)}, u32[]{:S(2)}) %collective-permute-start.8) | collective-permute-done | bytes 262176 | tf_op jit(solution)/shard_map/ppermute | solution.py:441
  64.6 4.0 %collective-permute-done.6.refs_3_ = bf16[2,256,256]{2,1,0:T(8,128)(2,1)S(1)} collective-permute-done((bf16[2,256,256]{2,1,0:T(8,128)(2,1)S(1)}, bf16[2,256,256]{2,1,0:T(8,128)(2,1)S(1)}, u32[]{:S(2)}, u32[]{:S(2)}) %collective-permute-start.6) | collective-permute-done | bytes 262176 | tf_op jit(solution)/shard_map/ppermute | solution.py:441
  68.7 1.5 collective-permute-done.10.refs_7_
  70.9 12.6 %forward.3 = (f32[2,256,256]{2,1,0:T(8,128)S(1)}, f32[1,2,256,256]{3,2,1,0:T(8,128)S(1)}, bf16[4,1,2,256,256]{4,3,2,1,0:T(8,128)(2,1)S(1)}, bf16[4,1,2,256,256]{4,3,2,1,0:T(8,128)(2,1)S(1)}) custom-call(s32[4]{0:T(128)S(1)} %and_select_fusion.refs_0_, s32[4]{0:T(128)S(1)} %pad_add_fusion.2.refs_1_, bf16[2,256,256]{2,1,0:T(8,128)(2,1)} %copy-done.11, ...), custom_call_target="tpu_custom_call" | custom-call | flops 4294967296 | bytes 4194304 | tf_op jit(solution)/shard_map/forward/pallas_call | solution.py:378
  85.7 4.4 %collective-permute-done.13.refs_3_.refs_5_ = bf16[4,2,2,256,256]{4,3,2,1,0:T(8,128)(2,1)} collective-permute-done((bf16[4,2,2,256,256]{4,3,2,1,0:T(8,128)(2,1)}, bf16[4,2,2,256,256]{4,3,2,1,0:T(8,128)(2,1)}, u32[]{:S(2)}, u32[]{:S(2)}) %collective-permute-start.13) | collective-permute-done | bytes 2097184 | tf_op jit(solution)/shard_map/ppermute | solution.py:441
  90.0 22.3 %forward.4 = (f32[2,256,256]{2,1,0:T(8,128)S(1)}, f32[2,2,256,256]{3,2,1,0:T(8,128)S(1)}) custom-call(s32[4]{0:T(128)S(1)} %and_select_fusion.refs_0_, s32[4]{0:T(128)S(1)} %pad_add_fusion.2.refs_1_, bf16[4,2,2,256,256]{4,3,2,1,0:T(8,128)(2,1)} %bitcast.37, bf16[4,2,2,256,256]{4,3,2,1,0:T(8,128)(2,1)} %collective-permute-done.13.refs_3_.refs_5_, ...), custom_call_target="tpu_custom_call" | custom-call | flops 8589934592 | bytes 8388608 | tf_op jit(solution)/shard_map/forward/pallas_call | solution.py:378
  112.3 1.1 copy-done.6
  113.5 2.7 %collective-permute-done.14.refs_3_.refs_5_ = bf16[4,1,2,256,256]{4,3,2,1,0:T(8,128)(2,1)S(1)} collective-permute-done((bf16[4,1,2,256,256]{4,3,2,1,0:T(8,128)(2,1)}, bf16[4,1,2,256,256]{4,3,2,1,0:T(8,128)(2,1)S(1)}, u32[]{:S(2)}, u32[]{:S(2)}) %collective-permute-start.14) | collective-permute-done | bytes 1048608 | tf_op jit(solution)/shard_map/ppermute | solution.py:441
  117.2 13.4 %forward.5 = (f32[2,256,256]{2,1,0:T(8,128)S(1)}, f32[1,2,256,256]{3,2,1,0:T(8,128)S(1)}) custom-call(s32[4]{0:T(128)S(1)} %and_select_fusion.refs_0_, s32[4]{0:T(128)S(1)} %pad_add_fusion.2.refs_1_, bf16[4,1,2,256,256]{4,3,2,1,0:T(8,128)(2,1)} %bitcast.42, bf16[4,1,2,256,256]{4,3,2,1,0:T(8,128)(2,1)} %copy-done.12, ...), custom_call_target="tpu_custom_call" | custom-call | flops 4294967296 | bytes 4194304 | tf_op jit(solution)/shard_map/forward/pallas_call | solution.py:378
  130.7 24.3 %backward.2 = (f32[2,256,256]{2,1,0:T(8,128)S(1)}, f32[16,2,2,16,256]{4,3,2,1,0:T(8,128)}) custom-call(s32[4]{0:T(128)S(1)} %and_select_fusion.refs_0_, s32[4]{0:T(128)S(1)} %pad_add_fusion.2.refs_1_, bf16[4,2,2,256,256]{4,3,2,1,0:T(8,128)(2,1)} %bitcast.39, bf16[4,2,2,256,256]{4,3,2,1,0:T(8,128)(2,1)} %collective-permute-done.13.refs_3_.refs_5_, ...), custom_call_target="tpu_custom_call" | custom-call | flops 8589934592 | bytes 8388608 | tf_op jit(solution)/shard_map/backward/pallas_call | solution.py:404
  155.0 4.7 %all-to-all-start.1 = ((f32[16,2,2,16,256]{4,3,2,1,0:T(8,128)}), f32[16,2,2,16,256]{4,3,2,1,0:T(8,128)S(1)}, u32[]{:S(2)}, u32[]{:S(2)}) async-start(f32[16,2,2,16,256]{4,3,2,1,0:T(8,128)} %get-tuple-element.43), calls=%async_computation.1 | async-start | bytes 2097152 | tf_op jit(solution)/shard_map/all_to_all | solution.py:511
  159.7 1.2 copy-done.8
  160.9 24.6 %backward.3 = (f32[2,256,256]{2,1,0:T(8,128)}, f32[16,2,2,16,256]{4,3,2,1,0:T(8,128)}) custom-call(s32[4]{0:T(128)S(1)} %and_select_fusion.refs_0_, s32[4]{0:T(128)S(1)} %pad_add_fusion.2.refs_1_, bf16[4,1,2,256,256]{4,3,2,1,0:T(8,128)(2,1)} %copy-done.4, bf16[4,1,2,256,256]{4,3,2,1,0:T(8,128)(2,1)} %copy-done.5, bf16[4,2,2,256,256]{4,3,2,1,0:T(8,128)(2,1)} %bitcast.40, ...), custom_call_target="tpu_custom_call" | custom-call | flops 8589934592 | bytes 8388608 | tf_op jit(solution)/shard_map/backward/pallas_call | solution.py:404
  185.6 7.2 %all-to-all-start.2 = ((f32[16,2,2,16,256]{4,3,2,1,0:T(8,128)}), f32[16,2,2,16,256]{4,3,2,1,0:T(8,128)S(1)}, u32[]{:S(2)}, u32[]{:S(2)}) async-start(f32[16,2,2,16,256]{4,3,2,1,0:T(8,128)} %get-tuple-element.49), calls=%async_computation.2 | async-start | bytes 2097152 | tf_op jit(solution)/shard_map/all_to_all | solution.py:514
  192.8 1.3 reduce.3
  194.2 15.9 %all-to-all-done.2.refs_3_ = f32[16,2,2,16,256]{4,3,2,1,0:T(8,128)S(1)} async-done(((f32[16,2,2,16,256]{4,3,2,1,0:T(8,128)}), f32[16,2,2,16,256]{4,3,2,1,0:T(8,128)S(1)}, u32[]{:S(2)}, u32[]{:S(2)}) %all-to-all-start.2) | async-done | bytes 1048608 | tf_op jit(solution)/shard_map/all_to_all | solution.py:514
  210.1 1.3 reduce.2
  211.5 13.1 %all_to_all.20 = f32[16,2,8,512]{3,2,1,0:T(8,128)S(1)} all-to-all(f32[16,2,8,512]{3,2,1,0:T(8,128)S(1)} %bitcast.34), channel_id=1, replica_groups=mesh['y'=4,'z'=4,'core'=2,'x'=4] {'x','y'}, dimensions={0} | all-to-all | bytes 1048576 | tf_op jit(solution)/shard_map/all_to_all | solution.py:519
  (88 shorter events, 16.5 us)
Async XLA Ops:
  6.5 11.1 %copy-start.10 = (f32[256,256]{1,0:T(8,128)S(1)}, f32[256,256]{1,0:T(8,128)}, u32[]{:S(2)}) copy-start(f32[256,256]{1,0:T(8,128)} %param.14) | copy-start | bytes 786436
  7.3 34.5 %collective-permute-start.4 = (s32[2,4]{1,0:T(2,128)S(1)}, s32[2,4]{1,0:T(2,128)S(1)}, u32[]{:S(2)}, u32[]{:S(2)}) collective-permute-start(s32[2,4]{1,0:T(2,128)S(1)} %get-tuple-element.70), channel_id=1, source_target_pairs={{0,2},{1,3},{2,0},{3,1},{4,6},{5,7},{6,4},{7,5},{8,10},{9,11},{10,... | collective-permute-start | bytes 104 | tf_op jit(solution)/shard_map/ppermute | solution.py:441
  10.4 31.4 %collective-permute-start.3 = (s32[2,4]{1,0:T(2,128)S(1)}, s32[2,4]{1,0:T(2,128)}, u32[]{:S(2)}, u32[]{:S(2)}) collective-permute-start(s32[2,4]{1,0:T(2,128)S(1)} %get-tuple-element.70), channel_id=1, source_target_pairs={{0,1},{1,2},{2,3},{3,0},{4,5},{5,6},{6,7},{7,4},{8,9},{9,10},{10,1... | collective-permute-start | bytes 104 | tf_op jit(solution)/shard_map/ppermute | solution.py:441
  11.0 13.6 %collective-permute-start.1 = (bf16[2,1,128,512]{3,2,1,0:T(8,128)(2,1)}, bf16[2,1,128,512]{3,2,1,0:T(8,128)(2,1)S(1)}, u32[]{:S(2)}, u32[]{:S(2)}) collective-permute-start(bf16[2,1,128,512]{3,2,1,0:T(8,128)(2,1)} %refs_0_.1), channel_id=1, source_target_pairs={{0,3},{1,0},{2,1},{3,2},{4,7},{5,4},{6,5},{7,6},{8,11},{9,8},{10,9... | collective-permute-start | bytes 786440 | tf_op jit(solution)/shard_map/ppermute | solution.py:441
  13.6 14.5 %collective-permute-start = (bf16[2,1,128,512]{3,2,1,0:T(8,128)(2,1)}, bf16[2,1,128,512]{3,2,1,0:T(8,128)(2,1)S(1)}, u32[]{:S(2)}, u32[]{:S(2)}) collective-permute-start(bf16[2,1,128,512]{3,2,1,0:T(8,128)(2,1)} %refs_0_.1), channel_id=1, source_target_pairs={{0,1},{1,2},{2,3},{3,0},{4,5},{5,6},{6,7},{7,4},{8,9},{9,10},{10,1... | collective-permute-start | bytes 786440 | tf_op jit(solution)/shard_map/ppermute | solution.py:441
  13.6 14.5 %collective-permute-start.2 = (bf16[2,1,128,512]{3,2,1,0:T(8,128)(2,1)}, bf16[2,1,128,512]{3,2,1,0:T(8,128)(2,1)S(1)}, u32[]{:S(2)}, u32[]{:S(2)}) collective-permute-start(bf16[2,1,128,512]{3,2,1,0:T(8,128)(2,1)} %refs_0_.1), channel_id=1, source_target_pairs={{0,2},{1,3},{2,0},{3,1},{4,6},{5,7},{6,4},{7,5},{8,10},{9,11},{10,... | collective-permute-start | bytes 786440 | tf_op jit(solution)/shard_map/ppermute | solution.py:441
  17.4 2.6 %copy-start.1 = (s32[4]{0:T(128)S(1)}, s32[4]{0:T(128)}, u32[]{:S(2)}) copy-start(s32[4]{0:T(128)} %cols_ref.1) | copy-start | bytes 52
  17.4 3.2 %copy-start.2 = (s32[4]{0:T(128)S(1)}, s32[4]{0:T(128)}, u32[]{:S(2)}) copy-start(s32[4]{0:T(128)} %rows_ref.1) | copy-start | bytes 52
  17.6 10.5 %copy-start = (bf16[2,1,128,512]{3,2,1,0:T(8,128)(2,1)S(1)}, bf16[2,1,128,512]{3,2,1,0:T(8,128)(2,1)}, u32[]{:S(2)}) copy-start(bf16[2,1,128,512]{3,2,1,0:T(8,128)(2,1)} %refs_0_.1) | copy-start | bytes 786436
  24.6 17.2 %collective-permute-start.5 = (s32[2,4]{1,0:T(2,128)S(1)}, s32[2,4]{1,0:T(2,128)}, u32[]{:S(2)}, u32[]{:S(2)}) collective-permute-start(s32[2,4]{1,0:T(2,128)S(1)} %get-tuple-element.70), channel_id=1, source_target_pairs={{0,3},{1,0},{2,1},{3,2},{4,7},{5,4},{6,5},{7,6},{8,11},{9,8},{10,9... | collective-permute-start | bytes 104 | tf_op jit(solution)/shard_map/ppermute | solution.py:441
  32.5 16.3 %all-to-all-start = ((bf16[4,2,256,256]{3,2,1,0:T(8,128)(2,1)}), bf16[4,2,256,256]{3,2,1,0:T(8,128)(2,1)S(1)}, u32[]{:S(2)}, u32[]{:S(2)}) async-start(bf16[4,2,256,256]{3,2,1,0:T(8,128)(2,1)} %cut.1), calls=%async_computation | async-start | bytes 2097152 | tf_op jit(solution)/shard_map/all_to_all | solution.py:489
  37.0 3.6 %copy-start.9 = (f32[2,256,128]{2,1,0:T(8,128)S(1)}, f32[2,256,128]{2,1,0:T(8,128)}, u32[]{:S(2)}) copy-start(f32[2,256,128]{2,1,0:T(8,128)} %rev.27) | copy-start | bytes 786436
  37.0 48.5 %all-gather.5.cloned.1.call-start = ((), (), s32[]{:S(2)}) async-start(), calls=%async_computation.4 | async-start | bytes 2621440 | tf_op jit(solution)/shard_map/all_gather | solution.py:492
  40.6 30.3 %copy-start.3 = (bf16[4,256,256]{2,1,0:T(8,128)(2,1)S(1)}, bf16[4,256,256]{2,1,0:T(8,128)(2,1)}, u32[]{:S(2)}) copy-start(bf16[4,256,256]{2,1,0:T(8,128)(2,1)} %constant.81.clone.refs_12_.refs_8_.refs_6_) | copy-start | bytes 1572868
  49.7 63.7 %all-gather.7.cloned.1.call-start = ((), (), s32[]{:S(2)}) async-start(), calls=%async_computation.5 | async-start | bytes 1310720 | tf_op jit(solution)/shard_map/all_gather | solution.py:493
  50.5 19.6 %copy-start.11 = (bf16[2,256,256]{2,1,0:T(8,128)(2,1)}, bf16[2,256,256]{2,1,0:T(8,128)(2,1)S(1)}, u32[]{:S(2)}) copy-start(bf16[2,256,256]{2,1,0:T(8,128)(2,1)S(1)} %get-tuple-element.52.refs_2_) | copy-start | bytes 786436
  50.5 13.6 %collective-permute-start.8 = (bf16[2,256,256]{2,1,0:T(8,128)(2,1)S(1)}, bf16[2,256,256]{2,1,0:T(8,128)(2,1)S(1)}, u32[]{:S(2)}, u32[]{:S(2)}) collective-permute-start(bf16[2,256,256]{2,1,0:T(8,128)(2,1)S(1)} %get-tuple-element.52.refs_2_), channel_id=1, source_target_pairs={{0,24},{8,0},{16,8},{24,16},{1,25},{9,1},{17,9},{25,17},{2,26},{10... | collective-permute-start | bytes 786440 | tf_op jit(solution)/shard_map/ppermute | solution.py:441
  54.5 9.6 %collective-permute-start.7 = (bf16[2,256,256]{2,1,0:T(8,128)(2,1)S(1)}, bf16[2,256,256]{2,1,0:T(8,128)(2,1)S(1)}, u32[]{:S(2)}, u32[]{:S(2)}) collective-permute-start(bf16[2,256,256]{2,1,0:T(8,128)(2,1)S(1)} %get-tuple-element.52.refs_2_), channel_id=1, source_target_pairs={{0,16},{8,24},{16,0},{24,8},{1,17},{9,25},{17,1},{25,9},{2,18},{10... | collective-permute-start | bytes 786440 | tf_op jit(solution)/shard_map/ppermute | solution.py:441
  54.5 14.1 %collective-permute-start.6 = (bf16[2,256,256]{2,1,0:T(8,128)(2,1)S(1)}, bf16[2,256,256]{2,1,0:T(8,128)(2,1)S(1)}, u32[]{:S(2)}, u32[]{:S(2)}) collective-permute-start(bf16[2,256,256]{2,1,0:T(8,128)(2,1)S(1)} %get-tuple-element.52.refs_2_), channel_id=1, source_target_pairs={{0,8},{8,16},{16,24},{24,0},{1,9},{9,17},{17,25},{25,1},{2,10},{10... | collective-permute-start | bytes 786440 | tf_op jit(solution)/shard_map/ppermute | solution.py:441
  55.8 12.8 %collective-permute-start.9 = (bf16[2,256,256]{2,1,0:T(8,128)(2,1)S(1)}, bf16[2,256,256]{2,1,0:T(8,128)(2,1)S(1)}, u32[]{:S(2)}, u32[]{:S(2)}) collective-permute-start(bf16[2,256,256]{2,1,0:T(8,128)(2,1)S(1)} %get-tuple-element.52.refs_2_), channel_id=1, source_target_pairs={{0,4},{4,0},{1,5},{5,1},{2,6},{6,2},{3,7},{7,3},{8,12},{12,8},{9,1... | collective-permute-start | bytes 786440 | tf_op jit(solution)/shard_map/ppermute | solution.py:441
  64.1 6.0 %copy-start.13 = (bf16[2,256,256]{2,1,0:T(8,128)(2,1)}, bf16[2,256,256]{2,1,0:T(8,128)(2,1)S(1)}, u32[]{:S(2)}) copy-start(bf16[2,256,256]{2,1,0:T(8,128)(2,1)S(1)} %collective-permute-done.8.refs_5_) | copy-start | bytes 786436
  64.1 4.5 %collective-permute-start.12 = (bf16[2,256,256]{2,1,0:T(8,128)(2,1)S(1)}, bf16[2,256,256]{2,1,0:T(8,128)(2,1)S(1)}, u32[]{:S(2)}, u32[]{:S(2)}) collective-permute-start(bf16[2,256,256]{2,1,0:T(8,128)(2,1)S(1)} %collective-permute-done.8.refs_5_), channel_id=1, source_target_pairs={{0,4},{4,0},{1,5},{5,1},{2,6},{6,2},{3,7},{7,3},{8,12},{12,8},{9,1... | collective-permute-start | bytes 786440 | tf_op jit(solution)/shard_map/ppermute | solution.py:441
  64.1 6.0 %copy-start.14 = (bf16[2,256,256]{2,1,0:T(8,128)(2,1)}, bf16[2,256,256]{2,1,0:T(8,128)(2,1)S(1)}, u32[]{:S(2)}) copy-start(bf16[2,256,256]{2,1,0:T(8,128)(2,1)S(1)} %collective-permute-done.7.refs_4_) | copy-start | bytes 786436
  64.1 4.5 %collective-permute-start.11 = (bf16[2,256,256]{2,1,0:T(8,128)(2,1)S(1)}, bf16[2,256,256]{2,1,0:T(8,128)(2,1)S(1)}, u32[]{:S(2)}, u32[]{:S(2)}) collective-permute-start(bf16[2,256,256]{2,1,0:T(8,128)(2,1)S(1)} %collective-permute-done.7.refs_4_), channel_id=1, source_target_pairs={{0,4},{4,0},{1,5},{5,1},{2,6},{6,2},{3,7},{7,3},{8,12},{12,8},{9,1... | collective-permute-start | bytes 786440 | tf_op jit(solution)/shard_map/ppermute | solution.py:441
  68.6 1.6 copy-start.15
  68.6 1.5 collective-permute-start.10
  68.6 1.5 copy-start.16
  85.5 4.5 %collective-permute-start.13 = (bf16[4,2,2,256,256]{4,3,2,1,0:T(8,128)(2,1)}, bf16[4,2,2,256,256]{4,3,2,1,0:T(8,128)(2,1)}, u32[]{:S(2)}, u32[]{:S(2)}) collective-permute-start(bf16[4,2,2,256,256]{4,3,2,1,0:T(8,128)(2,1)} %bitcast.36), channel_id=1, source_target_pairs={{0,4},{4,0},{1,5},{5,1},{2,6},{6,2},{3,7},{7,3},{8,12},{12,8},{9,1... | collective-permute-start | bytes 6291464 | tf_op jit(solution)/shard_map/ppermute | solution.py:441
  113.4 17.3 %copy-start.7 = (f32[2,2,256,256]{3,2,1,0:T(8,128)S(1)}, f32[2,2,256,256]{3,2,1,0:T(8,128)}, u32[]{:S(2)}) copy-start(f32[2,2,256,256]{3,2,1,0:T(8,128)} %copy-done.6) | copy-start | bytes 3145732
  113.4 2.9 %collective-permute-start.14 = (bf16[4,1,2,256,256]{4,3,2,1,0:T(8,128)(2,1)}, bf16[4,1,2,256,256]{4,3,2,1,0:T(8,128)(2,1)S(1)}, u32[]{:S(2)}, u32[]{:S(2)}) collective-permute-start(bf16[4,1,2,256,256]{4,3,2,1,0:T(8,128)(2,1)} %bitcast.41), channel_id=1, source_target_pairs={{0,4},{4,0},{1,5},{5,1},{2,6},{6,2},{3,7},{7,3},{8,12},{12,8},{9,1... | collective-permute-start | bytes 3145736 | tf_op jit(solution)/shard_map/ppermute | solution.py:441
  155.0 30.5 %all-to-all-start.1 = ((f32[16,2,2,16,256]{4,3,2,1,0:T(8,128)}), f32[16,2,2,16,256]{4,3,2,1,0:T(8,128)S(1)}, u32[]{:S(2)}, u32[]{:S(2)}) async-start(f32[16,2,2,16,256]{4,3,2,1,0:T(8,128)} %get-tuple-element.43), calls=%async_computation.1 | async-start | bytes 2097152 | tf_op jit(solution)/shard_map/all_to_all | solution.py:511
  185.6 24.5 %all-to-all-start.2 = ((f32[16,2,2,16,256]{4,3,2,1,0:T(8,128)}), f32[16,2,2,16,256]{4,3,2,1,0:T(8,128)S(1)}, u32[]{:S(2)}, u32[]{:S(2)}) async-start(f32[16,2,2,16,256]{4,3,2,1,0:T(8,128)} %get-tuple-element.49), calls=%async_computation.2 | async-start | bytes 2097152 | tf_op jit(solution)/shard_map/all_to_all | solution.py:514
  (8 other events, 9.0 us)
Sparse Core Ops, SparseCore 0:
  49.8 32.3 all-gather.4
  85.8 22.0 all-gather.6

commit v5 on v4

--- a/solution.py
+++ b/solution.py
@@ -134,6 +134,9 @@
 
 
 def load_pair(order, core, at, held, pair_ref):
+    if len(held) == 1:
+        pair_ref[...] = held[0][0]
+        return
     if len(held) == 2:
         pair_ref[core] = held[0][0, 0]
         pair_ref[1 - core] = held[1][0, 0]
@@ -157,7 +160,7 @@
         first += count
 
 
-def forward_kernel(gain, is_last, counts, stacks, order, scalars, *rest):
+def forward_kernel(is_last, counts, stacks, order, scalars, *rest):
     held, (wave_ref, prop_ref, tabs_ref, *rest) = rest[: sum(counts)], rest[sum(counts) :]
     inten_ref, rest = (rest[0], rest[1:]) if is_last else (None, rest)
     out_ref, kept_ref, *stack_refs, pair_ref, lhs_ref, rhs_ref = rest
@@ -187,8 +190,16 @@
                 put_folded(lhs_ref, part, at, fold(*mixed[part]))
         spec = two_sided(lhs_ref, rhs_ref, tabs)
         for at in BLOCKS:
-            real, imag = spectrum_rows(spec, at)
-            put_spectrum(lhs_ref, at, *times(real, imag, quads_at(prop_ref, (0,), at), quads_at(prop_ref, (1,), at)))
+            prop = quads_at(prop_ref, (0,), at), quads_at(prop_ref, (1,), at)
+            real, imag = times(*spectrum_rows(spec, at), *prop)
+            if is_last:
+                final = (step == pl.num_programs(0) - 1) & (j == 1)
+                measured = quads_at(inten_ref, (), at)
+                scale = [2.0 * (x * x + y * y - z) for x, y, z in zip(real, imag, measured)]
+                slope = [[s * x for s, x in zip(scale, values)] for values in (real, imag)]
+                back = conj_times(*prop, *slope)
+                real, imag = ([jnp.where(final, b, a) for a, b in zip(*pair)] for pair in zip((real, imag), back))
+            put_spectrum(lhs_ref, at, real, imag)
         wave = two_sided(lhs_ref, rhs_ref, tabs)
         for at in BLOCKS:
             for part in (0, 1):
@@ -197,24 +208,6 @@
 
     lax.fori_loop(0, 2, one_slice, 0)
 
-    if is_last:
-
-        @pl.when(step == pl.num_programs(0) - 1)
-        def _():
-            for at in BLOCKS:
-                for part in (0, 1):
-                    put_folded(lhs_ref, part, at, fold(*quads_at(out_ref, (part,), at)))
-            spec = two_sided(lhs_ref, rhs_ref, tabs)
-            for at in BLOCKS:
-                real, imag = spectrum_rows(spec, at)
-                measured = quads_at(inten_ref, (), at)
-                scale = [(2.0 / gain) * (x * x + y * y - z) for x, y, z in zip(real, imag, measured)]
-                put_spectrum(lhs_ref, at, [s * x for s, x in zip(scale, real)], [s * x for s, x in zip(scale, imag)])
-            wave = two_sided(lhs_ref, rhs_ref, tabs)
-            for at in BLOCKS:
-                for part in (0, 1):
-                    put_quads(out_ref, part, at, unfold(*rows_of(wave, part, at)))
-
 
 def paired_index(shape, axis):
     at = lax.broadcasted_iota(jnp.int32, shape, axis)
@@ -229,7 +222,7 @@
     return lax.broadcasted_iota(jnp.int32, shape, axis)
 
 
-def backward_kernel(counts, order, scalars, *rest):
+def backward_kernel(from_end, counts, order, scalars, *rest):
     chunks = len(counts)
     held, (ct_ref, prop_ref, tabs_ref, *rest) = rest[: sum(counts)], rest[sum(counts) :]
     kept_refs, rest = rest[:chunks], rest[chunks:]
@@ -247,21 +240,37 @@
 
     def one_slice(turn, carry):
         j = 1 - turn
-        for at in BLOCKS:
-            for part in (0, 1):
-                put_folded(lhs_ref, part, at, fold(*quads_at(out_ref, (part,), at)))
-        spec = two_sided(lhs_ref, rhs_ref, tabs)
-        for at in BLOCKS:
-            prop = quads_at(prop_ref, (0,), at), quads_at(prop_ref, (1,), at)
-            put_spectrum(lhs_ref, at, *conj_times(*prop, *spectrum_rows(spec, at)))
-        wave = two_sided(lhs_ref, rhs_ref, tabs)
-        for at in BLOCKS:
-            mixed = [unfold(*rows_of(wave, part, at)) for part in (0, 1)]
+
+        def put_back(at, mixed):
             objr, obji = as_f32(quads_at(pair_ref, (j, 0), at)), as_f32(quads_at(pair_ref, (j, 1), at))
             back = conj_times(objr, obji, *mixed)
             for part in (0, 1):
                 put_quads(mixed_ref, part, at, mixed[part])
                 put_quads(out_ref, part, at, back[part])
+
+        def through():
+            for at in BLOCKS:
+                for part in (0, 1):
+                    put_folded(lhs_ref, part, at, fold(*quads_at(out_ref, (part,), at)))
+            spec = two_sided(lhs_ref, rhs_ref, tabs)
+            for at in BLOCKS:
+                prop = quads_at(prop_ref, (0,), at), quads_at(prop_ref, (1,), at)
+                put_spectrum(lhs_ref, at, *conj_times(*prop, *spectrum_rows(spec, at)))
+            wave = two_sided(lhs_ref, rhs_ref, tabs)
+            for at in BLOCKS:
+                put_back(at, [unfold(*rows_of(wave, part, at)) for part in (0, 1)])
+
+        if from_end:
+            at_end = (step == 0) & (turn == 0)
+            pl.when(jnp.logical_not(at_end))(through)
+
+            @pl.when(at_end)
+            def _():
+                for at in BLOCKS:
+                    put_back(at, [quads_at(out_ref, (part,), at) for part in (0, 1)])
+
+        else:
+            through()
 
         for k in range(chunks):
 
@@ -361,17 +370,17 @@
             inside = jnp.clip(i - first, 0, 3)
             return (3 - inside if reverse else inside, at, 0, 0, 0)
 
-        specs += [pl.BlockSpec((1, 1, 2, N, N), block)] * 2
+        specs += [pl.BlockSpec((1, 3 - len(blocks), 2, N, N), block)] * len(blocks)
     return specs
 
 
-def run_forward(order, scalars, chunks, wave, prop, tabs, gain, inten=None, stacks=False):
+def run_forward(order, scalars, chunks, wave, prop, tabs, inten=None, stacks=False):
     counts = [len(blocks) for blocks, _ in chunks]
     last = inten is not None
     extra = (inten,) if last else ()
 
     def body(*refs):
-        forward_kernel(gain, last, counts, stacks, *refs)
+        forward_kernel(last, counts, stacks, *refs)
 
     kept = (len(chunks), *WAVE)
     stack = pl.BlockSpec((1, 1, 2, N, N), lambda i, *_: (i, 0, 0, 0, 0))
@@ -394,11 +403,11 @@
     )(order, scalars, *in_hbm([x for blocks, _ in chunks for x in blocks]), wave, prop, tabs, *extra)
 
 
-def run_backward(order, scalars, chunks, ct, prop, tabs, kept):
+def run_backward(order, scalars, chunks, ct, prop, tabs, kept, from_end=False):
     counts = [len(blocks) for blocks, _ in chunks]
 
     def body(*refs):
-        backward_kernel(counts, *refs)
+        backward_kernel(from_end, counts, *refs)
 
     sent = (16, len(chunks), 2, 16, N)
     return pl.pallas_call(
@@ -476,7 +485,6 @@
     moves = (0, 1, 3, 2)
     positions = jnp.stack([pos_rows, pos_cols])
     blocks = [object_field] + [from_neighbour(object_field, "x", d) for d in moves[1:]]
-    positions = jnp.stack([positions] + [from_neighbour(positions, "x", d) for d in (1, 2, 3)])
     starts = jnp.stack([(tile - d) % 4 for d in moves]) * strip
 
     *tabs, gain = tables()
@@ -486,28 +494,30 @@
     wave = start_wave(probe_wave)
     scalars = jnp.stack([z, core, pos_rows[row], pos_cols[row]])
     patches = cut(blocks, starts, pos_rows, pos_cols)
+    patches, positions = lax.optimization_barrier((patches, positions))
+    positions = jnp.stack([positions] + [from_neighbour(positions, "x", d) for d in (1, 2, 3)])
     patches = lax.all_to_all(patches, "y", 0, 0, tiled=True)
     small = (positions, prop, inten, wave, scalars)
     patches, (positions, prop, inten, wave, scalars) = lax.optimization_barrier((patches, small))
     middle = lax.all_gather(patches[1:3], "z", axis=0)
-    final = lax.all_gather(patches[3:], "z", axis=0)
+    final = lax.all_gather(patches[3:], ("z", "core"), axis=0)
     order = around_of(z)
 
     def forward(chunks, wave, **more):
-        return run_forward(order, scalars, chunks, wave, prop, tabs, gain, **more)
+        return run_forward(order, scalars, chunks, wave, prop, tabs, **more)
 
     wave, kept0, *stacked = forward([(ring_gather(patches[0]), 0)], wave, stacks=True)
     middle, wave = lax.optimization_barrier((middle, wave))
     middle = [middle, from_neighbour(middle, "core", 1)]
     wave, kept12 = forward([(middle, 0), (middle, 1)], wave)
     final, wave = lax.optimization_barrier((final, wave))
-    final = [final, from_neighbour(final, "core", 1)]
+    final = [final.reshape(4, 2, *WAVE)]
     wave, kept3 = forward([(final, 0)], wave, inten=inten)
 
-    def backward(chunks, wave, kept):
-        return run_backward(order, scalars, chunks, wave, prop, tabs, kept)
-
-    wave, sent23 = backward([(middle, 1), (final, 0)], wave, [(kept12, 1), (kept3, 0)])
+    def backward(chunks, wave, kept, **more):
+        return run_backward(order, scalars, chunks, wave, prop, tabs, kept, **more)
+
+    wave, sent23 = backward([(middle, 1), (final, 0)], wave, [(kept12, 1), (kept3, 0)], from_end=True)
     got23 = lax.all_to_all(sent23, ("x", "y"), 0, 0, tiled=True)
     wave, sent01 = backward([(stacked, 0), (middle, 0)], wave, [(kept0, 0), (kept12, 0)])
     got23, sent01 = lax.optimization_barrier((got23, sent01))

time: 233 us -> 226 us (0.970)
  starting transfers between devices: 33.8 us -> 29.1 us
    all_to_all x1, waiting for transfers between devices: 6.37 us -> 1.84 us  [on_device(): patches = lax.all_to_all(patches, 'y', 0, 0, tiled=True)]
    ppermute x15 -> x14, waiting for transfers between devices: 22.3 us -> 26.5 us  [from_neighbour(): lax.ppermute(block, axis, [(i, (i + distance) % size) for i in range(size)])]
    ppermute x15 -> x14, starting transfers between devices: 17.4 us -> 13.2 us  [from_neighbour(): lax.ppermute(block, axis, [(i, (i + distance) % size) for i in range(size)])]
  transfers between devices with their start and end apart: 20 -> 19, of which waited for: 8 -> 11; matrix products, arithmetic and copies ran while one was open for 6% -> 6% of each run, Pallas kernels for 28% -> 27%
where the time goes in v5:
time: 226 us; the launch traced here: 225 us
  Pallas kernels  103 us (46%)
  waiting for transfers between devices  44.3 us (20%)
  starting transfers between devices  29.1 us (13%)
  local copies, waits for them, and re-layouts  15.1 us (7%)
  between operations  13.8 us (6%)
  blocking collectives  13.1 us (6%)
  other arithmetic  7.19 us (3%)
    pallas_call x2, Pallas kernels, run_backward(): pl.pallas_call(body, grid_spec=pltpu.PrefetchScalarGridSpec(num_scalar_pr...  48 us
    pallas_call x3, Pallas kernels, run_forward(): pl.pallas_call(body, grid_spec=pltpu.PrefetchScalarGridSpec(num_scalar_pr...  47.8 us
    ppermute x14, waiting for transfers between devices, from_neighbour(): lax.ppermute(block, axis, [(i, (i + distance) % size) for i in range(size)])  26.5 us
    all_to_all x1, waiting for transfers between devices, on_device(): got01 = lax.all_to_all(sent01, ('x', 'y'), 0, 0, tiled=True)  15.9 us
    ppermute x14, starting transfers between devices, from_neighbour(): lax.ppermute(block, axis, [(i, (i + distance) % size) for i in range(size)])  13.2 us
    all_to_all x1, blocking collectives, on_device(): out = lax.all_to_all(sums, ('x', 'y'), 0, 0, tiled=True)  13.1 us
    all_to_all x1, starting transfers between devices, on_device(): got01 = lax.all_to_all(sent01, ('x', 'y'), 0, 0, tiled=True)  7.22 us
    unnamed x40, local copies, waits for them, and re-layouts  6.95 us
  transfers between devices with their start and end apart: 19, of which 11 were waited for; matrix products, arithmetic and copies ran while one was open for 6% of the time, Pallas kernels for 27%

profile of v5, /device:TPU:0, one launch (start us, length us, event | category | flops | bytes accessed | tf_op | source)
XLA Modules:
  0.0 225.3 jit_solution(5155652328005956997)
XLA Ops:
  6.5 2.8 %collective-permute-start.1 = (bf16[2,1,128,512]{3,2,1,0:T(8,128)(2,1)}, bf16[2,1,128,512]{3,2,1,0:T(8,128)(2,1)S(1)}, u32[]{:S(2)}, u32[]{:S(2)}) collective-permute-start(bf16[2,1,128,512]{3,2,1,0:T(8,128)(2,1)} %refs_0_.1), channel_id=1, source_target_pairs={{0,3},{1,0},{2,1},{3,2},{4,7},{5,4},{6,5},{7,6},{8,11},{9,8},{10,9... | collective-permute-start | bytes 786440 | tf_op jit(solution)/shard_map/ppermute | solution.py:450
  9.4 2.3 %collective-permute-start.2 = (bf16[2,1,128,512]{3,2,1,0:T(8,128)(2,1)}, bf16[2,1,128,512]{3,2,1,0:T(8,128)(2,1)S(1)}, u32[]{:S(2)}, u32[]{:S(2)}) collective-permute-start(bf16[2,1,128,512]{3,2,1,0:T(8,128)(2,1)} %refs_0_.1), channel_id=1, source_target_pairs={{0,2},{1,3},{2,0},{3,1},{4,6},{5,7},{6,4},{7,5},{8,10},{9,11},{10,... | collective-permute-start | bytes 786440 | tf_op jit(solution)/shard_map/ppermute | solution.py:450
  12.7 1.3 multiply_subtract_fusion
  18.3 1.6 rev.27
  20.9 3.3 %collective-permute-done.refs_1_ = bf16[2,1,128,512]{3,2,1,0:T(8,128)(2,1)S(1)} collective-permute-done((bf16[2,1,128,512]{3,2,1,0:T(8,128)(2,1)}, bf16[2,1,128,512]{3,2,1,0:T(8,128)(2,1)S(1)}, u32[]{:S(2)}, u32[]{:S(2)}) %collective-permute-start) | collective-permute-done | bytes 262176 | tf_op jit(solution)/shard_map/ppermute | solution.py:450
  24.2 4.4 %cut.1 = bf16[4,2,256,256]{3,2,1,0:T(8,128)(2,1)} custom-call(s32[4]{0:T(128)S(1)} %copy-done.2, s32[4]{0:T(128)S(1)} %copy-done.1, s32[4]{0:T(128)S(1)} %add_multiply_fusion.starts_ref, bf16[2,1,128,512]{3,2,1,0:T(8,128)(2,1)S(1)} %copy-done, bf16[2,1,128,512]{3,2,1,0:T(8,128)(2,1)S(1)} %collective-permute-done.refs_1_, ...), custom_call_target="tpu_custom_call" | custom-call | tf_op jit(solution)/shard_map/cut/pallas_call | solution.py:350
  28.6 4.5 %all-to-all-start = ((bf16[4,2,256,256]{3,2,1,0:T(8,128)(2,1)}), bf16[4,2,256,256]{3,2,1,0:T(8,128)(2,1)S(1)}, u32[]{:S(2)}, u32[]{:S(2)}) async-start(bf16[4,2,256,256]{3,2,1,0:T(8,128)(2,1)} %cut.1), calls=%async_computation | async-start | bytes 2097152 | tf_op jit(solution)/shard_map/all_to_all | solution.py:499
  34.3 1.4 pad_add_fusion.2.refs_1_
  36.7 1.2 pad_maximum_fusion
  38.7 1.3 collective-permute-start.3
  39.9 1.5 collective-permute-done.5
  41.5 1.8 collective-permute-done.4
  44.2 1.8 all-to-all-done
  47.7 4.0 %collective-permute-start.8 = (bf16[2,256,256]{2,1,0:T(8,128)(2,1)S(1)}, bf16[2,256,256]{2,1,0:T(8,128)(2,1)S(1)}, u32[]{:S(2)}, u32[]{:S(2)}) collective-permute-start(bf16[2,256,256]{2,1,0:T(8,128)(2,1)S(1)} %get-tuple-element.56.refs_2_), channel_id=1, source_target_pairs={{0,24},{8,0},{16,8},{24,16},{1,25},{9,1},{17,9},{25,17},{2,26},{10... | collective-permute-start | bytes 786440 | tf_op jit(solution)/shard_map/ppermute | solution.py:450
  51.7 1.3 collective-permute-start.6
  53.1 9.8 %collective-permute-done.8.refs_5_ = bf16[2,256,256]{2,1,0:T(8,128)(2,1)S(1)} collective-permute-done((bf16[2,256,256]{2,1,0:T(8,128)(2,1)S(1)}, bf16[2,256,256]{2,1,0:T(8,128)(2,1)S(1)}, u32[]{:S(2)}, u32[]{:S(2)}) %collective-permute-start.8) | collective-permute-done | bytes 262176 | tf_op jit(solution)/shard_map/ppermute | solution.py:450
  63.4 3.1 %collective-permute-done.6.refs_3_ = bf16[2,256,256]{2,1,0:T(8,128)(2,1)S(1)} collective-permute-done((bf16[2,256,256]{2,1,0:T(8,128)(2,1)S(1)}, bf16[2,256,256]{2,1,0:T(8,128)(2,1)S(1)}, u32[]{:S(2)}, u32[]{:S(2)}) %collective-permute-start.6) | collective-permute-done | bytes 262176 | tf_op jit(solution)/shard_map/ppermute | solution.py:450
  68.8 12.6 %forward.3 = (f32[2,256,256]{2,1,0:T(8,128)S(1)}, f32[1,2,256,256]{3,2,1,0:T(8,128)S(1)}, bf16[4,1,2,256,256]{4,3,2,1,0:T(8,128)(2,1)S(1)}, bf16[4,1,2,256,256]{4,3,2,1,0:T(8,128)(2,1)S(1)}) custom-call(s32[4]{0:T(128)S(1)} %and_select_fusion.refs_0_, s32[4]{0:T(128)S(1)} %pad_add_fusion.2.refs_1_, bf16[2,256,256]{2,1,0:T(8,128)(2,1)} %copy-done.11, ...), custom_call_target="tpu_custom_call" | custom-call | flops 4294967296 | bytes 4194304 | tf_op jit(solution)/shard_map/forward/pallas_call | solution.py:387
  82.4 1.0 copy-done.5
  83.6 4.2 %collective-permute-done.13.refs_3_.refs_5_ = bf16[4,2,2,256,256]{4,3,2,1,0:T(8,128)(2,1)S(1)} collective-permute-done((bf16[4,2,2,256,256]{4,3,2,1,0:T(8,128)(2,1)}, bf16[4,2,2,256,256]{4,3,2,1,0:T(8,128)(2,1)S(1)}, u32[]{:S(2)}, u32[]{:S(2)}) %collective-permute-start.13) | collective-permute-done | bytes 2097184 | tf_op jit(solution)/shard_map/ppermute | solution.py:450
  87.8 1.4 copy-done.12
  89.2 22.3 %forward.4 = (f32[2,256,256]{2,1,0:T(8,128)S(1)}, f32[2,2,256,256]{3,2,1,0:T(8,128)S(1)}) custom-call(s32[4]{0:T(128)S(1)} %and_select_fusion.refs_0_, s32[4]{0:T(128)S(1)} %pad_add_fusion.2.refs_1_, bf16[4,2,2,256,256]{4,3,2,1,0:T(8,128)(2,1)} %bitcast.40, bf16[4,2,2,256,256]{4,3,2,1,0:T(8,128)(2,1)} %copy-done.12, bf16[4,2,2,256,256]{4,3,2,1,0:T(8,128)(2,1)} %bitcast.41, ...), custom_call_target="tpu_custom_call" | custom-call | flops 8589934592 | bytes 8388608 | tf_op jit(solution)/shard_map/forward/pallas_call | solution.py:387
  112.4 12.9 %forward.5 = (f32[2,256,256]{2,1,0:T(8,128)S(1)}, f32[1,2,256,256]{3,2,1,0:T(8,128)S(1)}) custom-call(s32[4]{0:T(128)S(1)} %and_select_fusion.refs_0_, s32[4]{0:T(128)S(1)} %pad_add_fusion.2.refs_1_, bf16[4,2,2,256,256]{4,3,2,1,0:T(8,128)(2,1)} %bitcast.44, f32[2,256,256]{2,1,0:T(8,128)S(1)} %get-tuple-element.42.refs_3_, ...), custom_call_target="tpu_custom_call" | custom-call | flops 4294967296 | bytes 4194304 | tf_op jit(solution)/shard_map/forward/pallas_call | solution.py:387
  125.4 23.5 %backward.2 = (f32[2,256,256]{2,1,0:T(8,128)S(1)}, f32[16,2,2,16,256]{4,3,2,1,0:T(8,128)}) custom-call(s32[4]{0:T(128)S(1)} %and_select_fusion.refs_0_, s32[4]{0:T(128)S(1)} %pad_add_fusion.2.refs_1_, bf16[4,2,2,256,256]{4,3,2,1,0:T(8,128)(2,1)} %bitcast.42, bf16[4,2,2,256,256]{4,3,2,1,0:T(8,128)(2,1)} %copy-done.12, bf16[4,2,2,256,256]{4,3,2,1,0:T(8,128)(2,1)} %bitcast.45, ...), custom_call_target="tpu_custom_call" | custom-call | flops 8589934592 | bytes 8388608 | tf_op jit(solution)/shard_map/backward/pallas_call | solution.py:413
  148.8 4.1 %all-to-all-start.1 = ((f32[16,2,2,16,256]{4,3,2,1,0:T(8,128)}), f32[16,2,2,16,256]{4,3,2,1,0:T(8,128)S(1)}, u32[]{:S(2)}, u32[]{:S(2)}) async-start(f32[16,2,2,16,256]{4,3,2,1,0:T(8,128)} %get-tuple-element.47), calls=%async_computation.1 | async-start | bytes 2097152 | tf_op jit(solution)/shard_map/all_to_all | solution.py:521
  152.9 1.2 copy-done.8
  154.1 24.6 %backward.3 = (f32[2,256,256]{2,1,0:T(8,128)}, f32[16,2,2,16,256]{4,3,2,1,0:T(8,128)}) custom-call(s32[4]{0:T(128)S(1)} %and_select_fusion.refs_0_, s32[4]{0:T(128)S(1)} %pad_add_fusion.2.refs_1_, bf16[4,1,2,256,256]{4,3,2,1,0:T(8,128)(2,1)} %copy-done.4, bf16[4,1,2,256,256]{4,3,2,1,0:T(8,128)(2,1)} %copy-done.5, bf16[4,2,2,256,256]{4,3,2,1,0:T(8,128)(2,1)} %bitcast.43, ...), custom_call_target="tpu_custom_call" | custom-call | flops 8589934592 | bytes 8388608 | tf_op jit(solution)/shard_map/backward/pallas_call | solution.py:413
  178.7 7.2 %all-to-all-start.2 = ((f32[16,2,2,16,256]{4,3,2,1,0:T(8,128)}), f32[16,2,2,16,256]{4,3,2,1,0:T(8,128)S(1)}, u32[]{:S(2)}, u32[]{:S(2)}) async-start(f32[16,2,2,16,256]{4,3,2,1,0:T(8,128)} %get-tuple-element.53), calls=%async_computation.2 | async-start | bytes 2097152 | tf_op jit(solution)/shard_map/all_to_all | solution.py:524
  185.9 1.3 reduce.3
  187.3 15.9 %all-to-all-done.2.refs_3_ = f32[16,2,2,16,256]{4,3,2,1,0:T(8,128)S(1)} async-done(((f32[16,2,2,16,256]{4,3,2,1,0:T(8,128)}), f32[16,2,2,16,256]{4,3,2,1,0:T(8,128)S(1)}, u32[]{:S(2)}, u32[]{:S(2)}) %all-to-all-start.2) | async-done | bytes 1048608 | tf_op jit(solution)/shard_map/all_to_all | solution.py:524
  203.2 1.3 reduce.2
  204.6 13.1 %all_to_all.20 = f32[16,2,8,512]{3,2,1,0:T(8,128)S(1)} all-to-all(f32[16,2,8,512]{3,2,1,0:T(8,128)S(1)} %bitcast.34), channel_id=1, replica_groups=mesh['y'=4,'z'=4,'core'=2,'x'=4] {'x','y'}, dimensions={0} | all-to-all | bytes 1048576 | tf_op jit(solution)/shard_map/all_to_all | solution.py:529
  (86 shorter events, 17.6 us)
Async XLA Ops:
  6.5 7.7 %copy-start.10 = (f32[256,256]{1,0:T(8,128)S(1)}, f32[256,256]{1,0:T(8,128)}, u32[]{:S(2)}) copy-start(f32[256,256]{1,0:T(8,128)} %param.14) | copy-start | bytes 786436
  6.5 14.3 %collective-permute-start.1 = (bf16[2,1,128,512]{3,2,1,0:T(8,128)(2,1)}, bf16[2,1,128,512]{3,2,1,0:T(8,128)(2,1)S(1)}, u32[]{:S(2)}, u32[]{:S(2)}) collective-permute-start(bf16[2,1,128,512]{3,2,1,0:T(8,128)(2,1)} %refs_0_.1), channel_id=1, source_target_pairs={{0,3},{1,0},{2,1},{3,2},{4,7},{5,4},{6,5},{7,6},{8,11},{9,8},{10,9... | collective-permute-start | bytes 786440 | tf_op jit(solution)/shard_map/ppermute | solution.py:450
  9.4 14.8 %collective-permute-start = (bf16[2,1,128,512]{3,2,1,0:T(8,128)(2,1)}, bf16[2,1,128,512]{3,2,1,0:T(8,128)(2,1)S(1)}, u32[]{:S(2)}, u32[]{:S(2)}) collective-permute-start(bf16[2,1,128,512]{3,2,1,0:T(8,128)(2,1)} %refs_0_.1), channel_id=1, source_target_pairs={{0,1},{1,2},{2,3},{3,0},{4,5},{5,6},{6,7},{7,4},{8,9},{9,10},{10,1... | collective-permute-start | bytes 786440 | tf_op jit(solution)/shard_map/ppermute | solution.py:450
  9.4 14.8 %collective-permute-start.2 = (bf16[2,1,128,512]{3,2,1,0:T(8,128)(2,1)}, bf16[2,1,128,512]{3,2,1,0:T(8,128)(2,1)S(1)}, u32[]{:S(2)}, u32[]{:S(2)}) collective-permute-start(bf16[2,1,128,512]{3,2,1,0:T(8,128)(2,1)} %refs_0_.1), channel_id=1, source_target_pairs={{0,2},{1,3},{2,0},{3,1},{4,6},{5,7},{6,4},{7,5},{8,10},{9,11},{10,... | collective-permute-start | bytes 786440 | tf_op jit(solution)/shard_map/ppermute | solution.py:450
  14.0 2.8 %copy-start.1 = (s32[4]{0:T(128)S(1)}, s32[4]{0:T(128)}, u32[]{:S(2)}) copy-start(s32[4]{0:T(128)} %cols_ref.1) | copy-start | bytes 52
  14.0 3.4 %copy-start.2 = (s32[4]{0:T(128)S(1)}, s32[4]{0:T(128)}, u32[]{:S(2)}) copy-start(s32[4]{0:T(128)} %rows_ref.1) | copy-start | bytes 52
  14.2 9.9 %copy-start = (bf16[2,1,128,512]{3,2,1,0:T(8,128)(2,1)S(1)}, bf16[2,1,128,512]{3,2,1,0:T(8,128)(2,1)}, u32[]{:S(2)}) copy-start(bf16[2,1,128,512]{3,2,1,0:T(8,128)(2,1)} %refs_0_.1) | copy-start | bytes 786436
  28.6 17.4 %all-to-all-start = ((bf16[4,2,256,256]{3,2,1,0:T(8,128)(2,1)}), bf16[4,2,256,256]{3,2,1,0:T(8,128)(2,1)S(1)}, u32[]{:S(2)}, u32[]{:S(2)}) async-start(bf16[4,2,256,256]{3,2,1,0:T(8,128)(2,1)} %cut.1), calls=%async_computation | async-start | bytes 2097152 | tf_op jit(solution)/shard_map/all_to_all | solution.py:499
  33.0 3.6 %copy-start.9 = (f32[2,256,128]{2,1,0:T(8,128)S(1)}, f32[2,256,128]{2,1,0:T(8,128)}, u32[]{:S(2)}) copy-start(f32[2,256,128]{2,1,0:T(8,128)} %rev.27) | copy-start | bytes 786436
  33.0 50.4 %all-gather.5.cloned.1.call-start = ((), (), s32[]{:S(2)}) async-start(), calls=%async_computation.4 | async-start | bytes 2621440 | tf_op jit(solution)/shard_map/all_gather | solution.py:502
  36.7 32.1 %copy-start.3 = (bf16[4,256,256]{2,1,0:T(8,128)(2,1)S(1)}, bf16[4,256,256]{2,1,0:T(8,128)(2,1)}, u32[]{:S(2)}) copy-start(bf16[4,256,256]{2,1,0:T(8,128)(2,1)} %constant.81.clone.refs_12_.refs_8_.refs_5_.refs_7_) | copy-start | bytes 1572868
  37.8 3.6 %collective-permute-start.5 = (s32[2,4]{1,0:T(2,128)S(1)}, s32[2,4]{1,0:T(2,128)S(1)}, u32[]{:S(2)}, u32[]{:S(2)}) collective-permute-start(s32[2,4]{1,0:T(2,128)S(1)} %pad_add_fusion.1), channel_id=1, source_target_pairs={{0,3},{1,0},{2,1},{3,2},{4,7},{5,4},{6,5},{7,6},{8,11},{9,8},{10,9... | collective-permute-start | bytes 104 | tf_op jit(solution)/shard_map/ppermute | solution.py:450
  38.2 5.1 %collective-permute-start.4 = (s32[2,4]{1,0:T(2,128)S(1)}, s32[2,4]{1,0:T(2,128)S(1)}, u32[]{:S(2)}, u32[]{:S(2)}) collective-permute-start(s32[2,4]{1,0:T(2,128)S(1)} %pad_add_fusion.1), channel_id=1, source_target_pairs={{0,2},{1,3},{2,0},{3,1},{4,6},{5,7},{6,4},{7,5},{8,10},{9,11},{10,... | collective-permute-start | bytes 104 | tf_op jit(solution)/shard_map/ppermute | solution.py:450
  38.7 5.5 %collective-permute-start.3 = (s32[2,4]{1,0:T(2,128)S(1)}, s32[2,4]{1,0:T(2,128)S(1)}, u32[]{:S(2)}, u32[]{:S(2)}) collective-permute-start(s32[2,4]{1,0:T(2,128)S(1)} %pad_add_fusion.1), channel_id=1, source_target_pairs={{0,1},{1,2},{2,3},{3,0},{4,5},{5,6},{6,7},{7,4},{8,9},{9,10},{10,1... | collective-permute-start | bytes 104 | tf_op jit(solution)/shard_map/ppermute | solution.py:450
  46.9 65.6 %all-gather.7.cloned.1.call-start = ((), (), s32[]{:S(2)}) async-start(), calls=%async_computation.5 | async-start | bytes 2359296 | tf_op jit(solution)/shard_map/all_gather | solution.py:503
  47.7 20.4 %copy-start.11 = (bf16[2,256,256]{2,1,0:T(8,128)(2,1)}, bf16[2,256,256]{2,1,0:T(8,128)(2,1)S(1)}, u32[]{:S(2)}) copy-start(bf16[2,256,256]{2,1,0:T(8,128)(2,1)S(1)} %get-tuple-element.56.refs_2_) | copy-start | bytes 786436
  47.7 15.2 %collective-permute-start.8 = (bf16[2,256,256]{2,1,0:T(8,128)(2,1)S(1)}, bf16[2,256,256]{2,1,0:T(8,128)(2,1)S(1)}, u32[]{:S(2)}, u32[]{:S(2)}) collective-permute-start(bf16[2,256,256]{2,1,0:T(8,128)(2,1)S(1)} %get-tuple-element.56.refs_2_), channel_id=1, source_target_pairs={{0,24},{8,0},{16,8},{24,16},{1,25},{9,1},{17,9},{25,17},{2,26},{10... | collective-permute-start | bytes 786440 | tf_op jit(solution)/shard_map/ppermute | solution.py:450
  51.7 11.2 %collective-permute-start.7 = (bf16[2,256,256]{2,1,0:T(8,128)(2,1)S(1)}, bf16[2,256,256]{2,1,0:T(8,128)(2,1)S(1)}, u32[]{:S(2)}, u32[]{:S(2)}) collective-permute-start(bf16[2,256,256]{2,1,0:T(8,128)(2,1)S(1)} %get-tuple-element.56.refs_2_), channel_id=1, source_target_pairs={{0,16},{8,24},{16,0},{24,8},{1,17},{9,25},{17,1},{25,9},{2,18},{10... | collective-permute-start | bytes 786440 | tf_op jit(solution)/shard_map/ppermute | solution.py:450
  51.7 14.8 %collective-permute-start.6 = (bf16[2,256,256]{2,1,0:T(8,128)(2,1)S(1)}, bf16[2,256,256]{2,1,0:T(8,128)(2,1)S(1)}, u32[]{:S(2)}, u32[]{:S(2)}) collective-permute-start(bf16[2,256,256]{2,1,0:T(8,128)(2,1)S(1)} %get-tuple-element.56.refs_2_), channel_id=1, source_target_pairs={{0,8},{8,16},{16,24},{24,0},{1,9},{9,17},{17,25},{25,1},{2,10},{10... | collective-permute-start | bytes 786440 | tf_op jit(solution)/shard_map/ppermute | solution.py:450
  53.0 13.5 %collective-permute-start.9 = (bf16[2,256,256]{2,1,0:T(8,128)(2,1)S(1)}, bf16[2,256,256]{2,1,0:T(8,128)(2,1)S(1)}, u32[]{:S(2)}, u32[]{:S(2)}) collective-permute-start(bf16[2,256,256]{2,1,0:T(8,128)(2,1)S(1)} %get-tuple-element.56.refs_2_), channel_id=1, source_target_pairs={{0,4},{4,0},{1,5},{5,1},{2,6},{6,2},{3,7},{7,3},{8,12},{12,8},{9,1... | collective-permute-start | bytes 786440 | tf_op jit(solution)/shard_map/ppermute | solution.py:450
  62.9 3.7 %copy-start.13 = (bf16[2,256,256]{2,1,0:T(8,128)(2,1)}, bf16[2,256,256]{2,1,0:T(8,128)(2,1)S(1)}, u32[]{:S(2)}) copy-start(bf16[2,256,256]{2,1,0:T(8,128)(2,1)S(1)} %collective-permute-done.8.refs_5_) | copy-start | bytes 786436
  62.9 3.7 %collective-permute-start.12 = (bf16[2,256,256]{2,1,0:T(8,128)(2,1)S(1)}, bf16[2,256,256]{2,1,0:T(8,128)(2,1)S(1)}, u32[]{:S(2)}, u32[]{:S(2)}) collective-permute-start(bf16[2,256,256]{2,1,0:T(8,128)(2,1)S(1)} %collective-permute-done.8.refs_5_), channel_id=1, source_target_pairs={{0,4},{4,0},{1,5},{5,1},{2,6},{6,2},{3,7},{7,3},{8,12},{12,8},{9,1... | collective-permute-start | bytes 786440 | tf_op jit(solution)/shard_map/ppermute | solution.py:450
  62.9 3.7 %copy-start.14 = (bf16[2,256,256]{2,1,0:T(8,128)(2,1)}, bf16[2,256,256]{2,1,0:T(8,128)(2,1)S(1)}, u32[]{:S(2)}) copy-start(bf16[2,256,256]{2,1,0:T(8,128)(2,1)S(1)} %collective-permute-done.7.refs_4_) | copy-start | bytes 786436
  62.9 3.7 %collective-permute-start.11 = (bf16[2,256,256]{2,1,0:T(8,128)(2,1)S(1)}, bf16[2,256,256]{2,1,0:T(8,128)(2,1)S(1)}, u32[]{:S(2)}, u32[]{:S(2)}) collective-permute-start(bf16[2,256,256]{2,1,0:T(8,128)(2,1)S(1)} %collective-permute-done.7.refs_4_), channel_id=1, source_target_pairs={{0,4},{4,0},{1,5},{5,1},{2,6},{6,2},{3,7},{7,3},{8,12},{12,8},{9,1... | collective-permute-start | bytes 786440 | tf_op jit(solution)/shard_map/ppermute | solution.py:450
  66.5 1.5 collective-permute-start.10
  66.5 1.5 copy-start.16
  66.5 1.5 copy-start.17
  83.4 4.4 %collective-permute-start.13 = (bf16[4,2,2,256,256]{4,3,2,1,0:T(8,128)(2,1)}, bf16[4,2,2,256,256]{4,3,2,1,0:T(8,128)(2,1)S(1)}, u32[]{:S(2)}, u32[]{:S(2)}) collective-permute-start(bf16[4,2,2,256,256]{4,3,2,1,0:T(8,128)(2,1)} %bitcast.39), channel_id=1, source_target_pairs={{0,4},{4,0},{1,5},{5,1},{2,6},{6,2},{3,7},{7,3},{8,12},{12,8},{9,1... | collective-permute-start | bytes 6291464 | tf_op jit(solution)/shard_map/ppermute | solution.py:450
  87.8 1.4 copy-start.12
  112.4 12.9 %copy-start.7 = (f32[2,2,256,256]{3,2,1,0:T(8,128)S(1)}, f32[2,2,256,256]{3,2,1,0:T(8,128)}, u32[]{:S(2)}) copy-start(f32[2,2,256,256]{3,2,1,0:T(8,128)} %copy-done.6) | copy-start | bytes 3145732
  148.8 29.9 %all-to-all-start.1 = ((f32[16,2,2,16,256]{4,3,2,1,0:T(8,128)}), f32[16,2,2,16,256]{4,3,2,1,0:T(8,128)S(1)}, u32[]{:S(2)}, u32[]{:S(2)}) async-start(f32[16,2,2,16,256]{4,3,2,1,0:T(8,128)} %get-tuple-element.47), calls=%async_computation.1 | async-start | bytes 2097152 | tf_op jit(solution)/shard_map/all_to_all | solution.py:521
  178.7 24.5 %all-to-all-start.2 = ((f32[16,2,2,16,256]{4,3,2,1,0:T(8,128)}), f32[16,2,2,16,256]{4,3,2,1,0:T(8,128)S(1)}, u32[]{:S(2)}, u32[]{:S(2)}) async-start(f32[16,2,2,16,256]{4,3,2,1,0:T(8,128)} %get-tuple-element.53), calls=%async_computation.2 | async-start | bytes 2097152 | tf_op jit(solution)/shard_map/all_to_all | solution.py:524
  (7 other events, 6.5 us)
Sparse Core Ops, SparseCore 0:
  47.0 32.9 all-gather.4
  81.6 23.2 all-gather.6

commit v6 on v5

--- a/solution.py
+++ b/solution.py
@@ -396,7 +396,7 @@
             scratch_shapes=[pltpu.VMEM((2, 2, N, N), BF16)] * 3,
         ),
         out_shape=[jax.ShapeDtypeStruct(WAVE, F32), jax.ShapeDtypeStruct(kept, F32)]
-        + [jax.ShapeDtypeStruct((4, 1, 2, N, N), BF16)] * (2 * stacks),
+        + [pltpu.HBM((4, 1, 2, N, N), BF16)] * (2 * stacks),
         compiler_params=PARAMS,
         cost_estimate=cost(len(chunks)),
         name="forward",

time: 226 us -> 225 us (level)
    unnamed x40 -> x36, local copies, waits for them, and re-layouts: 6.95 us -> 4.93 us
  transfers between devices with their start and end apart: 19 -> 19, of which waited for: 11 -> 11; matrix products, arithmetic and copies ran while one was open for 6% -> 6% of each run, Pallas kernels for 27% -> 28%
where the time goes in v6:
time: 225 us; the launch traced here: 224 us
  Pallas kernels  104 us (46%)
  waiting for transfers between devices  44.1 us (20%)
  starting transfers between devices  29 us (13%)
  between operations  13.7 us (6%)
  local copies, waits for them, and re-layouts  13.1 us (6%)
  blocking collectives  13.1 us (6%)
  other arithmetic  7.24 us (3%)
    pallas_call x3, Pallas kernels, run_forward(): pl.pallas_call(body, grid_spec=pltpu.PrefetchScalarGridSpec(num_scalar_pr...  48.7 us
    pallas_call x2, Pallas kernels, run_backward(): pl.pallas_call(body, grid_spec=pltpu.PrefetchScalarGridSpec(num_scalar_pr...  48 us
    ppermute x14, waiting for transfers between devices, from_neighbour(): lax.ppermute(block, axis, [(i, (i + distance) % size) for i in range(size)])  26.4 us
    all_to_all x1, waiting for transfers between devices, on_device(): got01 = lax.all_to_all(sent01, ('x', 'y'), 0, 0, tiled=True)  15.9 us
    ppermute x14, starting transfers between devices, from_neighbour(): lax.ppermute(block, axis, [(i, (i + distance) % size) for i in range(size)])  13.3 us
    all_to_all x1, blocking collectives, on_device(): out = lax.all_to_all(sums, ('x', 'y'), 0, 0, tiled=True)  13.1 us
    all_to_all x1, starting transfers between devices, on_device(): got01 = lax.all_to_all(sent01, ('x', 'y'), 0, 0, tiled=True)  7.25 us
    unnamed x36, local copies, waits for them, and re-layouts  4.93 us
  transfers between devices with their start and end apart: 19, of which 11 were waited for; matrix products, arithmetic and copies ran while one was open for 6% of the time, Pallas kernels for 28%

profile of v6, /device:TPU:0, one launch (start us, length us, event | category | flops | bytes accessed | tf_op | source)
XLA Modules:
  0.0 223.9 jit_solution(14588203510589337993)
XLA Ops:
  6.5 2.8 %collective-permute-start.1 = (bf16[2,1,128,512]{3,2,1,0:T(8,128)(2,1)}, bf16[2,1,128,512]{3,2,1,0:T(8,128)(2,1)S(1)}, u32[]{:S(2)}, u32[]{:S(2)}) collective-permute-start(bf16[2,1,128,512]{3,2,1,0:T(8,128)(2,1)} %refs_0_.1), channel_id=1, source_target_pairs={{0,3},{1,0},{2,1},{3,2},{4,7},{5,4},{6,5},{7,6},{8,11},{9,8},{10,9... | collective-permute-start | bytes 786440 | tf_op jit(solution)/shard_map/ppermute | solution.py:450
  9.4 2.3 %collective-permute-start.2 = (bf16[2,1,128,512]{3,2,1,0:T(8,128)(2,1)}, bf16[2,1,128,512]{3,2,1,0:T(8,128)(2,1)S(1)}, u32[]{:S(2)}, u32[]{:S(2)}) collective-permute-start(bf16[2,1,128,512]{3,2,1,0:T(8,128)(2,1)} %refs_0_.1), channel_id=1, source_target_pairs={{0,2},{1,3},{2,0},{3,1},{4,6},{5,7},{6,4},{7,5},{8,10},{9,11},{10,... | collective-permute-start | bytes 786440 | tf_op jit(solution)/shard_map/ppermute | solution.py:450
  12.7 1.3 multiply_subtract_fusion
  18.3 1.6 rev.27
  19.9 1.0 collective-permute-done.1.refs_2_
  20.9 3.3 %collective-permute-done.refs_1_ = bf16[2,1,128,512]{3,2,1,0:T(8,128)(2,1)S(1)} collective-permute-done((bf16[2,1,128,512]{3,2,1,0:T(8,128)(2,1)}, bf16[2,1,128,512]{3,2,1,0:T(8,128)(2,1)S(1)}, u32[]{:S(2)}, u32[]{:S(2)}) %collective-permute-start) | collective-permute-done | bytes 262176 | tf_op jit(solution)/shard_map/ppermute | solution.py:450
  24.2 4.4 %cut.1 = bf16[4,2,256,256]{3,2,1,0:T(8,128)(2,1)} custom-call(s32[4]{0:T(128)S(1)} %copy-done.2, s32[4]{0:T(128)S(1)} %copy-done.1, s32[4]{0:T(128)S(1)} %add_multiply_fusion.starts_ref, bf16[2,1,128,512]{3,2,1,0:T(8,128)(2,1)S(1)} %copy-done, bf16[2,1,128,512]{3,2,1,0:T(8,128)(2,1)S(1)} %collective-permute-done.refs_1_, ...), custom_call_target="tpu_custom_call" | custom-call | tf_op jit(solution)/shard_map/cut/pallas_call | solution.py:350
  28.6 4.5 %all-to-all-start = ((bf16[4,2,256,256]{3,2,1,0:T(8,128)(2,1)}), bf16[4,2,256,256]{3,2,1,0:T(8,128)(2,1)S(1)}, u32[]{:S(2)}, u32[]{:S(2)}) async-start(bf16[4,2,256,256]{3,2,1,0:T(8,128)(2,1)} %cut.1), calls=%async_computation | async-start | bytes 2097152 | tf_op jit(solution)/shard_map/all_to_all | solution.py:499
  34.3 1.5 pad_add_fusion.2.refs_1_
  36.7 1.2 pad_maximum_fusion
  38.7 1.3 collective-permute-start.3
  40.0 1.5 collective-permute-done.5
  41.5 1.8 collective-permute-done.4
  44.2 1.8 all-to-all-done
  47.6 4.0 %collective-permute-start.8 = (bf16[2,256,256]{2,1,0:T(8,128)(2,1)S(1)}, bf16[2,256,256]{2,1,0:T(8,128)(2,1)S(1)}, u32[]{:S(2)}, u32[]{:S(2)}) collective-permute-start(bf16[2,256,256]{2,1,0:T(8,128)(2,1)S(1)} %get-tuple-element.56.refs_2_), channel_id=1, source_target_pairs={{0,24},{8,0},{16,8},{24,16},{1,25},{9,1},{17,9},{25,17},{2,26},{10... | collective-permute-start | bytes 786440 | tf_op jit(solution)/shard_map/ppermute | solution.py:450
  51.7 1.3 collective-permute-start.6
  53.1 9.6 %collective-permute-done.8.refs_5_ = bf16[2,256,256]{2,1,0:T(8,128)(2,1)S(1)} collective-permute-done((bf16[2,256,256]{2,1,0:T(8,128)(2,1)S(1)}, bf16[2,256,256]{2,1,0:T(8,128)(2,1)S(1)}, u32[]{:S(2)}, u32[]{:S(2)}) %collective-permute-start.8) | collective-permute-done | bytes 262176 | tf_op jit(solution)/shard_map/ppermute | solution.py:450
  63.2 3.1 %collective-permute-done.6.refs_3_ = bf16[2,256,256]{2,1,0:T(8,128)(2,1)S(1)} collective-permute-done((bf16[2,256,256]{2,1,0:T(8,128)(2,1)S(1)}, bf16[2,256,256]{2,1,0:T(8,128)(2,1)S(1)}, u32[]{:S(2)}, u32[]{:S(2)}) %collective-permute-start.6) | collective-permute-done | bytes 262176 | tf_op jit(solution)/shard_map/ppermute | solution.py:450
  68.6 13.5 %forward.3 = (f32[2,256,256]{2,1,0:T(8,128)S(1)}, f32[1,2,256,256]{3,2,1,0:T(8,128)S(1)}, bf16[4,1,2,256,256]{4,3,2,1,0:T(8,128)(2,1)}, bf16[4,1,2,256,256]{4,3,2,1,0:T(8,128)(2,1)}) custom-call(s32[4]{0:T(128)S(1)} %and_select_fusion.refs_0_, s32[4]{0:T(128)S(1)} %pad_add_fusion.2.refs_1_, bf16[2,256,256]{2,1,0:T(8,128)(2,1)} %copy-done.9, ...), custom_call_target="tpu_custom_call" | custom-call | flops 4294967296 | bytes 4194304 | tf_op jit(solution)/shard_map/forward/pallas_call | solution.py:387
  82.2 4.2 %collective-permute-done.13.refs_3_.refs_5_ = bf16[4,2,2,256,256]{4,3,2,1,0:T(8,128)(2,1)S(1)} collective-permute-done((bf16[4,2,2,256,256]{4,3,2,1,0:T(8,128)(2,1)}, bf16[4,2,2,256,256]{4,3,2,1,0:T(8,128)(2,1)S(1)}, u32[]{:S(2)}, u32[]{:S(2)}) %collective-permute-start.13) | collective-permute-done | bytes 2097184 | tf_op jit(solution)/shard_map/ppermute | solution.py:450
  86.5 1.3 copy-done.10
  87.8 22.3 %forward.4 = (f32[2,256,256]{2,1,0:T(8,128)S(1)}, f32[2,2,256,256]{3,2,1,0:T(8,128)S(1)}) custom-call(s32[4]{0:T(128)S(1)} %and_select_fusion.refs_0_, s32[4]{0:T(128)S(1)} %pad_add_fusion.2.refs_1_, bf16[4,2,2,256,256]{4,3,2,1,0:T(8,128)(2,1)} %bitcast.40, bf16[4,2,2,256,256]{4,3,2,1,0:T(8,128)(2,1)} %copy-done.10, bf16[4,2,2,256,256]{4,3,2,1,0:T(8,128)(2,1)} %bitcast.41, ...), custom_call_target="tpu_custom_call" | custom-call | flops 8589934592 | bytes 8388608 | tf_op jit(solution)/shard_map/forward/pallas_call | solution.py:387
  111.1 12.9 %forward.5 = (f32[2,256,256]{2,1,0:T(8,128)S(1)}, f32[1,2,256,256]{3,2,1,0:T(8,128)S(1)}) custom-call(s32[4]{0:T(128)S(1)} %and_select_fusion.refs_0_, s32[4]{0:T(128)S(1)} %pad_add_fusion.2.refs_1_, bf16[4,2,2,256,256]{4,3,2,1,0:T(8,128)(2,1)} %bitcast.44, f32[2,256,256]{2,1,0:T(8,128)S(1)} %get-tuple-element.42.refs_3_, ...), custom_call_target="tpu_custom_call" | custom-call | flops 4294967296 | bytes 4194304 | tf_op jit(solution)/shard_map/forward/pallas_call | solution.py:387
  124.0 23.5 %backward.2 = (f32[2,256,256]{2,1,0:T(8,128)S(1)}, f32[16,2,2,16,256]{4,3,2,1,0:T(8,128)}) custom-call(s32[4]{0:T(128)S(1)} %and_select_fusion.refs_0_, s32[4]{0:T(128)S(1)} %pad_add_fusion.2.refs_1_, bf16[4,2,2,256,256]{4,3,2,1,0:T(8,128)(2,1)} %bitcast.42, bf16[4,2,2,256,256]{4,3,2,1,0:T(8,128)(2,1)} %copy-done.10, bf16[4,2,2,256,256]{4,3,2,1,0:T(8,128)(2,1)} %bitcast.45, ...), custom_call_target="tpu_custom_call" | custom-call | flops 8589934592 | bytes 8388608 | tf_op jit(solution)/shard_map/backward/pallas_call | solution.py:413
  147.5 4.0 %all-to-all-start.1 = ((f32[16,2,2,16,256]{4,3,2,1,0:T(8,128)}), f32[16,2,2,16,256]{4,3,2,1,0:T(8,128)S(1)}, u32[]{:S(2)}, u32[]{:S(2)}) async-start(f32[16,2,2,16,256]{4,3,2,1,0:T(8,128)} %get-tuple-element.47), calls=%async_computation.1 | async-start | bytes 2097152 | tf_op jit(solution)/shard_map/all_to_all | solution.py:521
  151.5 1.2 copy-done.6
  152.7 24.5 %backward.3 = (f32[2,256,256]{2,1,0:T(8,128)}, f32[16,2,2,16,256]{4,3,2,1,0:T(8,128)}) custom-call(s32[4]{0:T(128)S(1)} %and_select_fusion.refs_0_, s32[4]{0:T(128)S(1)} %pad_add_fusion.2.refs_1_, bf16[4,1,2,256,256]{4,3,2,1,0:T(8,128)(2,1)} %get-tuple-element.48.refs_2_, bf16[4,1,2,256,256]{4,3,2,1,0:T(8,128)(2,1)} %get-tuple-element.49.refs_3_, ...), custom_call_target="tpu_custom_call" | custom-call | flops 8589934592 | bytes 8388608 | tf_op jit(solution)/shard_map/backward/pallas_call | solution.py:413
  177.2 7.2 %all-to-all-start.2 = ((f32[16,2,2,16,256]{4,3,2,1,0:T(8,128)}), f32[16,2,2,16,256]{4,3,2,1,0:T(8,128)S(1)}, u32[]{:S(2)}, u32[]{:S(2)}) async-start(f32[16,2,2,16,256]{4,3,2,1,0:T(8,128)} %get-tuple-element.53), calls=%async_computation.2 | async-start | bytes 2097152 | tf_op jit(solution)/shard_map/all_to_all | solution.py:524
  184.5 1.3 reduce.3
  185.9 15.9 %all-to-all-done.2.refs_3_ = f32[16,2,2,16,256]{4,3,2,1,0:T(8,128)S(1)} async-done(((f32[16,2,2,16,256]{4,3,2,1,0:T(8,128)}), f32[16,2,2,16,256]{4,3,2,1,0:T(8,128)S(1)}, u32[]{:S(2)}, u32[]{:S(2)}) %all-to-all-start.2) | async-done | bytes 1048608 | tf_op jit(solution)/shard_map/all_to_all | solution.py:524
  201.8 1.3 reduce.2
  203.2 13.1 %all_to_all.20 = f32[16,2,8,512]{3,2,1,0:T(8,128)S(1)} all-to-all(f32[16,2,8,512]{3,2,1,0:T(8,128)S(1)} %bitcast.34), channel_id=1, replica_groups=mesh['y'=4,'z'=4,'core'=2,'x'=4] {'x','y'}, dimensions={0} | all-to-all | bytes 1048576 | tf_op jit(solution)/shard_map/all_to_all | solution.py:529
  (82 shorter events, 15.6 us)
Async XLA Ops:
  6.5 7.7 %copy-start.8 = (f32[256,256]{1,0:T(8,128)S(1)}, f32[256,256]{1,0:T(8,128)}, u32[]{:S(2)}) copy-start(f32[256,256]{1,0:T(8,128)} %param.14) | copy-start | bytes 786436
  6.5 14.3 %collective-permute-start.1 = (bf16[2,1,128,512]{3,2,1,0:T(8,128)(2,1)}, bf16[2,1,128,512]{3,2,1,0:T(8,128)(2,1)S(1)}, u32[]{:S(2)}, u32[]{:S(2)}) collective-permute-start(bf16[2,1,128,512]{3,2,1,0:T(8,128)(2,1)} %refs_0_.1), channel_id=1, source_target_pairs={{0,3},{1,0},{2,1},{3,2},{4,7},{5,4},{6,5},{7,6},{8,11},{9,8},{10,9... | collective-permute-start | bytes 786440 | tf_op jit(solution)/shard_map/ppermute | solution.py:450
  9.4 14.8 %collective-permute-start = (bf16[2,1,128,512]{3,2,1,0:T(8,128)(2,1)}, bf16[2,1,128,512]{3,2,1,0:T(8,128)(2,1)S(1)}, u32[]{:S(2)}, u32[]{:S(2)}) collective-permute-start(bf16[2,1,128,512]{3,2,1,0:T(8,128)(2,1)} %refs_0_.1), channel_id=1, source_target_pairs={{0,1},{1,2},{2,3},{3,0},{4,5},{5,6},{6,7},{7,4},{8,9},{9,10},{10,1... | collective-permute-start | bytes 786440 | tf_op jit(solution)/shard_map/ppermute | solution.py:450
  9.4 14.8 %collective-permute-start.2 = (bf16[2,1,128,512]{3,2,1,0:T(8,128)(2,1)}, bf16[2,1,128,512]{3,2,1,0:T(8,128)(2,1)S(1)}, u32[]{:S(2)}, u32[]{:S(2)}) collective-permute-start(bf16[2,1,128,512]{3,2,1,0:T(8,128)(2,1)} %refs_0_.1), channel_id=1, source_target_pairs={{0,2},{1,3},{2,0},{3,1},{4,6},{5,7},{6,4},{7,5},{8,10},{9,11},{10,... | collective-permute-start | bytes 786440 | tf_op jit(solution)/shard_map/ppermute | solution.py:450
  14.0 2.8 %copy-start.1 = (s32[4]{0:T(128)S(1)}, s32[4]{0:T(128)}, u32[]{:S(2)}) copy-start(s32[4]{0:T(128)} %cols_ref.1) | copy-start | bytes 52
  14.0 3.4 %copy-start.2 = (s32[4]{0:T(128)S(1)}, s32[4]{0:T(128)}, u32[]{:S(2)}) copy-start(s32[4]{0:T(128)} %rows_ref.1) | copy-start | bytes 52
  14.2 9.9 %copy-start = (bf16[2,1,128,512]{3,2,1,0:T(8,128)(2,1)S(1)}, bf16[2,1,128,512]{3,2,1,0:T(8,128)(2,1)}, u32[]{:S(2)}) copy-start(bf16[2,1,128,512]{3,2,1,0:T(8,128)(2,1)} %refs_0_.1) | copy-start | bytes 786436
  28.6 17.4 %all-to-all-start = ((bf16[4,2,256,256]{3,2,1,0:T(8,128)(2,1)}), bf16[4,2,256,256]{3,2,1,0:T(8,128)(2,1)S(1)}, u32[]{:S(2)}, u32[]{:S(2)}) async-start(bf16[4,2,256,256]{3,2,1,0:T(8,128)(2,1)} %cut.1), calls=%async_computation | async-start | bytes 2097152 | tf_op jit(solution)/shard_map/all_to_all | solution.py:499
  33.0 3.7 %copy-start.7 = (f32[2,256,128]{2,1,0:T(8,128)S(1)}, f32[2,256,128]{2,1,0:T(8,128)}, u32[]{:S(2)}) copy-start(f32[2,256,128]{2,1,0:T(8,128)} %rev.27) | copy-start | bytes 786436
  33.0 49.1 %all-gather.5.cloned.1.call-start = ((), (), s32[]{:S(2)}) async-start(), calls=%async_computation.4 | async-start | bytes 2621440 | tf_op jit(solution)/shard_map/all_gather | solution.py:502
  36.7 31.9 %copy-start.3 = (bf16[4,256,256]{2,1,0:T(8,128)(2,1)S(1)}, bf16[4,256,256]{2,1,0:T(8,128)(2,1)}, u32[]{:S(2)}) copy-start(bf16[4,256,256]{2,1,0:T(8,128)(2,1)} %constant.81.clone.refs_12_.refs_8_.refs_5_.refs_7_) | copy-start | bytes 1572868
  37.9 3.6 %collective-permute-start.5 = (s32[2,4]{1,0:T(2,128)S(1)}, s32[2,4]{1,0:T(2,128)S(1)}, u32[]{:S(2)}, u32[]{:S(2)}) collective-permute-start(s32[2,4]{1,0:T(2,128)S(1)} %pad_add_fusion.1), channel_id=1, source_target_pairs={{0,3},{1,0},{2,1},{3,2},{4,7},{5,4},{6,5},{7,6},{8,11},{9,8},{10,9... | collective-permute-start | bytes 104 | tf_op jit(solution)/shard_map/ppermute | solution.py:450
  38.3 5.1 %collective-permute-start.4 = (s32[2,4]{1,0:T(2,128)S(1)}, s32[2,4]{1,0:T(2,128)S(1)}, u32[]{:S(2)}, u32[]{:S(2)}) collective-permute-start(s32[2,4]{1,0:T(2,128)S(1)} %pad_add_fusion.1), channel_id=1, source_target_pairs={{0,2},{1,3},{2,0},{3,1},{4,6},{5,7},{6,4},{7,5},{8,10},{9,11},{10,... | collective-permute-start | bytes 104 | tf_op jit(solution)/shard_map/ppermute | solution.py:450
  38.7 5.5 %collective-permute-start.3 = (s32[2,4]{1,0:T(2,128)S(1)}, s32[2,4]{1,0:T(2,128)S(1)}, u32[]{:S(2)}, u32[]{:S(2)}) collective-permute-start(s32[2,4]{1,0:T(2,128)S(1)} %pad_add_fusion.1), channel_id=1, source_target_pairs={{0,1},{1,2},{2,3},{3,0},{4,5},{5,6},{6,7},{7,4},{8,9},{9,10},{10,1... | collective-permute-start | bytes 104 | tf_op jit(solution)/shard_map/ppermute | solution.py:450
  46.8 64.3 %all-gather.7.cloned.1.call-start = ((), (), s32[]{:S(2)}) async-start(), calls=%async_computation.5 | async-start | bytes 2359296 | tf_op jit(solution)/shard_map/all_gather | solution.py:503
  47.6 20.2 %copy-start.9 = (bf16[2,256,256]{2,1,0:T(8,128)(2,1)}, bf16[2,256,256]{2,1,0:T(8,128)(2,1)S(1)}, u32[]{:S(2)}) copy-start(bf16[2,256,256]{2,1,0:T(8,128)(2,1)S(1)} %get-tuple-element.56.refs_2_) | copy-start | bytes 786436
  47.6 15.0 %collective-permute-start.8 = (bf16[2,256,256]{2,1,0:T(8,128)(2,1)S(1)}, bf16[2,256,256]{2,1,0:T(8,128)(2,1)S(1)}, u32[]{:S(2)}, u32[]{:S(2)}) collective-permute-start(bf16[2,256,256]{2,1,0:T(8,128)(2,1)S(1)} %get-tuple-element.56.refs_2_), channel_id=1, source_target_pairs={{0,24},{8,0},{16,8},{24,16},{1,25},{9,1},{17,9},{25,17},{2,26},{10... | collective-permute-start | bytes 786440 | tf_op jit(solution)/shard_map/ppermute | solution.py:450
  51.7 11.0 %collective-permute-start.7 = (bf16[2,256,256]{2,1,0:T(8,128)(2,1)S(1)}, bf16[2,256,256]{2,1,0:T(8,128)(2,1)S(1)}, u32[]{:S(2)}, u32[]{:S(2)}) collective-permute-start(bf16[2,256,256]{2,1,0:T(8,128)(2,1)S(1)} %get-tuple-element.56.refs_2_), channel_id=1, source_target_pairs={{0,16},{8,24},{16,0},{24,8},{1,17},{9,25},{17,1},{25,9},{2,18},{10... | collective-permute-start | bytes 786440 | tf_op jit(solution)/shard_map/ppermute | solution.py:450
  51.7 14.7 %collective-permute-start.6 = (bf16[2,256,256]{2,1,0:T(8,128)(2,1)S(1)}, bf16[2,256,256]{2,1,0:T(8,128)(2,1)S(1)}, u32[]{:S(2)}, u32[]{:S(2)}) collective-permute-start(bf16[2,256,256]{2,1,0:T(8,128)(2,1)S(1)} %get-tuple-element.56.refs_2_), channel_id=1, source_target_pairs={{0,8},{8,16},{16,24},{24,0},{1,9},{9,17},{17,25},{25,1},{2,10},{10... | collective-permute-start | bytes 786440 | tf_op jit(solution)/shard_map/ppermute | solution.py:450
  53.0 13.4 %collective-permute-start.9 = (bf16[2,256,256]{2,1,0:T(8,128)(2,1)S(1)}, bf16[2,256,256]{2,1,0:T(8,128)(2,1)S(1)}, u32[]{:S(2)}, u32[]{:S(2)}) collective-permute-start(bf16[2,256,256]{2,1,0:T(8,128)(2,1)S(1)} %get-tuple-element.56.refs_2_), channel_id=1, source_target_pairs={{0,4},{4,0},{1,5},{5,1},{2,6},{6,2},{3,7},{7,3},{8,12},{12,8},{9,1... | collective-permute-start | bytes 786440 | tf_op jit(solution)/shard_map/ppermute | solution.py:450
  62.7 3.7 %copy-start.11 = (bf16[2,256,256]{2,1,0:T(8,128)(2,1)}, bf16[2,256,256]{2,1,0:T(8,128)(2,1)S(1)}, u32[]{:S(2)}) copy-start(bf16[2,256,256]{2,1,0:T(8,128)(2,1)S(1)} %collective-permute-done.8.refs_5_) | copy-start | bytes 786436
  62.7 3.7 %collective-permute-start.12 = (bf16[2,256,256]{2,1,0:T(8,128)(2,1)S(1)}, bf16[2,256,256]{2,1,0:T(8,128)(2,1)S(1)}, u32[]{:S(2)}, u32[]{:S(2)}) collective-permute-start(bf16[2,256,256]{2,1,0:T(8,128)(2,1)S(1)} %collective-permute-done.8.refs_5_), channel_id=1, source_target_pairs={{0,4},{4,0},{1,5},{5,1},{2,6},{6,2},{3,7},{7,3},{8,12},{12,8},{9,1... | collective-permute-start | bytes 786440 | tf_op jit(solution)/shard_map/ppermute | solution.py:450
  62.7 3.7 %copy-start.12 = (bf16[2,256,256]{2,1,0:T(8,128)(2,1)}, bf16[2,256,256]{2,1,0:T(8,128)(2,1)S(1)}, u32[]{:S(2)}) copy-start(bf16[2,256,256]{2,1,0:T(8,128)(2,1)S(1)} %collective-permute-done.7.refs_4_) | copy-start | bytes 786436
  62.7 3.7 %collective-permute-start.11 = (bf16[2,256,256]{2,1,0:T(8,128)(2,1)S(1)}, bf16[2,256,256]{2,1,0:T(8,128)(2,1)S(1)}, u32[]{:S(2)}, u32[]{:S(2)}) collective-permute-start(bf16[2,256,256]{2,1,0:T(8,128)(2,1)S(1)} %collective-permute-done.7.refs_4_), channel_id=1, source_target_pairs={{0,4},{4,0},{1,5},{5,1},{2,6},{6,2},{3,7},{7,3},{8,12},{12,8},{9,1... | collective-permute-start | bytes 786440 | tf_op jit(solution)/shard_map/ppermute | solution.py:450
  66.3 1.5 collective-permute-start.10
  66.4 1.5 copy-start.14
  66.4 1.5 copy-start.15
  82.1 4.4 %collective-permute-start.13 = (bf16[4,2,2,256,256]{4,3,2,1,0:T(8,128)(2,1)}, bf16[4,2,2,256,256]{4,3,2,1,0:T(8,128)(2,1)S(1)}, u32[]{:S(2)}, u32[]{:S(2)}) collective-permute-start(bf16[4,2,2,256,256]{4,3,2,1,0:T(8,128)(2,1)} %bitcast.39), channel_id=1, source_target_pairs={{0,4},{4,0},{1,5},{5,1},{2,6},{6,2},{3,7},{7,3},{8,12},{12,8},{9,1... | collective-permute-start | bytes 6291464 | tf_op jit(solution)/shard_map/ppermute | solution.py:450
  86.5 1.4 copy-start.10
  111.1 12.9 %copy-start.5 = (f32[2,2,256,256]{3,2,1,0:T(8,128)S(1)}, f32[2,2,256,256]{3,2,1,0:T(8,128)}, u32[]{:S(2)}) copy-start(f32[2,2,256,256]{3,2,1,0:T(8,128)} %copy-done.4) | copy-start | bytes 3145732
  147.5 29.7 %all-to-all-start.1 = ((f32[16,2,2,16,256]{4,3,2,1,0:T(8,128)}), f32[16,2,2,16,256]{4,3,2,1,0:T(8,128)S(1)}, u32[]{:S(2)}, u32[]{:S(2)}) async-start(f32[16,2,2,16,256]{4,3,2,1,0:T(8,128)} %get-tuple-element.47), calls=%async_computation.1 | async-start | bytes 2097152 | tf_op jit(solution)/shard_map/all_to_all | solution.py:521
  177.2 24.5 %all-to-all-start.2 = ((f32[16,2,2,16,256]{4,3,2,1,0:T(8,128)}), f32[16,2,2,16,256]{4,3,2,1,0:T(8,128)S(1)}, u32[]{:S(2)}, u32[]{:S(2)}) async-start(f32[16,2,2,16,256]{4,3,2,1,0:T(8,128)} %get-tuple-element.53), calls=%async_computation.2 | async-start | bytes 2097152 | tf_op jit(solution)/shard_map/all_to_all | solution.py:524
  (5 other events, 4.5 us)
Sparse Core Ops, SparseCore 0:
  47.0 32.9 all-gather.4
  81.6 23.3 all-gather.6

commit v7 on v6

--- a/solution.py
+++ b/solution.py
@@ -226,7 +226,11 @@
     chunks = len(counts)
     held, (ct_ref, prop_ref, tabs_ref, *rest) = rest[: sum(counts)], rest[sum(counts) :]
     kept_refs, rest = rest[:chunks], rest[chunks:]
-    out_ref, sent_ref, grad_ref, mixed_ref, pair_ref, lhs_ref, rhs_ref = rest
+    if from_end:
+        out_ref, sent_ref, *rest = rest
+    else:
+        sent_ref, out_ref, *rest = rest
+    grad_ref, mixed_ref, pair_ref, lhs_ref, rhs_ref = rest
     step = pl.program_id(0)
     chunk, at_z = chunks - 1 - step // 4, 3 - step % 4
     core = scalars[1]
@@ -286,10 +290,10 @@
 
     @pl.when(at_z == 0)
     def _():
-        at = iota((N, N), 0)
-        slot = M * (at // 8 % 2) + 8 * (at // 16) + at % 8
-        rows = one_hot((paired_index((N, N), 1) + scalars[2]) % N, slot)
-        cols = one_hot((paired_index((N, N), 0) + scalars[3]) % N, iota((N, N), 1))
+        at = iota((N, 1), 0)
+        slot = M * ((at >> 3) & 1) + 8 * (at >> 4) + (at & 7)
+        rows = one_hot((paired_index((1, N), 1) + scalars[2]) & (N - 1), slot)
+        cols = one_hot((paired_index((N, 1), 0) + scalars[3]) & (N - 1), iota((1, N), 1))
         for part in (0, 1):
             high, low = split(grad_ref[part])
             rolled = [dot(rows, dot(x, cols).astype(BF16)) for x in (high, low)]
@@ -322,11 +326,9 @@
     strip, width = blocks[0].shape[-2:]
     height = strip * len(blocks)
     at = pl.program_id(0)
-    held = iota((N, height), 1) % strip
-    for i in range(len(blocks)):
-        held += jnp.where(iota((N, height), 1) // strip == i, starts_ref[i], 0)
-    rows = one_hot(paired_index((N, height), 0) + rows_ref[at], held)
-    cols = one_hot(paired_index((width, N), 1) + cols_ref[at], iota((width, N), 0))
+    held = jnp.concatenate([iota((1, strip), 1) + starts_ref[i] for i in range(len(blocks))], axis=1)
+    rows = one_hot(paired_index((N, 1), 0) + rows_ref[at], held)
+    cols = one_hot(paired_index((1, N), 1) + cols_ref[at], iota((width, 1), 0))
     for part in (0, 1):
         whole_part = jnp.concatenate([block[part, 0] for block in blocks], axis=0)
         out_ref[0, part] = dot(dot(rows, whole_part).astype(BF16), cols).astype(BF16)
@@ -418,10 +420,10 @@
             in_specs=chunk_specs(chunks, True)
             + [whole(WAVE), whole(WAVE), whole((4, N, N))]
             + [pl.BlockSpec((1, *WAVE), lambda *_, at=at: (at, 0, 0, 0)) for _, at in kept],
-            out_specs=[whole(WAVE), whole(sent)],
-            scratch_shapes=[pltpu.VMEM(WAVE, F32)] * 2 + [pltpu.VMEM((2, 2, N, N), BF16)] * 3,
+            out_specs=[whole(WAVE)] * from_end + [whole(sent)],
+            scratch_shapes=[pltpu.VMEM(WAVE, F32)] * (3 - from_end) + [pltpu.VMEM((2, 2, N, N), BF16)] * 3,
         ),
-        out_shape=[jax.ShapeDtypeStruct(WAVE, F32), jax.ShapeDtypeStruct(sent, F32)],
+        out_shape=[jax.ShapeDtypeStruct(WAVE, F32)] * from_end + [jax.ShapeDtypeStruct(sent, F32)],
         compiler_params=PARAMS,
         cost_estimate=cost(len(chunks)),
         name="backward",
@@ -499,6 +501,7 @@
     patches = lax.all_to_all(patches, "y", 0, 0, tiled=True)
     small = (positions, prop, inten, wave, scalars)
     patches, (positions, prop, inten, wave, scalars) = lax.optimization_barrier((patches, small))
+    first, patches = lax.optimization_barrier((patches[0], patches))
     middle = lax.all_gather(patches[1:3], "z", axis=0)
     final = lax.all_gather(patches[3:], ("z", "core"), axis=0)
     order = around_of(z)
@@ -506,7 +509,7 @@
     def forward(chunks, wave, **more):
         return run_forward(order, scalars, chunks, wave, prop, tabs, **more)
 
-    wave, kept0, *stacked = forward([(ring_gather(patches[0]), 0)], wave, stacks=True)
+    wave, kept0, *stacked = forward([(ring_gather(first), 0)], wave, stacks=True)
     middle, wave = lax.optimization_barrier((middle, wave))
     middle = [middle, from_neighbour(middle, "core", 1)]
     wave, kept12 = forward([(middle, 0), (middle, 1)], wave)
@@ -519,7 +522,7 @@
 
     wave, sent23 = backward([(middle, 1), (final, 0)], wave, [(kept12, 1), (kept3, 0)], from_end=True)
     got23 = lax.all_to_all(sent23, ("x", "y"), 0, 0, tiled=True)
-    wave, sent01 = backward([(stacked, 0), (middle, 0)], wave, [(kept0, 0), (kept12, 0)])
+    (sent01,) = backward([(stacked, 0), (middle, 0)], wave, [(kept0, 0), (kept12, 0)])
     got23, sent01 = lax.optimization_barrier((got23, sent01))
     got01 = lax.all_to_all(sent01, ("x", "y"), 0, 0, tiled=True)
     got = [got01, got23]

time: 225 us -> 223 us (level)
    unnamed x36 -> x30, local copies, waits for them, and re-layouts: 4.93 us -> 4.27 us
where the time goes in v7:
time: 223 us
  Pallas kernels  103 us (46%)
  waiting for transfers between devices  43.2 us (19%)
  starting transfers between devices  29.6 us (13%)
  between operations  13.7 us (6%)
  blocking collectives  13.1 us (6%)
  local copies, waits for them, and re-layouts  12.4 us (6%)
  other arithmetic  7.13 us (3%)
    pallas_call x3, Pallas kernels, run_forward(): pl.pallas_call(body, grid_spec=pltpu.PrefetchScalarGridSpec(num_scalar_pr...  48.7 us
    pallas_call x2, Pallas kernels, run_backward(): pl.pallas_call(body, grid_spec=pltpu.PrefetchScalarGridSpec(num_scalar_pr...  47.8 us
    ppermute x14, waiting for transfers between devices, from_neighbour(): lax.ppermute(block, axis, [(i, (i + distance) % size) for i in range(size)])  25.5 us
    all_to_all x1, waiting for transfers between devices, on_device(): got01 = lax.all_to_all(sent01, ('x', 'y'), 0, 0, tiled=True)  15.8 us
    ppermute x14, starting transfers between devices, from_neighbour(): lax.ppermute(block, axis, [(i, (i + distance) % size) for i in range(size)])  13.3 us
    all_to_all x1, blocking collectives, on_device(): out = lax.all_to_all(sums, ('x', 'y'), 0, 0, tiled=True)  13.1 us
    all_to_all x1, starting transfers between devices, on_device(): got01 = lax.all_to_all(sent01, ('x', 'y'), 0, 0, tiled=True)  7.22 us
    all_to_all x1, starting transfers between devices, on_device(): got23 = lax.all_to_all(sent23, ('x', 'y'), 0, 0, tiled=True)  4.53 us
  transfers between devices with their start and end apart: 19, of which 11 were waited for; matrix products, arithmetic and copies ran while one was open for 6% of the time, Pallas kernels for 28%

profile of v7, /device:TPU:0, one launch (start us, length us, event | category | flops | bytes accessed | tf_op | source)
XLA Modules:
  0.0 222.7 jit_solution(16135794149860665382)
XLA Ops:
  6.5 2.8 %collective-permute-start.1 = (bf16[2,1,128,512]{3,2,1,0:T(8,128)(2,1)}, bf16[2,1,128,512]{3,2,1,0:T(8,128)(2,1)S(1)}, u32[]{:S(2)}, u32[]{:S(2)}) collective-permute-start(bf16[2,1,128,512]{3,2,1,0:T(8,128)(2,1)} %refs_0_.1), channel_id=1, source_target_pairs={{0,3},{1,0},{2,1},{3,2},{4,7},{5,4},{6,5},{7,6},{8,11},{9,8},{10,9... | collective-permute-start | bytes 786440 | tf_op jit(solution)/shard_map/ppermute | solution.py:452
  9.4 2.3 %collective-permute-start.2 = (bf16[2,1,128,512]{3,2,1,0:T(8,128)(2,1)}, bf16[2,1,128,512]{3,2,1,0:T(8,128)(2,1)S(1)}, u32[]{:S(2)}, u32[]{:S(2)}) collective-permute-start(bf16[2,1,128,512]{3,2,1,0:T(8,128)(2,1)} %refs_0_.1), channel_id=1, source_target_pairs={{0,2},{1,3},{2,0},{3,1},{4,6},{5,7},{6,4},{7,5},{8,10},{9,11},{10,... | collective-permute-start | bytes 786440 | tf_op jit(solution)/shard_map/ppermute | solution.py:452
  12.7 1.3 multiply_subtract_fusion
  18.2 1.6 rev.27
  20.9 3.3 %collective-permute-done.refs_1_ = bf16[2,1,128,512]{3,2,1,0:T(8,128)(2,1)S(1)} collective-permute-done((bf16[2,1,128,512]{3,2,1,0:T(8,128)(2,1)}, bf16[2,1,128,512]{3,2,1,0:T(8,128)(2,1)S(1)}, u32[]{:S(2)}, u32[]{:S(2)}) %collective-permute-start) | collective-permute-done | bytes 262176 | tf_op jit(solution)/shard_map/ppermute | solution.py:452
  24.2 4.4 %cut.1 = bf16[4,2,256,256]{3,2,1,0:T(8,128)(2,1)} custom-call(s32[4]{0:T(128)S(1)} %copy-done.2, s32[4]{0:T(128)S(1)} %copy-done.1, s32[4]{0:T(128)S(1)} %add_multiply_fusion.starts_ref, bf16[2,1,128,512]{3,2,1,0:T(8,128)(2,1)S(1)} %copy-done, bf16[2,1,128,512]{3,2,1,0:T(8,128)(2,1)S(1)} %collective-permute-done.refs_1_, ...), custom_call_target="tpu_custom_call" | custom-call | tf_op jit(solution)/shard_map/cut/pallas_call | solution.py:352
  28.5 4.5 %all-to-all-start = ((bf16[4,2,256,256]{3,2,1,0:T(8,128)(2,1)}), bf16[4,2,256,256]{3,2,1,0:T(8,128)(2,1)S(1)}, u32[]{:S(2)}, u32[]{:S(2)}) async-start(bf16[4,2,256,256]{3,2,1,0:T(8,128)(2,1)} %cut.1), calls=%async_computation | async-start | bytes 2097152 | tf_op jit(solution)/shard_map/all_to_all | solution.py:501
  34.3 1.4 pad_add_fusion.2.refs_1_
  36.6 1.2 pad_maximum_fusion
  38.6 1.3 collective-permute-start.3
  39.9 1.5 collective-permute-done.5
  41.4 1.8 collective-permute-done.4
  44.1 1.8 all-to-all-done
  47.0 4.1 %collective-permute-start.8 = (bf16[2,256,256]{2,1,0:T(8,128)(2,1)S(1)}, bf16[2,256,256]{2,1,0:T(8,128)(2,1)}, u32[]{:S(2)}, u32[]{:S(2)}) collective-permute-start(bf16[2,256,256]{2,1,0:T(8,128)(2,1)S(1)} %slice_bitcast_fusion.refs_2_), channel_id=1, source_target_pairs={{0,24},{8,0},{16,8},{24,16},{1,25},{9,1},{17,9},{25,17},{2,26},{10... | collective-permute-start | bytes 786440 | tf_op jit(solution)/shard_map/ppermute | solution.py:452
  51.1 1.3 collective-permute-start.6
  53.2 7.7 %collective-permute-done.8.refs_5_ = bf16[2,256,256]{2,1,0:T(8,128)(2,1)} collective-permute-done((bf16[2,256,256]{2,1,0:T(8,128)(2,1)S(1)}, bf16[2,256,256]{2,1,0:T(8,128)(2,1)}, u32[]{:S(2)}, u32[]{:S(2)}) %collective-permute-start.8) | collective-permute-done | bytes 262176 | tf_op jit(solution)/shard_map/ppermute | solution.py:452
  61.4 3.2 %collective-permute-done.6.refs_3_ = bf16[2,256,256]{2,1,0:T(8,128)(2,1)} collective-permute-done((bf16[2,256,256]{2,1,0:T(8,128)(2,1)S(1)}, bf16[2,256,256]{2,1,0:T(8,128)(2,1)}, u32[]{:S(2)}, u32[]{:S(2)}) %collective-permute-start.6) | collective-permute-done | bytes 262176 | tf_op jit(solution)/shard_map/ppermute | solution.py:452
  64.7 1.7 collective-permute-done.10.refs_7_
  67.1 13.5 %forward.3 = (f32[2,256,256]{2,1,0:T(8,128)S(1)}, f32[1,2,256,256]{3,2,1,0:T(8,128)S(1)}, bf16[4,1,2,256,256]{4,3,2,1,0:T(8,128)(2,1)}, bf16[4,1,2,256,256]{4,3,2,1,0:T(8,128)(2,1)}) custom-call(s32[4]{0:T(128)S(1)} %and_select_fusion.refs_0_, s32[4]{0:T(128)S(1)} %pad_add_fusion.2.refs_1_, bf16[2,256,256]{2,1,0:T(8,128)(2,1)} %copy-done.9, ...), custom_call_target="tpu_custom_call" | custom-call | flops 4294967296 | bytes 4194304 | tf_op jit(solution)/shard_map/forward/pallas_call | solution.py:389
  80.8 4.2 %collective-permute-done.13.refs_3_.refs_5_ = bf16[4,2,2,256,256]{4,3,2,1,0:T(8,128)(2,1)S(1)} collective-permute-done((bf16[4,2,2,256,256]{4,3,2,1,0:T(8,128)(2,1)}, bf16[4,2,2,256,256]{4,3,2,1,0:T(8,128)(2,1)S(1)}, u32[]{:S(2)}, u32[]{:S(2)}) %collective-permute-start.13) | collective-permute-done | bytes 2097184 | tf_op jit(solution)/shard_map/ppermute | solution.py:452
  85.0 1.4 copy-done.10
  86.4 22.3 %forward.4 = (f32[2,256,256]{2,1,0:T(8,128)S(1)}, f32[2,2,256,256]{3,2,1,0:T(8,128)S(1)}) custom-call(s32[4]{0:T(128)S(1)} %and_select_fusion.refs_0_, s32[4]{0:T(128)S(1)} %pad_add_fusion.2.refs_1_, bf16[4,2,2,256,256]{4,3,2,1,0:T(8,128)(2,1)} %bitcast.40, bf16[4,2,2,256,256]{4,3,2,1,0:T(8,128)(2,1)} %copy-done.10, bf16[4,2,2,256,256]{4,3,2,1,0:T(8,128)(2,1)} %bitcast.41, ...), custom_call_target="tpu_custom_call" | custom-call | flops 8589934592 | bytes 8388608 | tf_op jit(solution)/shard_map/forward/pallas_call | solution.py:389
  109.6 12.9 %forward.5 = (f32[2,256,256]{2,1,0:T(8,128)S(1)}, f32[1,2,256,256]{3,2,1,0:T(8,128)S(1)}) custom-call(s32[4]{0:T(128)S(1)} %and_select_fusion.refs_0_, s32[4]{0:T(128)S(1)} %pad_add_fusion.2.refs_1_, bf16[4,2,2,256,256]{4,3,2,1,0:T(8,128)(2,1)} %bitcast.44, f32[2,256,256]{2,1,0:T(8,128)S(1)} %get-tuple-element.45.refs_3_, ...), custom_call_target="tpu_custom_call" | custom-call | flops 4294967296 | bytes 4194304 | tf_op jit(solution)/shard_map/forward/pallas_call | solution.py:389
  122.5 23.4 %backward.2 = (f32[2,256,256]{2,1,0:T(8,128)S(1)}, f32[16,2,2,16,256]{4,3,2,1,0:T(8,128)}) custom-call(s32[4]{0:T(128)S(1)} %and_select_fusion.refs_0_, s32[4]{0:T(128)S(1)} %pad_add_fusion.2.refs_1_, bf16[4,2,2,256,256]{4,3,2,1,0:T(8,128)(2,1)} %bitcast.42, bf16[4,2,2,256,256]{4,3,2,1,0:T(8,128)(2,1)} %copy-done.10, bf16[4,2,2,256,256]{4,3,2,1,0:T(8,128)(2,1)} %bitcast.45, ...), custom_call_target="tpu_custom_call" | custom-call | flops 8589934592 | bytes 8388608 | tf_op jit(solution)/shard_map/backward/pallas_call | solution.py:415
  145.9 4.5 %all-to-all-start.1 = ((f32[16,2,2,16,256]{4,3,2,1,0:T(8,128)}), f32[16,2,2,16,256]{4,3,2,1,0:T(8,128)S(1)}, u32[]{:S(2)}, u32[]{:S(2)}) async-start(f32[16,2,2,16,256]{4,3,2,1,0:T(8,128)} %get-tuple-element.50), calls=%async_computation.1 | async-start | bytes 2097152 | tf_op jit(solution)/shard_map/all_to_all | solution.py:524
  150.5 1.2 copy-done.6
  151.7 24.4 %backward.3 = f32[16,2,2,16,256]{4,3,2,1,0:T(8,128)} custom-call(s32[4]{0:T(128)S(1)} %and_select_fusion.refs_0_, s32[4]{0:T(128)S(1)} %pad_add_fusion.2.refs_1_, bf16[4,1,2,256,256]{4,3,2,1,0:T(8,128)(2,1)} %get-tuple-element.51.refs_2_, bf16[4,1,2,256,256]{4,3,2,1,0:T(8,128)(2,1)} %get-tuple-element.52.refs_3_, bf16[4,2,2,256,256]{4,3,2,1,0:T(8,128)(2,1)} %bitcast.43, ...), custom_call_target="tpu_custom_call" | custom-call | flops 8589934592 | bytes 8388608 | tf_op jit(solution)/shard_map/backward/pallas_call | solution.py:415
  176.1 7.2 %all-to-all-start.2 = ((f32[16,2,2,16,256]{4,3,2,1,0:T(8,128)}), f32[16,2,2,16,256]{4,3,2,1,0:T(8,128)S(1)}, u32[]{:S(2)}, u32[]{:S(2)}) async-start(f32[16,2,2,16,256]{4,3,2,1,0:T(8,128)} %backward.3), calls=%async_computation.2 | async-start | bytes 2097152 | tf_op jit(solution)/shard_map/all_to_all | solution.py:527
  183.3 1.3 reduce.3
  184.7 15.8 %all-to-all-done.2.refs_3_ = f32[16,2,2,16,256]{4,3,2,1,0:T(8,128)S(1)} async-done(((f32[16,2,2,16,256]{4,3,2,1,0:T(8,128)}), f32[16,2,2,16,256]{4,3,2,1,0:T(8,128)S(1)}, u32[]{:S(2)}, u32[]{:S(2)}) %all-to-all-start.2) | async-done | bytes 1048608 | tf_op jit(solution)/shard_map/all_to_all | solution.py:527
  200.5 1.3 reduce.2
  201.9 13.1 %all_to_all.20 = f32[16,2,8,512]{3,2,1,0:T(8,128)S(1)} all-to-all(f32[16,2,8,512]{3,2,1,0:T(8,128)S(1)} %bitcast.34), channel_id=1, replica_groups=mesh['y'=4,'z'=4,'core'=2,'x'=4] {'x','y'}, dimensions={0} | all-to-all | bytes 1048576 | tf_op jit(solution)/shard_map/all_to_all | solution.py:532
  (77 shorter events, 15.2 us)
Async XLA Ops:
  6.5 7.7 %copy-start.8 = (f32[256,256]{1,0:T(8,128)S(1)}, f32[256,256]{1,0:T(8,128)}, u32[]{:S(2)}) copy-start(f32[256,256]{1,0:T(8,128)} %param.14) | copy-start | bytes 786436
  6.5 14.3 %collective-permute-start.1 = (bf16[2,1,128,512]{3,2,1,0:T(8,128)(2,1)}, bf16[2,1,128,512]{3,2,1,0:T(8,128)(2,1)S(1)}, u32[]{:S(2)}, u32[]{:S(2)}) collective-permute-start(bf16[2,1,128,512]{3,2,1,0:T(8,128)(2,1)} %refs_0_.1), channel_id=1, source_target_pairs={{0,3},{1,0},{2,1},{3,2},{4,7},{5,4},{6,5},{7,6},{8,11},{9,8},{10,9... | collective-permute-start | bytes 786440 | tf_op jit(solution)/shard_map/ppermute | solution.py:452
  9.4 14.8 %collective-permute-start = (bf16[2,1,128,512]{3,2,1,0:T(8,128)(2,1)}, bf16[2,1,128,512]{3,2,1,0:T(8,128)(2,1)S(1)}, u32[]{:S(2)}, u32[]{:S(2)}) collective-permute-start(bf16[2,1,128,512]{3,2,1,0:T(8,128)(2,1)} %refs_0_.1), channel_id=1, source_target_pairs={{0,1},{1,2},{2,3},{3,0},{4,5},{5,6},{6,7},{7,4},{8,9},{9,10},{10,1... | collective-permute-start | bytes 786440 | tf_op jit(solution)/shard_map/ppermute | solution.py:452
  9.4 14.8 %collective-permute-start.2 = (bf16[2,1,128,512]{3,2,1,0:T(8,128)(2,1)}, bf16[2,1,128,512]{3,2,1,0:T(8,128)(2,1)S(1)}, u32[]{:S(2)}, u32[]{:S(2)}) collective-permute-start(bf16[2,1,128,512]{3,2,1,0:T(8,128)(2,1)} %refs_0_.1), channel_id=1, source_target_pairs={{0,2},{1,3},{2,0},{3,1},{4,6},{5,7},{6,4},{7,5},{8,10},{9,11},{10,... | collective-permute-start | bytes 786440 | tf_op jit(solution)/shard_map/ppermute | solution.py:452
  14.0 2.7 %copy-start.1 = (s32[4]{0:T(128)S(1)}, s32[4]{0:T(128)}, u32[]{:S(2)}) copy-start(s32[4]{0:T(128)} %cols_ref.1) | copy-start | bytes 52
  14.0 3.4 %copy-start.2 = (s32[4]{0:T(128)S(1)}, s32[4]{0:T(128)}, u32[]{:S(2)}) copy-start(s32[4]{0:T(128)} %rows_ref.1) | copy-start | bytes 52
  14.2 9.9 %copy-start = (bf16[2,1,128,512]{3,2,1,0:T(8,128)(2,1)S(1)}, bf16[2,1,128,512]{3,2,1,0:T(8,128)(2,1)}, u32[]{:S(2)}) copy-start(bf16[2,1,128,512]{3,2,1,0:T(8,128)(2,1)} %refs_0_.1) | copy-start | bytes 786436
  28.5 17.4 %all-to-all-start = ((bf16[4,2,256,256]{3,2,1,0:T(8,128)(2,1)}), bf16[4,2,256,256]{3,2,1,0:T(8,128)(2,1)S(1)}, u32[]{:S(2)}, u32[]{:S(2)}) async-start(bf16[4,2,256,256]{3,2,1,0:T(8,128)(2,1)} %cut.1), calls=%async_computation | async-start | bytes 2097152 | tf_op jit(solution)/shard_map/all_to_all | solution.py:501
  33.0 3.6 %copy-start.7 = (f32[2,256,128]{2,1,0:T(8,128)S(1)}, f32[2,256,128]{2,1,0:T(8,128)}, u32[]{:S(2)}) copy-start(f32[2,256,128]{2,1,0:T(8,128)} %rev.27) | copy-start | bytes 786436
  33.0 47.6 %all-gather.5.cloned.1.call-start = ((), (), s32[]{:S(2)}) async-start(), calls=%async_computation.4 | async-start | bytes 2621440 | tf_op jit(solution)/shard_map/all_gather | solution.py:505
  36.6 30.5 %copy-start.3 = (bf16[4,256,256]{2,1,0:T(8,128)(2,1)S(1)}, bf16[4,256,256]{2,1,0:T(8,128)(2,1)}, u32[]{:S(2)}) copy-start(bf16[4,256,256]{2,1,0:T(8,128)(2,1)} %constant.81.clone.refs_12_.refs_8_.refs_5_.refs_7_) | copy-start | bytes 1572868
  37.8 3.6 %collective-permute-start.5 = (s32[2,4]{1,0:T(2,128)S(1)}, s32[2,4]{1,0:T(2,128)S(1)}, u32[]{:S(2)}, u32[]{:S(2)}) collective-permute-start(s32[2,4]{1,0:T(2,128)S(1)} %pad_add_fusion.1), channel_id=1, source_target_pairs={{0,3},{1,0},{2,1},{3,2},{4,7},{5,4},{6,5},{7,6},{8,11},{9,8},{10,9... | collective-permute-start | bytes 104 | tf_op jit(solution)/shard_map/ppermute | solution.py:452
  38.2 5.1 %collective-permute-start.4 = (s32[2,4]{1,0:T(2,128)S(1)}, s32[2,4]{1,0:T(2,128)S(1)}, u32[]{:S(2)}, u32[]{:S(2)}) collective-permute-start(s32[2,4]{1,0:T(2,128)S(1)} %pad_add_fusion.1), channel_id=1, source_target_pairs={{0,2},{1,3},{2,0},{3,1},{4,6},{5,7},{6,4},{7,5},{8,10},{9,11},{10,... | collective-permute-start | bytes 104 | tf_op jit(solution)/shard_map/ppermute | solution.py:452
  38.6 5.5 %collective-permute-start.3 = (s32[2,4]{1,0:T(2,128)S(1)}, s32[2,4]{1,0:T(2,128)S(1)}, u32[]{:S(2)}, u32[]{:S(2)}) collective-permute-start(s32[2,4]{1,0:T(2,128)S(1)} %pad_add_fusion.1), channel_id=1, source_target_pairs={{0,1},{1,2},{2,3},{3,0},{4,5},{5,6},{6,7},{7,4},{8,9},{9,10},{10,1... | collective-permute-start | bytes 104 | tf_op jit(solution)/shard_map/ppermute | solution.py:452
  46.0 20.4 %copy-start.9 = (bf16[2,256,256]{2,1,0:T(8,128)(2,1)}, bf16[2,256,256]{2,1,0:T(8,128)(2,1)S(1)}, u32[]{:S(2)}) copy-start(bf16[2,256,256]{2,1,0:T(8,128)(2,1)S(1)} %slice_bitcast_fusion.refs_2_) | copy-start | bytes 786436
  46.9 62.7 %all-gather.7.cloned.1.call-start = ((), (), s32[]{:S(2)}) async-start(), calls=%async_computation.5 | async-start | bytes 2359296 | tf_op jit(solution)/shard_map/all_gather | solution.py:506
  47.0 14.0 %collective-permute-start.8 = (bf16[2,256,256]{2,1,0:T(8,128)(2,1)S(1)}, bf16[2,256,256]{2,1,0:T(8,128)(2,1)}, u32[]{:S(2)}, u32[]{:S(2)}) collective-permute-start(bf16[2,256,256]{2,1,0:T(8,128)(2,1)S(1)} %slice_bitcast_fusion.refs_2_), channel_id=1, source_target_pairs={{0,24},{8,0},{16,8},{24,16},{1,25},{9,1},{17,9},{25,17},{2,26},{10... | collective-permute-start | bytes 786440 | tf_op jit(solution)/shard_map/ppermute | solution.py:452
  51.1 9.9 %collective-permute-start.7 = (bf16[2,256,256]{2,1,0:T(8,128)(2,1)S(1)}, bf16[2,256,256]{2,1,0:T(8,128)(2,1)}, u32[]{:S(2)}, u32[]{:S(2)}) collective-permute-start(bf16[2,256,256]{2,1,0:T(8,128)(2,1)S(1)} %slice_bitcast_fusion.refs_2_), channel_id=1, source_target_pairs={{0,16},{8,24},{16,0},{24,8},{1,17},{9,25},{17,1},{25,9},{2,18},{10... | collective-permute-start | bytes 786440 | tf_op jit(solution)/shard_map/ppermute | solution.py:452
  51.1 13.6 %collective-permute-start.6 = (bf16[2,256,256]{2,1,0:T(8,128)(2,1)S(1)}, bf16[2,256,256]{2,1,0:T(8,128)(2,1)}, u32[]{:S(2)}, u32[]{:S(2)}) collective-permute-start(bf16[2,256,256]{2,1,0:T(8,128)(2,1)S(1)} %slice_bitcast_fusion.refs_2_), channel_id=1, source_target_pairs={{0,8},{8,16},{16,24},{24,0},{1,9},{9,17},{17,25},{25,1},{2,10},{10... | collective-permute-start | bytes 786440 | tf_op jit(solution)/shard_map/ppermute | solution.py:452
  53.1 11.6 %collective-permute-start.9 = (bf16[2,256,256]{2,1,0:T(8,128)(2,1)S(1)}, bf16[2,256,256]{2,1,0:T(8,128)(2,1)S(1)}, u32[]{:S(2)}, u32[]{:S(2)}) collective-permute-start(bf16[2,256,256]{2,1,0:T(8,128)(2,1)S(1)} %slice_bitcast_fusion.refs_2_), channel_id=1, source_target_pairs={{0,4},{4,0},{1,5},{5,1},{2,6},{6,2},{3,7},{7,3},{8,12},{12,8},{9,1... | collective-permute-start | bytes 786440 | tf_op jit(solution)/shard_map/ppermute | solution.py:452
  60.9 3.8 %collective-permute-start.12 = (bf16[2,256,256]{2,1,0:T(8,128)(2,1)}, bf16[2,256,256]{2,1,0:T(8,128)(2,1)S(1)}, u32[]{:S(2)}, u32[]{:S(2)}) collective-permute-start(bf16[2,256,256]{2,1,0:T(8,128)(2,1)} %collective-permute-done.8.refs_5_), channel_id=1, source_target_pairs={{0,4},{4,0},{1,5},{5,1},{2,6},{6,2},{3,7},{7,3},{8,12},{12,8},{9,1... | collective-permute-start | bytes 786440 | tf_op jit(solution)/shard_map/ppermute | solution.py:452
  60.9 3.8 %collective-permute-start.11 = (bf16[2,256,256]{2,1,0:T(8,128)(2,1)}, bf16[2,256,256]{2,1,0:T(8,128)(2,1)S(1)}, u32[]{:S(2)}, u32[]{:S(2)}) collective-permute-start(bf16[2,256,256]{2,1,0:T(8,128)(2,1)} %collective-permute-done.7.refs_4_), channel_id=1, source_target_pairs={{0,4},{4,0},{1,5},{5,1},{2,6},{6,2},{3,7},{7,3},{8,12},{12,8},{9,1... | collective-permute-start | bytes 786440 | tf_op jit(solution)/shard_map/ppermute | solution.py:452
  64.7 1.7 collective-permute-start.10
  64.7 1.7 copy-start.11
  64.7 1.7 copy-start.12
  64.7 1.7 copy-start.13
  80.6 4.4 %collective-permute-start.13 = (bf16[4,2,2,256,256]{4,3,2,1,0:T(8,128)(2,1)}, bf16[4,2,2,256,256]{4,3,2,1,0:T(8,128)(2,1)S(1)}, u32[]{:S(2)}, u32[]{:S(2)}) collective-permute-start(bf16[4,2,2,256,256]{4,3,2,1,0:T(8,128)(2,1)} %bitcast.39), channel_id=1, source_target_pairs={{0,4},{4,0},{1,5},{5,1},{2,6},{6,2},{3,7},{7,3},{8,12},{12,8},{9,1... | collective-permute-start | bytes 6291464 | tf_op jit(solution)/shard_map/ppermute | solution.py:452
  85.0 1.4 copy-start.10
  109.6 12.9 %copy-start.5 = (f32[2,2,256,256]{3,2,1,0:T(8,128)S(1)}, f32[2,2,256,256]{3,2,1,0:T(8,128)}, u32[]{:S(2)}) copy-start(f32[2,2,256,256]{3,2,1,0:T(8,128)} %copy-done.4) | copy-start | bytes 3145732
  145.9 30.1 %all-to-all-start.1 = ((f32[16,2,2,16,256]{4,3,2,1,0:T(8,128)}), f32[16,2,2,16,256]{4,3,2,1,0:T(8,128)S(1)}, u32[]{:S(2)}, u32[]{:S(2)}) async-start(f32[16,2,2,16,256]{4,3,2,1,0:T(8,128)} %get-tuple-element.50), calls=%async_computation.1 | async-start | bytes 2097152 | tf_op jit(solution)/shard_map/all_to_all | solution.py:524
  150.5 1.2 copy-start.6
  176.1 24.4 %all-to-all-start.2 = ((f32[16,2,2,16,256]{4,3,2,1,0:T(8,128)}), f32[16,2,2,16,256]{4,3,2,1,0:T(8,128)S(1)}, u32[]{:S(2)}, u32[]{:S(2)}) async-start(f32[16,2,2,16,256]{4,3,2,1,0:T(8,128)} %backward.3), calls=%async_computation.2 | async-start | bytes 2097152 | tf_op jit(solution)/shard_map/all_to_all | solution.py:527
  (2 other events, 1.7 us)
Sparse Core Ops, SparseCore 0:
  47.0 32.2 all-gather.4
  81.0 23.9 all-gather.6
